TPU v7x, 32 devices: a whole 2x2x4 slice. The times are simulated.
32 devices in a mesh: dp: 4 (over x, core), ctx: 4 (over z), tensor: 2 (over y).
Axes of the slice: x: 2, y: 2, z: 4, core: 2. Of those that a mesh axis runs over, the one named last changes fastest.
Arguments:
- inputs: bfloat16 [4, 1024, 2048], P('dp', 'ctx'), may hold values from -6 to 6
- segment_ids: int32 [4, 1024], P('dp', 'ctx'), may hold values from 0 to 3, as said below
- positions: int32 [4, 1024], P('dp', 'ctx'), may hold values from 0 to 383, as said below
- out_grad: bfloat16 [4, 1024, 2048], P('dp', 'ctx'), may hold values from -6 to 6
- attn_gain: bfloat16 [2048], P(('dp', 'ctx')), may hold values from 0.5 to 1.5
- w_query: bfloat16 [2048, 2048], P(('dp', 'ctx'), 'tensor'), may hold values from -0.125 to 0.125
- w_key: bfloat16 [2048, 1024], P(('dp', 'ctx'), 'tensor'), may hold values from -0.125 to 0.125
- w_value: bfloat16 [2048, 1024], P(('dp', 'ctx'), 'tensor'), may hold values from -0.125 to 0.125
- q_gain: bfloat16 [128], P(('dp', 'ctx')), may hold values from 0.5 to 7, as said below
- k_gain: bfloat16 [128], P(('dp', 'ctx')), may hold values from 0.5 to 7, as said below
- w_out: bfloat16 [2048, 2048], P('tensor', ('dp', 'ctx')), may hold values from -1.5 to 1.5
- mlp_gain: bfloat16 [2048], P(('dp', 'ctx')), may hold values from 0.5 to 1.5
- w_gate: bfloat16 [2048, 6144], P(('dp', 'ctx'), 'tensor'), may hold values from -0.125 to 0.125
- w_up: bfloat16 [2048, 6144], P(('dp', 'ctx'), 'tensor'), may hold values from -0.125 to 0.125
- w_down: bfloat16 [6144, 2048], P('tensor', ('dp', 'ctx')), may hold values from -0.3125 to 0.3125
Outputs:
- output: bfloat16 [4, 1024, 2048], P('dp', 'ctx')
- input_grad: bfloat16 [4, 1024, 2048], P('dp', 'ctx')
- attn_gain_grad: float32 [2048], P(('dp', 'ctx'))
- w_query_grad: float32 [2048, 2048], P(('dp', 'ctx'), 'tensor')
- w_key_grad: float32 [2048, 1024], P(('dp', 'ctx'), 'tensor')
- w_value_grad: float32 [2048, 1024], P(('dp', 'ctx'), 'tensor')
- q_gain_grad: float32 [128], P(('dp', 'ctx'))
- k_gain_grad: float32 [128], P(('dp', 'ctx'))
- w_out_grad: float32 [2048, 2048], P('tensor', ('dp', 'ctx'))
- mlp_gain_grad: float32 [2048], P(('dp', 'ctx'))
- w_gate_grad: float32 [2048, 6144], P(('dp', 'ctx'), 'tensor')
- w_up_grad: float32 [2048, 6144], P(('dp', 'ctx'), 'tensor')
- w_down_grad: float32 [6144, 2048], P('tensor', ('dp', 'ctx'))
Inputs may be any that keep to these rules, and one draw needn't show every extreme that they name: `segment_ids`: segment numbers never fall along a sequence, start at 0, and each of 0 to 3 names one document in every sequence. `positions`: a token's position counts the tokens before it in its own document. `q_gain`: positive gains. `k_gain`: positive gains.
All inputs are finite; a program needn't handle non-finite values.
Results may differ from a plain program's by a relative error of at most 0.025.
The roundings to bfloat16 on the way count: a program that leaves them out, or rounds other values in their place, can miss the bound.
Values may be sent and summed in bfloat16 or wider, within the bound.
A program may use at most 256 MiB of HBM per device.

v0:
```python
import math

import jax
import jax.numpy as jnp
from jax import lax
from jax.sharding import PartitionSpec as P

HEAD_DIM = 128


epsilon = 1e-06
rope_base = 1000000.0
masked_value = -1e30


def from_behind(value, axis, steps):
    count = lax.axis_size(axis)
    pairs = [(source, (source + steps) % count) for source in range(count)]
    return lax.ppermute(value, axis, pairs)


def rope_tables(positions, head_size):
    half_dim = head_size // 2
    frequency = rope_base ** (-(jnp.arange(half_dim, dtype=jnp.float32) * 2.0) / head_size)
    angles = positions.astype(jnp.float32)[..., None] * frequency
    return (jnp.cos(angles), jnp.sin(angles))


def rotate(values, cosine_table, sine_table):
    half_dim = values.shape[-1] // 2
    first_half = values[..., :half_dim]
    second_half = values[..., half_dim:]
    return jnp.concatenate(
        [
            first_half * cosine_table - second_half * sine_table,
            second_half * cosine_table + first_half * sine_table,
        ],
        axis=-1,
    )


def head_norm(raw_heads, gain_vector, cosine_table, sine_table):
    scaled = (
        raw_heads
        * lax.rsqrt(jnp.mean(raw_heads * raw_heads, axis=-1, keepdims=True) + epsilon)
        * gain_vector
    )
    return rotate(scaled, cosine_table, sine_table)


def rms_norm(stream, gain_vector):
    return (
        stream
        * lax.rsqrt(jnp.mean(stream * stream, axis=-1, keepdims=True) + epsilon)
        * gain_vector
    )


def silu_product(gate, upward):
    return jax.nn.silu(gate) * upward


def on_device(
    inputs,
    segment_ids,
    positions,
    out_grad,
    attn_gain,
    w_query,
    w_key,
    w_value,
    q_gain,
    k_gain,
    w_out,
    mlp_gain,
    w_gate,
    w_up,
    w_down,
):
    seq_count, tok_count, width = inputs.shape
    row_count = seq_count * tok_count
    cycle_size = lax.axis_size("ctx")
    cycle_rank = lax.axis_index("ctx")
    gathered_attn = (
        lax.all_gather(w_query, ("dp", "ctx"), axis=0, tiled=True),
        lax.all_gather(w_key, ("dp", "ctx"), axis=0, tiled=True),
        lax.all_gather(w_value, ("dp", "ctx"), axis=0, tiled=True),
        lax.all_gather(w_out, ("dp", "ctx"), axis=1, tiled=True),
        lax.all_gather(attn_gain, ("dp", "ctx"), axis=0, tiled=True),
        lax.all_gather(q_gain, ("dp", "ctx"), axis=0, tiled=True),
        lax.all_gather(k_gain, ("dp", "ctx"), axis=0, tiled=True),
    )
    query_weight, key_weight, value_weight, out_weight, attn_scale, query_scale, key_scale = (
        gathered_attn
    )
    gathered_mlp = (
        lax.all_gather(w_gate, ("dp", "ctx"), axis=0, tiled=True),
        lax.all_gather(w_up, ("dp", "ctx"), axis=0, tiled=True),
        lax.all_gather(w_down, ("dp", "ctx"), axis=1, tiled=True),
        lax.all_gather(mlp_gain, ("dp", "ctx"), axis=0, tiled=True),
    )
    gate_weight, up_weight, down_weight, mlp_scale = gathered_mlp
    segments_all = lax.all_gather(segment_ids, "ctx", axis=1, tiled=True)
    local_heads = query_weight.shape[1] // HEAD_DIM
    local_kv = key_weight.shape[1] // HEAD_DIM
    group_size = local_heads // local_kv
    kv_width = local_kv * HEAD_DIM
    score_scale = 1.0 / math.sqrt(HEAD_DIM)
    stream = inputs.astype(jnp.float32).reshape(row_count, width)
    normed_attn, attn_norm_pullback = jax.vjp(rms_norm, stream, attn_scale.astype(jnp.float32))
    normed_low = normed_attn.astype(jnp.bfloat16)
    query_raw = jnp.dot(normed_low, query_weight, preferred_element_type=jnp.float32).reshape(
        seq_count, tok_count, local_heads, HEAD_DIM
    )
    key_raw = jnp.dot(normed_low, key_weight, preferred_element_type=jnp.float32).reshape(
        seq_count, tok_count, local_kv, HEAD_DIM
    )
    value_low = (
        jnp.dot(normed_low, value_weight, preferred_element_type=jnp.float32)
        .astype(jnp.bfloat16)
        .reshape(seq_count, tok_count, kv_width)
    )
    cosine_table, sine_table = rope_tables(positions, HEAD_DIM)
    cosine_table = cosine_table[:, :, None, :]
    sine_table = sine_table[:, :, None, :]

    def norm_rope(raw_heads, gain_vector):
        return head_norm(raw_heads, gain_vector, cosine_table, sine_table)

    query_rot, query_pullback = jax.vjp(norm_rope, query_raw, query_scale.astype(jnp.float32))
    key_rot, key_pullback = jax.vjp(norm_rope, key_raw, key_scale.astype(jnp.float32))
    query_low = query_rot.astype(jnp.bfloat16).reshape(
        seq_count, tok_count, local_kv, group_size, HEAD_DIM
    )
    key_low = key_rot.astype(jnp.bfloat16).reshape(seq_count, tok_count, kv_width)
    query_index = cycle_rank * tok_count + jnp.arange(tok_count, dtype=jnp.int32)

    def block_scores(key_block, first_row):
        key_count = key_block.shape[1]
        key_heads = key_block.reshape(seq_count, key_count, local_kv, HEAD_DIM)
        raw_scores = (
            jnp.einsum(
                "stkgd,snkd->skgtn", query_low, key_heads, preferred_element_type=jnp.float32
            )
            * score_scale
        )
        key_index = first_row + jnp.arange(key_count, dtype=jnp.int32)
        key_segments = lax.dynamic_slice_in_dim(segments_all, first_row, key_count, 1)
        allowed = (key_index[None, None, :] <= query_index[None, :, None]) & (
            key_segments[:, None, :] == segment_ids[:, :, None]
        )
        return (raw_scores, allowed[:, None, None, :, :])

    stat_shape = (seq_count, local_kv, group_size, tok_count)
    pieces = (
        lax.all_gather(key_low, "ctx", axis=1, tiled=True),
        lax.all_gather(value_low, "ctx", axis=1, tiled=True),
    )
    row_best = jnp.full(stat_shape, masked_value, jnp.float32)
    raw_scores, allowed = block_scores(pieces[0], jnp.int32(0))
    masked = jnp.where(allowed, raw_scores, masked_value)
    new_best = jnp.maximum(row_best, jnp.max(masked, axis=-1))
    weights = jnp.where(allowed, jnp.exp(masked - new_best[..., None]), 0.0)
    value_heads = pieces[1].reshape(seq_count, pieces[1].shape[1], local_kv, HEAD_DIM)
    added = jnp.einsum(
        "skgtn,snkd->skgtd",
        weights.astype(jnp.bfloat16),
        value_heads,
        preferred_element_type=jnp.float32,
    )
    row_total = jnp.sum(weights, axis=-1)
    log_total = new_best + jnp.log(row_total)
    attended = added / row_total[..., None]
    attended_low = (
        jnp.transpose(attended, (0, 3, 1, 2, 4))
        .reshape(row_count, local_heads * HEAD_DIM)
        .astype(jnp.bfloat16)
    )
    attn_part = jnp.dot(attended_low, out_weight, preferred_element_type=jnp.float32)
    middle = stream + lax.psum(attn_part.astype(jnp.bfloat16), "tensor").astype(jnp.float32)
    normed_mid, mlp_norm_pullback = jax.vjp(rms_norm, middle, mlp_scale.astype(jnp.float32))
    mid_low = normed_mid.astype(jnp.bfloat16)
    gate = jnp.dot(mid_low, gate_weight, preferred_element_type=jnp.float32)
    upward = jnp.dot(mid_low, up_weight, preferred_element_type=jnp.float32)
    hidden, silu_pullback = jax.vjp(silu_product, gate, upward)
    hidden_low = hidden.astype(jnp.bfloat16)
    down_part = jnp.dot(hidden_low, down_weight, preferred_element_type=jnp.float32)
    down_sum = lax.psum(down_part.astype(jnp.bfloat16), "tensor").astype(jnp.float32)
    output = (middle + down_sum).astype(jnp.bfloat16).reshape(seq_count, tok_count, width)
    grad_low = out_grad.reshape(row_count, width)
    down_weight_grad = jnp.dot(hidden_low.T, grad_low, preferred_element_type=jnp.float32)
    hidden_grad = jnp.dot(grad_low, down_weight.T, preferred_element_type=jnp.float32)
    gate_grad, upward_grad = silu_pullback(hidden_grad)
    gate_grad_low = gate_grad.astype(jnp.bfloat16)
    upward_grad_low = upward_grad.astype(jnp.bfloat16)
    gate_weight_grad = jnp.dot(mid_low.T, gate_grad_low, preferred_element_type=jnp.float32)
    up_weight_grad = jnp.dot(mid_low.T, upward_grad_low, preferred_element_type=jnp.float32)
    mid_grad_part = jnp.dot(
        gate_grad_low, gate_weight.T, preferred_element_type=jnp.float32
    ) + jnp.dot(upward_grad_low, up_weight.T, preferred_element_type=jnp.float32)
    mid_grad = lax.psum(mid_grad_part.astype(jnp.bfloat16), "tensor").astype(jnp.float32)
    middle_norm_grad, mlp_gain_grad = mlp_norm_pullback(mid_grad)
    middle_grad = grad_low.astype(jnp.float32) + middle_norm_grad
    mlp_grads = (
        lax.psum_scatter(gate_weight_grad, ("dp", "ctx"), scatter_dimension=0, tiled=True),
        lax.psum_scatter(up_weight_grad, ("dp", "ctx"), scatter_dimension=0, tiled=True),
        lax.psum_scatter(down_weight_grad, ("dp", "ctx"), scatter_dimension=1, tiled=True),
        lax.psum_scatter(mlp_gain_grad, ("dp", "ctx"), scatter_dimension=0, tiled=True),
    )
    branch_grad = middle_grad.astype(jnp.bfloat16)
    out_weight_grad = jnp.dot(attended_low.T, branch_grad, preferred_element_type=jnp.float32)
    attended_grad = jnp.dot(branch_grad, out_weight.T, preferred_element_type=jnp.float32).astype(
        jnp.bfloat16
    )
    attended_grad_heads = jnp.transpose(
        attended_grad.reshape(seq_count, tok_count, local_kv, group_size, HEAD_DIM), (0, 2, 3, 1, 4)
    )
    row_delta = jnp.sum(attended_grad_heads.astype(jnp.float32) * attended, axis=-1)

    def key_block_grads(key_block, value_block, first_row):
        raw_scores, allowed = block_scores(key_block, first_row)
        probability = jnp.where(allowed, jnp.exp(raw_scores - log_total[..., None]), 0.0)
        key_count = key_block.shape[1]
        value_heads = value_block.reshape(seq_count, key_count, local_kv, HEAD_DIM)
        key_heads = key_block.reshape(seq_count, key_count, local_kv, HEAD_DIM)
        prob_grad = jnp.einsum(
            "skgtd,snkd->skgtn",
            attended_grad_heads,
            value_heads,
            preferred_element_type=jnp.float32,
        )
        score_grad = (probability * (prob_grad - row_delta[..., None])).astype(jnp.bfloat16)
        query_add = jnp.einsum(
            "skgtn,snkd->skgtd", score_grad, key_heads, preferred_element_type=jnp.float32
        )
        key_add = jnp.einsum(
            "skgtn,stkgd->snkd", score_grad, query_low, preferred_element_type=jnp.float32
        ).reshape(seq_count, key_count, kv_width)
        value_add = jnp.einsum(
            "skgtn,skgtd->snkd",
            probability.astype(jnp.bfloat16),
            attended_grad_heads,
            preferred_element_type=jnp.float32,
        ).reshape(seq_count, key_count, kv_width)
        return (query_add, key_add, value_add)

    query_zero = jnp.zeros(stat_shape + (HEAD_DIM,), jnp.float32)
    kv_zero = jnp.zeros((seq_count, tok_count, kv_width), jnp.float32)

    def cycle_turn(turn_index, state):
        key_block, value_block, key_grad_acc, value_grad_acc, query_grad_acc = state
        owner_rank = (cycle_rank + turn_index) % cycle_size
        query_add, key_add, value_add = key_block_grads(
            key_block, value_block, owner_rank * tok_count
        )
        moved_blocks = from_behind((key_block, value_block), "ctx", -1)
        moved_grads = (
            from_behind((key_grad_acc + key_add).astype(jnp.bfloat16), "ctx", -1).astype(
                jnp.float32
            ),
            from_behind((value_grad_acc + value_add).astype(jnp.bfloat16), "ctx", -1).astype(
                jnp.float32
            ),
        )
        return (
            moved_blocks[0],
            moved_blocks[1],
            moved_grads[0],
            moved_grads[1],
            query_grad_acc + query_add,
        )

    final_state = lax.fori_loop(
        0, cycle_size, cycle_turn, (key_low, value_low, kv_zero, kv_zero, query_zero)
    )
    key_grad_sum = final_state[2]
    value_grad_sum = final_state[3]
    query_grad_sum = final_state[4]
    query_grad = (
        jnp.transpose(query_grad_sum, (0, 3, 1, 2, 4)).reshape(
            seq_count, tok_count, local_heads, HEAD_DIM
        )
        * score_scale
    )
    query_raw_grad, query_gain_grad = query_pullback(query_grad)
    key_raw_grad, key_gain_grad = key_pullback(
        (key_grad_sum * score_scale).reshape(seq_count, tok_count, local_kv, HEAD_DIM)
    )
    query_grad_low = query_raw_grad.reshape(row_count, local_heads * HEAD_DIM).astype(jnp.bfloat16)
    key_grad_low = key_raw_grad.reshape(row_count, kv_width).astype(jnp.bfloat16)
    value_grad_low = value_grad_sum.reshape(row_count, kv_width).astype(jnp.bfloat16)
    query_weight_grad = jnp.dot(normed_low.T, query_grad_low, preferred_element_type=jnp.float32)
    key_weight_grad = jnp.dot(normed_low.T, key_grad_low, preferred_element_type=jnp.float32)
    value_weight_grad = jnp.dot(normed_low.T, value_grad_low, preferred_element_type=jnp.float32)
    normed_grad_part = (
        jnp.dot(query_grad_low, query_weight.T, preferred_element_type=jnp.float32)
        + jnp.dot(key_grad_low, key_weight.T, preferred_element_type=jnp.float32)
        + jnp.dot(value_grad_low, value_weight.T, preferred_element_type=jnp.float32)
    )
    normed_grad, query_gain_total, key_gain_total = (
        lax.psum(normed_grad_part.astype(jnp.bfloat16), "tensor").astype(jnp.float32),
        lax.psum(query_gain_grad.astype(jnp.bfloat16), "tensor").astype(jnp.float32),
        lax.psum(key_gain_grad.astype(jnp.bfloat16), "tensor").astype(jnp.float32),
    )
    stream_norm_grad, attn_gain_grad = attn_norm_pullback(normed_grad)
    input_grad = (
        (middle_grad + stream_norm_grad).astype(jnp.bfloat16).reshape(seq_count, tok_count, width)
    )
    attn_grads = (
        lax.psum_scatter(query_weight_grad, ("dp", "ctx"), scatter_dimension=0, tiled=True),
        lax.psum_scatter(key_weight_grad, ("dp", "ctx"), scatter_dimension=0, tiled=True),
        lax.psum_scatter(value_weight_grad, ("dp", "ctx"), scatter_dimension=0, tiled=True),
        lax.psum_scatter(out_weight_grad, ("dp", "ctx"), scatter_dimension=1, tiled=True),
        lax.psum_scatter(attn_gain_grad, ("dp", "ctx"), scatter_dimension=0, tiled=True),
        lax.psum_scatter(query_gain_total, ("dp", "ctx"), scatter_dimension=0, tiled=True),
        lax.psum_scatter(key_gain_total, ("dp", "ctx"), scatter_dimension=0, tiled=True),
    )
    return (
        output,
        input_grad,
        attn_grads[4],
        attn_grads[0],
        attn_grads[1],
        attn_grads[2],
        attn_grads[5],
        attn_grads[6],
        attn_grads[3],
        mlp_grads[3],
        mlp_grads[0],
        mlp_grads[1],
        mlp_grads[2],
    )


def solution(mesh):
    in_specs = (
        P("dp", "ctx", None),
        P("dp", "ctx"),
        P("dp", "ctx"),
        P("dp", "ctx", None),
        P(("dp", "ctx")),
        P(("dp", "ctx"), "tensor"),
        P(("dp", "ctx"), "tensor"),
        P(("dp", "ctx"), "tensor"),
        P(("dp", "ctx")),
        P(("dp", "ctx")),
        P("tensor", ("dp", "ctx")),
        P(("dp", "ctx")),
        P(("dp", "ctx"), "tensor"),
        P(("dp", "ctx"), "tensor"),
        P("tensor", ("dp", "ctx")),
    )
    out_specs = (
        P("dp", "ctx", None),
        P("dp", "ctx", None),
        P(("dp", "ctx")),
        P(("dp", "ctx"), "tensor"),
        P(("dp", "ctx"), "tensor"),
        P(("dp", "ctx"), "tensor"),
        P(("dp", "ctx")),
        P(("dp", "ctx")),
        P("tensor", ("dp", "ctx")),
        P(("dp", "ctx")),
        P(("dp", "ctx"), "tensor"),
        P(("dp", "ctx"), "tensor"),
        P("tensor", ("dp", "ctx")),
    )
    return jax.shard_map(
        on_device, mesh=mesh, in_specs=in_specs, out_specs=out_specs, check_vma=False
    )
```

profile of v0, /device:TPU:0, one launch (start us, length us, event | category | flops | bytes accessed | tf_op | source)
XLA Modules:
  0.0 2004.8 jit_solution(2352949684466906551)
XLA Ops:
  8.7 34.1 %all-gather.1 = bf16[16,1,128]{2,1,0:T(2,128)(2,1)S(1)} all-gather(bf16[1,1,128]{2,1,0:T(2,128)(2,1)} %bitcast.364), channel_id=1, replica_groups=mesh['dp'=4,'ctx'=4,'tensor'=2] {'dp','ctx'}, dimensions={0}, use_global_device_ids=true | all-gather | bytes 4352 | tf_op jit(solution)/shard_map/all_gather | solution.py:89
  44.4 10.0 all-gather.19.cloned.1.call-done
  54.4 3.5 convolution_convert_fusion.3
  60.3 31.9 %all-reduce.11 = (bf16[128]{0:T(256)(128)(2,1)S(1)}, bf16[128]{0:T(256)(128)(2,1)S(1)}) all-reduce(bf16[128]{0:T(256)(128)(2,1)S(1)} %dynamic-update-slice, bf16[128]{0:T(256)(128)(2,1)S(1)} %dynamic-update-slice.1), channel_id=1, replica_groups=mesh['dp'=4,'ctx'=4,'tensor'=2] {'dp','ctx'}, use_global_device_ids=true, to_apply=%add.4 | all-reduce | flops 256 | bytes 1024
  92.9 4.1 all-gather.13.cloned.1.call-done
  97.0 2.3 fusion.106
  103.0 10.8 all_gather.44
  114.7 10.6 all-gather.29.cloned.1.call-done
  125.3 2.3 copy.168
  127.6 49.5 %all-gather.17.cloned.1.call-done = bf16[2048,1024]{1,0:T(8,128)(2,1)} async-done(((bf16[128,1024]{1,0:T(8,128)(2,1)}), bf16[2048,1024]{1,0:T(8,128)(2,1)}) %all-gather.17.cloned.1.call-update) | async-done | bytes 4194320 | tf_op jit(solution)/shard_map/all_gather | solution.py:85
  177.1 3.5 convolution_bitcast_fusion.1
  184.0 23.6 %all-gather.15.cloned.1.call-done = bf16[1,1024,512]{1,2,0:T(8,128)(2,1)} async-done(((bf16[1,256,512]{1,2,0:T(8,128)(2,1)}), bf16[1,1024,512]{1,2,0:T(8,128)(2,1)}) %all-gather.15.cloned.1.call-update) | async-done | bytes 1048592 | tf_op jit(solution)/shard_map/all_gather | solution.py:156
  207.6 3.2 fusion.20
  210.8 2.0 fusion.21
  212.9 3.1 bitcast_convert_fusion
  216.0 44.3 %all-gather.21.cloned.1.call-done = bf16[1024,2048]{1,0:T(8,128)(2,1)} async-done(((bf16[1024,128]{1,0:T(8,128)(2,1)}), bf16[1024,2048]{1,0:T(8,128)(2,1)}) %all-gather.21.cloned.1.call-update) | async-done | bytes 4194320 | tf_op jit(solution)/shard_map/all_gather | solution.py:88
  260.3 4.4 convolution_convert_fusion
  266.9 29.9 %all-gather.2 = bf16[16,1,128]{2,1,0:T(2,128)(2,1)S(1)} all-gather(bf16[1,1,128]{2,1,0:T(2,128)(2,1)S(1)} %bitcast.365), channel_id=1, replica_groups=mesh['dp'=4,'ctx'=4,'tensor'=2] {'dp','ctx'}, dimensions={0}, use_global_device_ids=true | all-gather | bytes 4352 | tf_op jit(solution)/shard_map/all_gather | solution.py:100
  299.9 3.3 all-reduce.18.cloned.1.call-done
  305.5 100.5 %all-gather.23.cloned.1.call-done = bf16[2048,3072]{1,0:T(8,128)(2,1)} async-done(((bf16[128,3072]{1,0:T(8,128)(2,1)}), bf16[2048,3072]{1,0:T(8,128)(2,1)}) %all-gather.23.cloned.1.call-update) | async-done | bytes 12582928 | tf_op jit(solution)/shard_map/all_gather | solution.py:97
  406.0 9.6 fusion.113
  415.6 91.4 %all-gather.25.cloned.1.call-done = bf16[2048,3072]{1,0:T(8,128)(2,1)} async-done(((bf16[128,3072]{1,0:T(8,128)(2,1)}), bf16[2048,3072]{1,0:T(8,128)(2,1)}) %all-gather.25.cloned.1.call-update) | async-done | bytes 12582928 | tf_op jit(solution)/shard_map/all_gather | solution.py:98
  507.0 9.6 fusion.114
  516.6 94.1 %all-gather.27.cloned.1.call-done = bf16[3072,2048]{1,0:T(8,128)(2,1)} async-done(((bf16[3072,128]{1,0:T(8,128)(2,1)}), bf16[3072,2048]{1,0:T(8,128)(2,1)}) %all-gather.27.cloned.1.call-update) | async-done | bytes 12582928 | tf_op jit(solution)/shard_map/all_gather | solution.py:99
  610.7 13.4 multiply_convert_fusion
  624.1 7.4 fusion.115
  631.5 9.1 fusion.36
  640.6 9.8 convolution_convert_fusion.1
  650.5 28.6 %all-reduce.20.cloned.1.call-done = bf16[256,2048]{1,0:T(8,128)(2,1)} async-done(((bf16[256,2048]{1,0:T(8,128)(2,1)}), bf16[256,2048]{1,0:T(8,128)(2,1)}) %all-reduce.20.cloned.1.call-update) | async-done | bytes 1048592 | tf_op jit(solution)/shard_map/psum | solution.py:201
  679.1 2.9 fusion.48
  682.0 4.6 convolution_convert_fusion.2
  689.2 111.6 %while.24 = (s32[]{:T(128)}, bf16[1,256,512]{2,1,0:T(8,128)(2,1)}, bf16[1,256,512]{2,1,0:T(8,128)(2,1)}, f32[1,256,512]{1,2,0:T(8,128)}, f32[1,256,512]{1,2,0:T(...) while((s32[]{:T(128)}, bf16[1,256,512]{2,1,0:T(8,128)(2,1)}, ...), condition=%wide.region_12.13_spmd.clone, body=%wide.region_11.12_spmd.clone.sunk | while | flops 676528640 | bytes 31351396 | solution.py:273
  690.3 3.3 collective-permute-start
  705.8 5.9 collective-permute-done.2
  713.5 2.5 collective-permute-done.3
  718.7 4.3 collective-permute-start
  732.7 2.8 fusion.181
  735.5 5.6 collective-permute-done.2
  747.3 4.3 collective-permute-start
  761.2 2.8 fusion.181
  763.9 5.5 collective-permute-done.2
  774.9 4.3 collective-permute-start
  788.9 2.8 fusion.181
  791.6 4.6 collective-permute-done.2
  814.2 2.0 fusion.53
  816.3 3.7 fusion.72
  824.3 3.0 fusion.83
  827.5 2.9 fusion.86
  832.1 6.3 fusion.78
  839.4 4.7 fusion.70
  845.4 11.7 fusion.116
  857.2 12.3 fusion.117
  870.7 11.5 fusion.59
  883.5 4.9 all-reduce.12
  888.5 2.3 fusion.49
  890.7 61.8 %all-reduce.10 = (f32[2048]{0:T(1024)S(1)}, f32[128]{0:T(128)S(1)}, f32[128]{0:T(128)S(1)}, f32[2048]{0:T(1024)S(1)}) all-reduce(f32[2048]{0:T(1024)S(1)} %get-tuple-element.457, bf16[128]{0:T(256)(128)(2,1)S(1)} %get-tuple-element.495, ...), channel_id=3, replica_groups=mesh['dp'=4,'ctx'=4,'tensor'=2] {'dp','ctx'}, use_global_device_ids=true, to_apply=%region_18.19.clone | all-reduce | flops 4352 | bytes 34304
  954.9 4.8 fusion.55
  959.7 5.5 reduce-scatter.10.cloned.1.call-done
  965.2 76.2 %reduce-scatter.12.cloned.1.call-done = f32[128,512]{1,0:T(8,128)} async-done(((f32[2048,512]{1,0:T(8,128)}), f32[128,512]{1,0:T(8,128)}) %reduce-scatter.12.cloned.1.call-update) | async-done | bytes 262160 | tf_op jit(solution)/shard_map/reduce_scatter | solution.py:312
  1041.4 107.1 %reduce-scatter.14.cloned.1.call-done = f32[1024,128]{1,0:T(8,128)} async-done(((f32[1024,2048]{1,0:T(8,128)}), f32[1024,128]{1,0:T(8,128)}) %reduce-scatter.14.cloned.1.call-update) | async-done | bytes 524304 | tf_op jit(solution)/shard_map/reduce_scatter | solution.py:313
  1148.6 107.6 %reduce-scatter.8.cloned.1.call-done = f32[128,1024]{1,0:T(8,128)} async-done(((f32[2048,1024]{1,0:T(8,128)}), f32[128,1024]{1,0:T(8,128)}) %reduce-scatter.8.cloned.1.call-update) | async-done | bytes 524304 | tf_op jit(solution)/shard_map/reduce_scatter | solution.py:310
  1256.2 247.7 %reduce-scatter.16.cloned.1.call-done = f32[128,3072]{1,0:T(8,128)} async-done(((f32[2048,3072]{1,0:T(8,128)}), f32[128,3072]{1,0:T(8,128)}) %reduce-scatter.16.cloned.1.call-update) | async-done | bytes 1572880 | tf_op jit(solution)/shard_map/reduce_scatter | solution.py:205
  1503.9 247.2 %reduce-scatter.18.cloned.1.call-done = f32[128,3072]{1,0:T(8,128)} async-done(((f32[2048,3072]{1,0:T(8,128)}), f32[128,3072]{1,0:T(8,128)}) %reduce-scatter.18.cloned.1.call-update) | async-done | bytes 1572880 | tf_op jit(solution)/shard_map/reduce_scatter | solution.py:206
  1751.1 247.0 %reduce-scatter.20.cloned.1.call-done = f32[3072,128]{1,0:T(8,128)} async-done(((f32[3072,2048]{1,0:T(8,128)}), f32[3072,128]{1,0:T(8,128)}) %reduce-scatter.20.cloned.1.call-update) | async-done | bytes 1572880 | tf_op jit(solution)/shard_map/reduce_scatter | solution.py:207
  (346 shorter events, 111.1 us)
Async XLA Ops:
  7.2 47.2 %all-gather.19.cloned.1.call-start = ((), (), s32[]{:S(2)}) async-start(), calls=%async_computation.10 | async-start | bytes 2228224 | tf_op jit(solution)/shard_map/all_gather | solution.py:87
  7.9 89.1 %all-gather.13.cloned.1.call-start = ((), (), s32[]{:S(2)}) async-start(), calls=%async_computation.7 | async-start | bytes 2228224 | tf_op jit(solution)/shard_map/all_gather | solution.py:86
  8.7 116.7 %all-gather.29.cloned.1.call-start = ((), (), s32[]{:S(2)}) async-start(), calls=%async_computation.24 | async-start | bytes 1310720 | tf_op jit(solution)/shard_map/all_gather | solution.py:157
  44.3 10.0 copy-start.50
  44.4 132.8 %copy-start.43 = (f32[256]{0:T(256)}, f32[256]{0:T(256)S(1)}, u32[]{:S(2)}) copy-start(f32[256]{0:T(256)S(1)} %fusion.95) | copy-start | bytes 3076
  54.4 4.2 copy-start.58
  54.4 5.4 copy-start.62
  54.4 5.7 copy-start.63
  54.4 37.9 %copy-start.59 = (s32[1,256]{1,0:T(1,128)S(1)}, s32[1,256]{1,0:T(1,128)}, u32[]{:S(2)}) copy-start(s32[1,256]{1,0:T(1,128)} %param.19) | copy-start | bytes 3076
  54.4 42.6 %copy-start = (bf16[1,256,2048]{2,1,0:T(8,128)(2,1)S(1)}, bf16[1,256,2048]{2,1,0:T(8,128)(2,1)}, u32[]{:S(2)}) copy-start(bf16[1,256,2048]{2,1,0:T(8,128)(2,1)} %param.17) | copy-start | bytes 3145732
  57.9 119.2 %all-gather.17.cloned.1.call-start = ((), (), s32[]{:S(2)}) async-start(), calls=%async_computation.9 | async-start | bytes 4456448 | tf_op jit(solution)/shard_map/all_gather | solution.py:85
  58.5 149.1 %all-gather.15.cloned.1.call-start = ((), (), s32[]{:S(2)}) async-start(), calls=%async_computation.8 | async-start | bytes 1310720 | tf_op jit(solution)/shard_map/all_gather | solution.py:156
  92.3 7.8 copy-start.54
  92.8 7.7 copy-start.21
  102.3 158.0 %all-gather.21.cloned.1.call-start = ((), (), s32[]{:S(2)}) async-start(), calls=%async_computation.11 | async-start | bytes 4456448 | tf_op jit(solution)/shard_map/all_gather | solution.py:88
  102.9 200.3 %all-reduce.18.cloned.1.call-start = ((), (), s32[]{:S(2)}) async-start(), calls=%async_computation.12 | async-start | bytes 2097152 | tf_op jit(solution)/shard_map/psum | solution.py:180
  103.0 78.4 %copy-start.56 = (f32[128]{0:T(128)}, f32[128]{0:T(128)S(1)}, u32[]{:S(2)}) copy-start(f32[128]{0:T(128)S(1)} %convert_element_type.220) | copy-start | bytes 1540
  216.0 48.7 %copy-start.36 = (bf16[1,4,2,256,128]{3,4,2,1,0:T(8,128)(2,1)}, bf16[1,4,2,256,128]{3,4,2,1,0:T(8,128)(2,1)S(1)}, u32[]{:S(2)}) copy-start(bf16[1,4,2,256,128]{3,4,2,1,0:T(8,128)(2,1)S(1)} %get-tuple-element.522) | copy-start | bytes 1572868
  264.7 32.1 %copy-start.24 = (bf16[1,256,4,128]{1,3,2,0:T(8,128)(2,1)S(1)}, bf16[1,256,4,128]{1,3,2,0:T(8,128)(2,1)}, u32[]{:S(2)}) copy-start(bf16[1,256,4,128]{1,3,2,0:T(8,128)(2,1)} %copy.132) | copy-start | bytes 786436
  264.8 141.2 %all-gather.23.cloned.1.call-start = ((), (), s32[]{:S(2)}) async-start(), calls=%async_computation.13 | async-start | bytes 13369344 | tf_op jit(solution)/shard_map/all_gather | solution.py:97
  265.5 241.5 %all-gather.25.cloned.1.call-start = ((), (), s32[]{:S(2)}) async-start(), calls=%async_computation.14 | async-start | bytes 13369344 | tf_op jit(solution)/shard_map/all_gather | solution.py:98
  266.3 33.0 %copy-start.40 = (f32[4,2,256]{2,1,0:T(2,128)S(1)}, f32[4,2,256]{2,1,0:T(2,128)}, u32[]{:S(2)}) copy-start(f32[4,2,256]{2,1,0:T(2,128)} %copy-done.39) | copy-start | bytes 24580
  266.3 344.4 %all-gather.27.cloned.1.call-start = ((), (), s32[]{:S(2)}) async-start(), calls=%async_computation.15 | async-start | bytes 13369344 | tf_op jit(solution)/shard_map/all_gather | solution.py:99
  266.9 412.2 %all-reduce.20.cloned.1.call-start = ((), (), s32[]{:S(2)}) async-start(), calls=%async_computation.16 | async-start | bytes 2097152 | tf_op jit(solution)/shard_map/psum | solution.py:201
  296.9 385.1 %copy-start.37 = (f32[16,1,128]{2,1,0:T(1,128)}, f32[16,1,128]{2,1,0:T(1,128)S(1)}, u32[]{:S(2)}) copy-start(f32[16,1,128]{2,1,0:T(1,128)S(1)} %convert_element_type.258) | copy-start | bytes 24580
  304.9 377.0 %copy-start.48 = (f32[256]{0:T(256)}, f32[256]{0:T(256)S(1)}, u32[]{:S(2)}) copy-start(f32[256]{0:T(256)S(1)} %fusion.96) | copy-start | bytes 3076
  305.4 201.5 %copy-start.12 = (bf16[256,2048]{1,0:T(8,128)(2,1)}, bf16[256,2048]{1,0:T(8,128)(2,1)S(1)}, u32[]{:S(2)}) copy-start(bf16[256,2048]{1,0:T(8,128)(2,1)S(1)} %multiply_convert_fusion.2) | copy-start | bytes 3145732
  624.1 7.4 copy-start.34
  640.6 247.9 %all-reduce.22.cloned.1.call-start = ((), (), s32[]{:S(2)}) async-start(), calls=%async_computation.25 | async-start | bytes 4194304 | tf_op jit(solution)/shard_map/psum | solution.py:188
  650.4 31.5 %copy-start.15 = (bf16[1,256,2048]{2,1,0:T(8,128)(2,1)S(1)}, bf16[1,256,2048]{2,1,0:T(8,128)(2,1)}, u32[]{:S(2)}) copy-start(bf16[1,256,2048]{2,1,0:T(8,128)(2,1)} %param.20) | copy-start | bytes 3145732
  682.0 4.6 copy-start.52
  690.3 27.5 %collective-permute-start = (bf16[1,256,512]{2,1,0:T(8,128)(2,1)S(1)}, bf16[1,256,512]{2,1,0:T(8,128)(2,1)}, u32[]{:S(2)}, u32[]{:S(2)}) collective-permute-start(bf16[1,256,512]{2,1,0:T(8,128)(2,1)S(1)} %copy.225), channel_id=1, source_target_pairs={{0,6},{2,0},{4,2},{6,4},{1,7},{3,1},{5,3},{7,5},{8,14},{10,8},{12,... | collective-permute-start | bytes 786440 | tf_op jit(solution)/shard_map/while/body/eval_jaxpr/ppermute | solution.py:19
  694.6 23.2 %collective-permute-start.1 = (bf16[1,256,512]{2,1,0:T(8,128)(2,1)S(1)}, bf16[1,256,512]{2,1,0:T(8,128)(2,1)}, u32[]{:S(2)}, u32[]{:S(2)}) collective-permute-start(bf16[1,256,512]{2,1,0:T(8,128)(2,1)S(1)} %copy.226), channel_id=1, source_target_pairs={{0,6},{2,0},{4,2},{6,4},{1,7},{3,1},{5,3},{7,5},{8,14},{10,8},{12,... | collective-permute-start | bytes 786440 | tf_op jit(solution)/shard_map/while/body/eval_jaxpr/ppermute | solution.py:19
  696.0 3.1 copy-start.6
  701.9 9.8 collective-permute-start.2
  703.7 12.3 collective-permute-start.3
  718.7 27.6 %collective-permute-start = (bf16[1,256,512]{2,1,0:T(8,128)(2,1)S(1)}, bf16[1,256,512]{2,1,0:T(8,128)(2,1)}, u32[]{:S(2)}, u32[]{:S(2)}) collective-permute-start(bf16[1,256,512]{2,1,0:T(8,128)(2,1)S(1)} %copy.225), channel_id=1, source_target_pairs={{0,6},{2,0},{4,2},{6,4},{1,7},{3,1},{5,3},{7,5},{8,14},{10,8},{12,... | collective-permute-start | bytes 786440 | tf_op jit(solution)/shard_map/while/body/eval_jaxpr/ppermute | solution.py:19
  724.0 22.3 %collective-permute-start.1 = (bf16[1,256,512]{2,1,0:T(8,128)(2,1)S(1)}, bf16[1,256,512]{2,1,0:T(8,128)(2,1)}, u32[]{:S(2)}, u32[]{:S(2)}) collective-permute-start(bf16[1,256,512]{2,1,0:T(8,128)(2,1)S(1)} %copy.226), channel_id=1, source_target_pairs={{0,6},{2,0},{4,2},{6,4},{1,7},{3,1},{5,3},{7,5},{8,14},{10,8},{12,... | collective-permute-start | bytes 786440 | tf_op jit(solution)/shard_map/while/body/eval_jaxpr/ppermute | solution.py:19
  724.8 3.1 copy-start.6
  730.7 10.3 collective-permute-start.2
  732.0 12.5 collective-permute-start.3
  747.3 26.7 %collective-permute-start = (bf16[1,256,512]{2,1,0:T(8,128)(2,1)S(1)}, bf16[1,256,512]{2,1,0:T(8,128)(2,1)}, u32[]{:S(2)}, u32[]{:S(2)}) collective-permute-start(bf16[1,256,512]{2,1,0:T(8,128)(2,1)S(1)} %copy.225), channel_id=1, source_target_pairs={{0,6},{2,0},{4,2},{6,4},{1,7},{3,1},{5,3},{7,5},{8,14},{10,8},{12,... | collective-permute-start | bytes 786440 | tf_op jit(solution)/shard_map/while/body/eval_jaxpr/ppermute | solution.py:19
  752.5 21.5 %collective-permute-start.1 = (bf16[1,256,512]{2,1,0:T(8,128)(2,1)S(1)}, bf16[1,256,512]{2,1,0:T(8,128)(2,1)}, u32[]{:S(2)}, u32[]{:S(2)}) collective-permute-start(bf16[1,256,512]{2,1,0:T(8,128)(2,1)S(1)} %copy.226), channel_id=1, source_target_pairs={{0,6},{2,0},{4,2},{6,4},{1,7},{3,1},{5,3},{7,5},{8,14},{10,8},{12,... | collective-permute-start | bytes 786440 | tf_op jit(solution)/shard_map/while/body/eval_jaxpr/ppermute | solution.py:19
  753.3 3.2 copy-start.6
  759.3 10.1 collective-permute-start.2
  760.6 11.6 collective-permute-start.3
  774.9 25.9 %collective-permute-start = (bf16[1,256,512]{2,1,0:T(8,128)(2,1)S(1)}, bf16[1,256,512]{2,1,0:T(8,128)(2,1)}, u32[]{:S(2)}, u32[]{:S(2)}) collective-permute-start(bf16[1,256,512]{2,1,0:T(8,128)(2,1)S(1)} %copy.225), channel_id=1, source_target_pairs={{0,6},{2,0},{4,2},{6,4},{1,7},{3,1},{5,3},{7,5},{8,14},{10,8},{12,... | collective-permute-start | bytes 786440 | tf_op jit(solution)/shard_map/while/body/eval_jaxpr/ppermute | solution.py:19
  780.2 20.6 %collective-permute-start.1 = (bf16[1,256,512]{2,1,0:T(8,128)(2,1)S(1)}, bf16[1,256,512]{2,1,0:T(8,128)(2,1)}, u32[]{:S(2)}, u32[]{:S(2)}) collective-permute-start(bf16[1,256,512]{2,1,0:T(8,128)(2,1)S(1)} %copy.226), channel_id=1, source_target_pairs={{0,6},{2,0},{4,2},{6,4},{1,7},{3,1},{5,3},{7,5},{8,14},{10,8},{12,... | collective-permute-start | bytes 786440 | tf_op jit(solution)/shard_map/while/body/eval_jaxpr/ppermute | solution.py:19
  781.0 3.2 copy-start.6
  787.0 9.2 collective-permute-start.2
  788.2 10.8 collective-permute-start.3
  800.8 4.1 copy-start.1
  816.3 3.7 copy-start.26
  816.3 3.7 copy-start.23
  816.3 3.7 copy-start.25
  823.6 141.6 %reduce-scatter.10.cloned.1.call-start = ((), (), s32[]{:S(2)}) async-start(), calls=%async_computation.18 | async-start | bytes 4456448 | tf_op jit(solution)/shard_map/reduce_scatter | solution.py:311
  827.3 214.2 %reduce-scatter.12.cloned.1.call-start = ((), (), s32[]{:S(2)}) async-start(), calls=%async_computation.19 | async-start | bytes 4456448 | tf_op jit(solution)/shard_map/reduce_scatter | solution.py:312
  830.5 318.1 %reduce-scatter.14.cloned.1.call-start = ((), (), s32[]{:S(2)}) async-start(), calls=%async_computation.20 | async-start | bytes 8912896 | tf_op jit(solution)/shard_map/reduce_scatter | solution.py:313
  838.4 417.8 %reduce-scatter.8.cloned.1.call-start = ((), (), s32[]{:S(2)}) async-start(), calls=%async_computation.17 | async-start | bytes 8912896 | tf_op jit(solution)/shard_map/reduce_scatter | solution.py:310
  844.2 659.7 %reduce-scatter.16.cloned.1.call-start = ((), (), s32[]{:S(2)}) async-start(), calls=%async_computation.21 | async-start | bytes 26738688 | tf_op jit(solution)/shard_map/reduce_scatter | solution.py:205
  857.1 893.9 %reduce-scatter.18.cloned.1.call-start = ((), (), s32[]{:S(2)}) async-start(), calls=%async_computation.22 | async-start | bytes 26738688 | tf_op jit(solution)/shard_map/reduce_scatter | solution.py:206
  869.5 1128.6 %reduce-scatter.20.cloned.1.call-start = ((), (), s32[]{:S(2)}) async-start(), calls=%async_computation.23 | async-start | bytes 26738688 | tf_op jit(solution)/shard_map/reduce_scatter | solution.py:207
  882.2 8.5 copy-start.47
  882.2 72.7 %copy-start.51 = (f32[256]{0:T(256)S(1)}, f32[256]{0:T(256)}, u32[]{:S(2)}) copy-start(f32[256]{0:T(256)} %copy-done.50) | copy-start | bytes 3076
  (44 other events, 71.7 us)
Sparse Core Ops, SparseCore 0:
  10.2 44.1 all-gather.18
  56.6 40.3 all-gather.12
  98.5 26.7 all-gather.28
  127.4 49.6 all-gather.16
  179.1 28.4 all-gather.14
  209.6 50.7 all-gather.20
  264.9 38.2 all-reduce.17
  305.5 100.4 all-gather.22
  408.3 98.6 all-gather.24
  508.9 101.7 all-gather.26
  640.7 38.2 all-reduce.19
  823.8 63.9 all-reduce.21
  892.2 73.0 reduce-scatter.9
  969.5 71.8 reduce-scatter.11
  1045.9 102.5 reduce-scatter.13
  1153.1 103.0 reduce-scatter.7
  1260.7 243.1 reduce-scatter.15
  1508.4 242.5 reduce-scatter.17
  1755.7 242.3 reduce-scatter.19
where the time goes:
time: 2010 us; the launch traced here: 2000 us
  waiting for transfers between devices  1530 us (76%)
  blocking collectives  173 us (9%)
  matrix products  168 us (8%)
  other arithmetic  56.1 us (3%)
  local copies, waits for them, and re-layouts  38 us (2%)
  starting transfers between devices  20.7 us (1%)
    reduce_scatter x1, waiting for transfers between devices, on_device(): lax.psum_scatter(gate_weight_grad, ('dp', 'ctx'), scatter_dimension=0, ti...  248 us
    reduce_scatter x1, waiting for transfers between devices, on_device(): lax.psum_scatter(up_weight_grad, ('dp', 'ctx'), scatter_dimension=0, tile...  247 us
    reduce_scatter x1, waiting for transfers between devices, on_device(): lax.psum_scatter(down_weight_grad, ('dp', 'ctx'), scatter_dimension=1, ti...  247 us
    reduce_scatter x1, waiting for transfers between devices, on_device(): lax.psum_scatter(query_weight_grad, ('dp', 'ctx'), scatter_dimension=0, t...  108 us
    reduce_scatter x1, waiting for transfers between devices, on_device(): lax.psum_scatter(out_weight_grad, ('dp', 'ctx'), scatter_dimension=1, til...  107 us
    all_gather x1, waiting for transfers between devices, on_device(): lax.all_gather(w_gate, ('dp', 'ctx'), axis=0, tiled=True)  101 us
    all_gather x1, waiting for transfers between devices, on_device(): lax.all_gather(w_down, ('dp', 'ctx'), axis=1, tiled=True)  94.1 us
    unnamed x2, blocking collectives  93.7 us
  transfers between devices with their start and end apart: 35, of which 26 were waited for; matrix products, arithmetic and copies ran while one was open for 9% of the time, Pallas kernels for 0%

commit v1 on v0

--- a/solution.py
+++ b/solution.py
@@ -6,7 +6,8 @@
 from jax.sharding import PartitionSpec as P
 
 HEAD_DIM = 128
-
+BF16 = jnp.bfloat16
+F32 = jnp.float32
 
 epsilon = 1e-06
 rope_base = 1000000.0
@@ -58,6 +59,308 @@
 
 def silu_product(gate, upward):
     return jax.nn.silu(gate) * upward
+
+
+def dot32(left, right, spec):
+    return jnp.einsum(spec, left, right, preferred_element_type=F32)
+
+
+def shift(value, axis, steps):
+    count = lax.axis_size(axis)
+    pairs = [(source, (source + steps) % count) for source in range(count)]
+    return lax.ppermute(value, axis, pairs)
+
+
+def take_ring(blocks, first):
+    return lax.dynamic_slice_in_dim(jnp.concatenate([blocks, blocks]), first, blocks.shape[0], 0)
+
+
+def reversed_ring(blocks):
+    return jnp.concatenate([blocks[:1], blocks[:0:-1]])
+
+
+def gather_behind(block):
+    count = lax.axis_size("ctx")
+    return jnp.stack([block] + [shift(block, "ctx", d) for d in range(1, count)])
+
+
+def scatter_sum(blocks):
+    total = blocks[0].astype(F32)
+    for d in range(1, blocks.shape[0]):
+        total = total + shift(blocks[d], "ctx", -d).astype(F32)
+    return total
+
+
+def swap_by_target(blocks):
+    count = lax.axis_size("ctx")
+    rank = lax.axis_index("ctx")
+    ahead = take_ring(blocks, rank)
+    got = jnp.stack([ahead[0]] + [shift(ahead[d], "ctx", d) for d in range(1, count)])
+    return take_ring(reversed_ring(got), (count - rank) % count)
+
+
+def swap_behind(blocks):
+    count = lax.axis_size("ctx")
+    rank = lax.axis_index("ctx")
+    got = jnp.stack([blocks[0]] + [shift(blocks[d], "ctx", -d) for d in range(1, count)])
+    return take_ring(got, (count - rank) % count)
+
+
+def swap_to_behind(blocks):
+    count = lax.axis_size("ctx")
+    ahead = take_ring(blocks, lax.axis_index("ctx"))
+    return jnp.stack([ahead[0]] + [shift(ahead[d], "ctx", d) for d in range(1, count)])
+
+
+def slices_of(shard):
+    count = lax.axis_size("ctx")
+    rows, width = shard.shape
+    mine = swap_by_target(shard.reshape(rows, count, width // count).transpose(1, 0, 2))
+    mine = mine.reshape(count * rows, width // count)
+    full = lax.all_gather(mine, ("tensor", "dp"), axis=0, tiled=True)
+    tensors = lax.axis_size("tensor")
+    return full.reshape(tensors, full.shape[0] // tensors, full.shape[1])
+
+
+def shards_of(partial):
+    count = lax.axis_size("ctx")
+    width = partial.shape[2]
+    flat = partial.astype(BF16).reshape(-1, width)
+    mine = lax.psum_scatter(flat, ("tensor", "dp"), scatter_dimension=0, tiled=True)
+    got = swap_by_target(mine.reshape(count, mine.shape[0] // count, width))
+    return got.transpose(1, 0, 2).reshape(got.shape[1], count * width).astype(F32)
+
+
+def with_twin(own):
+    other = shift(own, "tensor", 1)
+    first = lax.axis_index("tensor") == 0
+    return jnp.concatenate([jnp.where(first, own, other), jnp.where(first, other, own)])
+
+
+def on_device_sliced(
+    inputs,
+    segment_ids,
+    positions,
+    out_grad,
+    attn_gain,
+    w_query,
+    w_key,
+    w_value,
+    q_gain,
+    k_gain,
+    w_out,
+    mlp_gain,
+    w_gate,
+    w_up,
+    w_down,
+):
+    _, tok_count, width = inputs.shape
+    count = lax.axis_size("ctx")
+    tensors = lax.axis_size("tensor")
+    rank = lax.axis_index("ctx")
+    half = lax.axis_index("tensor")
+    own_rows = tok_count // tensors
+    rows = own_rows * count
+    head_rows = w_out.shape[0]
+    score_scale = 1.0 / math.sqrt(HEAD_DIM)
+
+    q_cols = w_query.shape[1] // count
+    k_cols = w_key.shape[1] // count
+    local_kv = k_cols // HEAD_DIM
+    group = q_cols // k_cols
+    in_width = q_cols + 2 * k_cols
+    in_shard = jnp.concatenate(
+        [
+            w_query.reshape(-1, count, q_cols),
+            w_key.reshape(-1, count, k_cols),
+            w_value.reshape(-1, count, k_cols),
+        ],
+        axis=2,
+    ).reshape(w_query.shape[0], count * in_width)
+    in_weight = slices_of(in_shard)
+    out_weight = lax.all_gather(w_out.T, ("tensor", "dp", "ctx"), axis=0, tiled=True).reshape(
+        tensors, width, head_rows
+    )
+    gate_weight = slices_of(w_gate)
+    up_weight = slices_of(w_up)
+    down_weight = slices_of(w_down.T)
+
+    gains = lax.all_gather(
+        jnp.concatenate([attn_gain, mlp_gain, q_gain, k_gain]), ("dp", "ctx"), axis=0
+    )
+    piece = attn_gain.shape[0]
+    small = q_gain.shape[0]
+    attn_scale = gains[:, :piece].reshape(-1).astype(F32)
+    mlp_scale = gains[:, piece : 2 * piece].reshape(-1).astype(F32)
+    query_scale = gains[:, 2 * piece : 2 * piece + small].reshape(-1).astype(F32)
+    key_scale = gains[:, 2 * piece + small :].reshape(-1).astype(F32)
+
+    marks = lax.all_gather(jnp.stack([segment_ids[0], positions[0]]), "ctx", axis=0)
+    marks = marks.reshape(count, 2, tensors, own_rows)
+    behind = (rank - jnp.arange(count)) % count
+    marks = marks[behind]
+    starts = behind * tok_count
+    offsets = starts[:, None] + jnp.arange(own_rows)[None, :]
+
+    def marks_of(which):
+        segs = lax.dynamic_index_in_dim(marks[:, 0], which, 1, keepdims=False).reshape(rows)
+        return segs, (offsets + which * own_rows).reshape(rows)
+
+    own_segs, own_index = marks_of(half)
+    twin_segs, twin_index = marks_of(1 - half)
+    own_positions = lax.dynamic_index_in_dim(marks[:, 1], half, 1, keepdims=False).reshape(rows)
+    key_segs = jnp.concatenate([own_segs, twin_segs])
+    key_index = jnp.concatenate([own_index, twin_index])
+    allowed = (key_index[None, :] <= own_index[:, None]) & (key_segs[None, :] == own_segs[:, None])
+
+    stream = lax.dynamic_slice_in_dim(inputs[0], half * own_rows, own_rows, 0).astype(F32)
+    grad_own = lax.dynamic_slice_in_dim(out_grad[0], half * own_rows, own_rows, 0)
+    normed_attn, attn_norm_pullback = jax.vjp(rms_norm, stream, attn_scale)
+    normed_low = gather_behind(normed_attn.astype(BF16)).reshape(rows, width)
+    raw = dot32(normed_low, in_weight, "mk,tkc->mtc")
+    query_raw = raw[..., :q_cols].reshape(rows, tensors * local_kv * group, HEAD_DIM)
+    key_raw = raw[..., q_cols : q_cols + k_cols].reshape(rows, tensors * local_kv, HEAD_DIM)
+    kv_heads = tensors * local_kv
+    value_low = raw[..., q_cols + k_cols :].astype(BF16).reshape(rows, kv_heads, HEAD_DIM)
+    cosine_table, sine_table = rope_tables(own_positions, HEAD_DIM)
+    cosine_table = cosine_table[:, None, :]
+    sine_table = sine_table[:, None, :]
+
+    def norm_rope(raw_heads, gain_vector):
+        return head_norm(raw_heads, gain_vector, cosine_table, sine_table)
+
+    query_rot, query_pullback = jax.vjp(norm_rope, query_raw, query_scale)
+    key_rot, key_pullback = jax.vjp(norm_rope, key_raw, key_scale)
+    query_low = query_rot.astype(BF16).reshape(rows, kv_heads, group, HEAD_DIM)
+    key_low = key_rot.astype(BF16)
+    kv_own = jnp.stack([key_low, value_low])
+    kv_all = jnp.concatenate([kv_own, shift(kv_own, "tensor", 1)], axis=1)
+    keys, values = kv_all[0], kv_all[1]
+
+    scores = dot32(query_low, keys, "mkgd,nkd->kgmn") * score_scale
+    masked = jnp.where(allowed, scores, masked_value)
+    best = jnp.max(masked, axis=-1, keepdims=True)
+    weights = jnp.where(allowed, jnp.exp(masked - best), 0.0)
+    total = jnp.sum(weights, axis=-1, keepdims=True)
+    prob = weights / total
+    prob_low = prob.astype(BF16)
+    attended = dot32(prob_low, values, "kgmn,nkd->mkgd")
+    attended_heads = attended.astype(BF16).reshape(count, own_rows, tensors, q_cols)
+    attended_own = swap_behind(attended_heads)
+    attended_own = attended_own.transpose(1, 2, 0, 3).reshape(own_rows, tensors, head_rows)
+    middle = stream + dot32(attended_own, out_weight, "mtr,tkr->mk")
+    normed_mid, mlp_norm_pullback = jax.vjp(rms_norm, middle, mlp_scale)
+    mid_low = gather_behind(normed_mid.astype(BF16)).reshape(rows, width)
+    grad_low = gather_behind(grad_own).reshape(rows, width)
+
+    gate = dot32(mid_low, gate_weight, "mk,tkc->tmc")
+    upward = dot32(mid_low, up_weight, "mk,tkc->tmc")
+    hidden, silu_pullback = jax.vjp(silu_product, gate, upward)
+    hidden_low = hidden.astype(BF16)
+    hidden_grad = dot32(grad_low, down_weight, "mk,tkc->tmc")
+    gate_grad, upward_grad = silu_pullback(hidden_grad)
+    gate_grad_low = gate_grad.astype(BF16)
+    upward_grad_low = upward_grad.astype(BF16)
+    mid_grad_part = dot32(gate_grad_low, gate_weight, "tmc,tkc->mk") + dot32(
+        upward_grad_low, up_weight, "tmc,tkc->mk"
+    )
+    mid_grad = scatter_sum(mid_grad_part.astype(BF16).reshape(count, own_rows, width))
+    down_part = dot32(hidden_low, down_weight, "tmc,tkc->mk")
+    down_sum = scatter_sum(down_part.astype(BF16).reshape(count, own_rows, width))
+    output = with_twin((middle + down_sum).astype(BF16))[None]
+    down_weight_grad = shards_of(dot32(grad_low, hidden_low, "mk,tmc->tkc")).T
+    gate_weight_grad = shards_of(dot32(mid_low, gate_grad_low, "mk,tmc->tkc"))
+    up_weight_grad = shards_of(dot32(mid_low, upward_grad_low, "mk,tmc->tkc"))
+
+    middle_norm_grad, mlp_gain_grad = mlp_norm_pullback(mid_grad)
+    middle_grad = grad_own.astype(F32) + middle_norm_grad
+    branch_grad = middle_grad.astype(BF16)
+    out_weight_grad = dot32(branch_grad, attended_own, "mk,mtr->tkr").astype(BF16)
+    out_weight_grad = (
+        lax.psum_scatter(
+            out_weight_grad.reshape(tensors * width, head_rows),
+            ("tensor", "dp", "ctx"),
+            scatter_dimension=0,
+            tiled=True,
+        )
+        .astype(F32)
+        .T
+    )
+    attended_grad = dot32(branch_grad, out_weight, "mk,tkr->mtr").astype(BF16)
+    attended_grad = attended_grad.reshape(own_rows, tensors, count, q_cols).transpose(2, 0, 1, 3)
+    attended_grad = swap_to_behind(attended_grad).reshape(rows, kv_heads, group, HEAD_DIM)
+    prob_grad = dot32(attended_grad, values, "mkgd,nkd->kgmn")
+    delta = jnp.sum(prob * prob_grad, axis=-1, keepdims=True)
+    score_grad = (prob * (prob_grad - delta)).astype(BF16)
+    query_grad = dot32(score_grad, keys, "kgmn,nkd->mkgd") * score_scale
+    key_grad_all = dot32(score_grad, query_low, "kgmn,mkgd->nkd")
+    value_grad_all = dot32(prob_low, attended_grad, "kgmn,mkgd->nkd")
+    kv_grad_all = jnp.stack([key_grad_all, value_grad_all])
+    kv_grad = kv_grad_all[:, :rows] + shift(
+        kv_grad_all[:, rows:].astype(BF16), "tensor", 1
+    ).astype(F32)
+    query_raw_grad, query_gain_grad = query_pullback(query_grad.reshape(query_raw.shape))
+    key_raw_grad, key_gain_grad = key_pullback(kv_grad[0] * score_scale)
+    raw_grad_low = jnp.concatenate(
+        [
+            query_raw_grad.astype(BF16).reshape(rows, tensors, q_cols),
+            key_raw_grad.astype(BF16).reshape(rows, tensors, k_cols),
+            kv_grad[1].astype(BF16).reshape(rows, tensors, k_cols),
+        ],
+        axis=2,
+    )
+    normed_grad_part = dot32(raw_grad_low, in_weight, "mtc,tkc->mk")
+    normed_grad = scatter_sum(normed_grad_part.astype(BF16).reshape(count, own_rows, width))
+    in_weight_grad = shards_of(dot32(normed_low, raw_grad_low, "mk,mtc->tkc"))
+    in_weight_grad = in_weight_grad.reshape(-1, count, in_width)
+    query_weight_grad = in_weight_grad[..., :q_cols].reshape(w_query.shape)
+    key_weight_grad = in_weight_grad[..., q_cols : q_cols + k_cols].reshape(w_key.shape)
+    value_weight_grad = in_weight_grad[..., q_cols + k_cols :].reshape(w_value.shape)
+    stream_norm_grad, attn_gain_grad = attn_norm_pullback(normed_grad)
+    input_grad = with_twin((middle_grad + stream_norm_grad).astype(BF16))[None]
+
+    gain_grads = jnp.concatenate(
+        [
+            attn_gain_grad.reshape(-1, piece),
+            mlp_gain_grad.reshape(-1, piece),
+            query_gain_grad.reshape(-1, small),
+            key_gain_grad.reshape(-1, small),
+        ],
+        axis=1,
+    )
+    gain_grads = lax.psum(gain_grads, ("dp", "ctx", "tensor"))
+    owner = lax.axis_index("dp") * count + rank
+    gain_grads = lax.dynamic_index_in_dim(gain_grads, owner, 0, keepdims=False)
+    return (
+        output,
+        input_grad,
+        gain_grads[:piece],
+        query_weight_grad,
+        key_weight_grad,
+        value_weight_grad,
+        gain_grads[2 * piece : 2 * piece + small],
+        gain_grads[2 * piece + small :],
+        out_weight_grad,
+        gain_grads[piece : 2 * piece],
+        gate_weight_grad,
+        up_weight_grad,
+        down_weight_grad,
+    )
+
+
+def can_slice(mesh, inputs, w_key, w_gate):
+    tensors, count = mesh.shape["tensor"], mesh.shape["ctx"]
+    return (
+        tensors == 2
+        and inputs.shape[0] == mesh.shape["dp"]
+        and (inputs.shape[1] // count) % (16 * tensors) == 0
+        and w_key.shape[1] % (tensors * count * HEAD_DIM) == 0
+        and w_gate.shape[1] % (tensors * count * 128) == 0
+    )
+
+
+def from_behind(value, axis, steps):
+    return shift(value, axis, steps)
 
 
 def on_device(
@@ -365,6 +668,11 @@
         P(("dp", "ctx"), "tensor"),
         P("tensor", ("dp", "ctx")),
     )
-    return jax.shard_map(
-        on_device, mesh=mesh, in_specs=in_specs, out_specs=out_specs, check_vma=False
-    )
+
+    def step(*args):
+        body = on_device_sliced if can_slice(mesh, args[0], args[6], args[12]) else on_device
+        return jax.shard_map(
+            body, mesh=mesh, in_specs=in_specs, out_specs=out_specs, check_vma=False
+        )(*args)
+
+    return step

time: 2010 us -> 1060 us (0.53)
  waiting for transfers between devices: 1530 us -> 476 us
  local copies, waits for them, and re-layouts: 38 us -> 110 us
  starting transfers between devices: 20.7 us -> 77.8 us
  matrix products: 168 us -> 118 us
  blocking collectives: 173 us -> 200 us
    reduce_scatter x7 -> x5, waiting for transfers between devices: 1040 us -> 198 us  [the longest x1 153 us: on_device_sliced(): lax.psum_scatter(out_weight_grad.reshape(tensors * width, head_rows), ('t...]
    all_gather x9 -> x5, waiting for transfers between devices: 428 us -> 0.01 us  [the longest x4 0.01 us: slices_of(): full = lax.all_gather(mine, ('tensor', 'dp'), axis=0, tiled=True)]
    ppermute x16 -> x52, waiting for transfers between devices: 27.8 us -> 278 us  [shift(): return lax.ppermute(value, axis, pairs)]
    dot_general x43 -> x20, matrix products: 168 us -> 109 us  [dot32(): return jnp.einsum(spec, left, right, preferred_element_type=F32)]
    ppermute x16 -> x52, starting transfers between devices: 19.8 us -> 77.2 us  [shift(): return lax.ppermute(value, axis, pairs)]
    convert_element_type x1 -> x12, local copies, waits for them, and re-layouts: 1.24 us -> 49 us  [the longest x4 32.3 us: shards_of(): flat = partial.astype(BF16).reshape(-1, width)]
    psum x1, blocking collectives: 4.94 us -> 52.2 us  [on_device_sliced(): gain_grads = lax.psum(gain_grads, ('dp', 'ctx', 'tensor'))]
    psum x3 -> x0, waiting for transfers between devices: 31.9 us -> none  [the longest x1 28.6 us: on_device(): lax.psum(mid_grad_part.astype(jnp.bfloat16), 'tensor').astype(jnp.float32)]
  transfers between devices with their start and end apart: 35 -> 62, of which waited for: 26 -> 28; matrix products, arithmetic and copies ran while one was open for 9% -> 19% of each run, Pallas kernels for 0% -> 0%
where the time goes in v1:
time: 1060 us; the launch traced here: 1050 us
  waiting for transfers between devices  476 us (45%)
  blocking collectives  200 us (19%)
  matrix products  118 us (11%)
  local copies, waits for them, and re-layouts  110 us (10%)
  starting transfers between devices  77.8 us (7%)
  other arithmetic  55.5 us (5%)
  between operations  16.7 us (2%)
    ppermute x52, waiting for transfers between devices, shift(): return lax.ppermute(value, axis, pairs)  278 us
    reduce_scatter x1, waiting for transfers between devices, on_device_sliced(): lax.psum_scatter(out_weight_grad.reshape(tensors * width, head_rows), ('t...  153 us
    dot_general x20, matrix products, dot32(): return jnp.einsum(spec, left, right, preferred_element_type=F32)  109 us
    all_gather x1, blocking collectives, on_device_sliced(): lax.all_gather(jnp.stack([segment_ids[0], positions[0]]), 'ctx', axis=0)  78.2 us
    ppermute x52, starting transfers between devices, shift(): return lax.ppermute(value, axis, pairs)  77.2 us
    unnamed x1, blocking collectives  69.7 us
    psum x1, blocking collectives, on_device_sliced(): gain_grads = lax.psum(gain_grads, ('dp', 'ctx', 'tensor'))  52.2 us
    reduce_scatter x4, waiting for transfers between devices, shards_of(): lax.psum_scatter(flat, ('tensor', 'dp'), scatter_dimension=0, tiled=True)  44.6 us
  transfers between devices with their start and end apart: 62, of which 28 were waited for; matrix products, arithmetic and copies ran while one was open for 19% of the time, Pallas kernels for 0%

profile of v1, /device:TPU:0, one launch (start us, length us, event | category | flops | bytes accessed | tf_op | source)
XLA Modules:
  0.0 1053.9 jit_solution(16120850212495904573)
XLA Ops:
  10.7 5.1 collective-permute-start.5
  16.9 2.9 collective-permute-done.5
  19.7 7.3 collective-permute-done.4
  34.8 2.2 collective-permute-done.12
  37.0 12.7 %collective-permute-done.11 = bf16[128,768]{0,1:T(8,128)(2,1)S(1)} collective-permute-done((bf16[128,768]{0,1:T(8,128)(2,1)S(1)}, bf16[128,768]{0,1:T(8,128)(2,1)S(1)}, u32[]{:S(2)}, u32[]{:S(2)}) %collective-permute-start.11) | collective-permute-done | bytes 196640 | tf_op jit(solution)/shard_map/ppermute | solution.py:71
  61.1 11.3 %collective-permute-done.20 = bf16[128,768]{0,1:T(8,128)(2,1)S(1)} collective-permute-done((bf16[128,768]{0,1:T(8,128)(2,1)S(1)}, bf16[128,768]{0,1:T(8,128)(2,1)S(1)}, u32[]{:S(2)}, u32[]{:S(2)}) %collective-permute-start.20) | collective-permute-done | bytes 196640 | tf_op jit(solution)/shard_map/ppermute | solution.py:71
  72.5 15.7 %collective-permute-done.17 = bf16[128,768]{0,1:T(8,128)(2,1)S(1)} collective-permute-done((bf16[128,768]{0,1:T(8,128)(2,1)S(1)}, bf16[128,768]{0,1:T(8,128)(2,1)S(1)}, u32[]{:S(2)}, u32[]{:S(2)}) %collective-permute-start.17) | collective-permute-done | bytes 196640 | tf_op jit(solution)/shard_map/ppermute | solution.py:71
  94.1 69.7 %all-reduce.4 = bf16[4352]{0:T(1024)(128)(2,1)S(1)} all-reduce(bf16[4352]{0:T(1024)(128)(2,1)S(1)} %dynamic-update-slice), channel_id=2, replica_groups=mesh['dp'=4,'ctx'=4,'tensor'=2] {'dp','ctx'}, use_global_device_ids=true, to_apply=%add.4 | all-reduce | flops 4352 | bytes 17408
  169.5 3.8 collective-permute-start.28
  173.3 78.2 %all-gather.2 = s32[4,2,256]{2,1,0:T(2,128)S(1)} all-gather(s32[1,2,256]{2,1,0:T(2,128)S(1)} %add_bitcast_fusion), channel_id=3, replica_groups=mesh['dp'=4,'ctx'=4,'tensor'=2] {'ctx'}, dimensions={0}, use_global_device_ids=true | all-gather | bytes 10240 | tf_op jit(solution)/shard_map/all_gather | solution.py:198
  257.7 3.1 pad_maximum_fusion
  260.8 5.2 fusion.121
  275.9 12.7 %collective-permute-done.6 = bf16[2,512,2,128]{1,3,2,0:T(8,128)(2,1)} collective-permute-done((bf16[2,512,2,128]{1,3,2,0:T(8,128)(2,1)}, bf16[2,512,2,128]{1,3,2,0:T(8,128)(2,1)}, u32[]{:S(2)}, u32[]{:S(2)}) %collective-permute-start.6) | collective-permute-done | bytes 524320 | tf_op jit(solution)/shard_map/ppermute | solution.py:71
  290.8 9.2 fusion.120
  300.6 4.4 fusion.36
  305.2 3.4 collective-permute-start.7
  309.4 3.0 collective-permute-done.7
  312.5 7.5 collective-permute-done.8
  321.7 11.9 %copy.237 = bf16[4096,1024]{1,0:T(8,128)(2,1)} copy(bf16[4096,1024]{0,1:T(8,128)(2,1)} %all-gather.11.cloned.1.call-done) | data formatting | bytes 16777216 | tf_op jit(solution)/shard_map/all_gather | solution.py:181
  333.6 6.6 multiply_reduce_fusion.4
  340.4 2.6 collective-permute-start.15
  345.7 3.0 pad_maximum_fusion.2
  348.9 6.6 collective-permute-done.15
  355.4 33.8 %collective-permute-done.14 = bf16[128,2048]{1,0:T(8,128)(2,1)S(1)} collective-permute-done((bf16[128,2048]{1,0:T(8,128)(2,1)S(1)}, bf16[128,2048]{1,0:T(8,128)(2,1)S(1)}, u32[]{:S(2)}, u32[]{:S(2)}) %collective-permute-start.14) | collective-permute-done | bytes 524320 | tf_op jit(solution)/shard_map/ppermute | solution.py:71
  390.8 8.6 fusion.122
  399.4 8.5 fusion.123
  408.0 10.6 %fusion.14 = (bf16[2,512,768]{1,2,0:T(8,128)(2,1)S(1)}, bf16[2,512,768]{1,2,0:T(8,128)(2,1)S(1)}, bf16[2,512,768]{1,2,0:T(8,128)(2,1)S(1)}) fusion(f32[2,768,512]{2,1,0:T(8,128)} %fusion.122, f32[2,768,512]{2,1,0:T(8,128)} %fusion.123, bf16[2,2048,768]{2,1,0:T(8,128)(2,1)} %bitcast.518, bf16[512,2048,1]{1,0,2:T(8,128)(2,1)} %bitcast.456), kind=kOutput, calls=%fused_computation.30 | convolution fusion | flops 3233808384 | bytes 19398656 | tf_op jit(solution)/shard_map/mk,tkc->tmc/dot_general | solution.py:65
  418.6 7.3 fusion.124
  425.9 3.7 fusion.7
  430.8 2.9 collective-permute-start.29
  433.8 3.7 bitcast_convert_fusion.1
  439.8 6.8 collective-permute-done.31
  446.6 22.5 %collective-permute-done.30 = bf16[128,2048]{1,0:T(8,128)(2,1)S(1)} collective-permute-done((bf16[128,2048]{1,0:T(8,128)(2,1)S(1)}, bf16[128,2048]{1,0:T(8,128)(2,1)S(1)}, u32[]{:S(2)}, u32[]{:S(2)}) %collective-permute-start.30) | collective-permute-done | bytes 524320 | tf_op jit(solution)/shard_map/ppermute | solution.py:71
  470.3 10.1 collective-permute-done.24
  480.4 32.2 %collective-permute-done.23 = bf16[128,2048]{1,0:T(8,128)(2,1)S(1)} collective-permute-done((bf16[128,2048]{1,0:T(8,128)(2,1)S(1)}, bf16[128,2048]{1,0:T(8,128)(2,1)S(1)}, u32[]{:S(2)}, u32[]{:S(2)}) %collective-permute-start.23) | collective-permute-done | bytes 524320 | tf_op jit(solution)/shard_map/ppermute | solution.py:71
  516.1 11.6 %collective-permute-start.34 = (bf16[128,2,256]{2,0,1:T(8,128)(2,1)S(1)}, bf16[128,2,256]{2,0,1:T(8,128)(2,1)S(1)}, u32[]{:S(2)}, u32[]{:S(2)}) collective-permute-start(bf16[128,2,256]{2,0,1:T(8,128)(2,1)S(1)} %get-tuple-element.132), channel_id=1, source_target_pairs={{0,6},{2,0},{4,2},{6,4},{1,7},{3,1},{5,3},{7,5},{8,14},{10,8},{12,... | collective-permute-start | bytes 393224 | tf_op jit(solution)/shard_map/ppermute | solution.py:71
  528.6 3.0 collective-permute-done.34
  531.6 7.9 collective-permute-done.33
  544.5 4.9 fusion.1
  549.4 4.9 fusion.24
  554.4 5.0 fusion.3
  566.7 8.7 collective-permute-done.35
  581.9 6.2 convert_bitcast_fusion.4
  588.1 6.2 copy.266
  596.0 6.7 convert_bitcast_fusion.3
  602.7 8.8 copy.272
  611.6 6.7 convert_bitcast_fusion.2
  618.3 8.5 copy.274
  628.4 6.7 convert_bitcast_fusion.1
  635.2 8.7 copy.276
  644.9 5.7 convert_bitcast_fusion
  650.6 12.4 %copy.271 = bf16[2,2048,1024]{2,1,0:T(8,128)(2,1)} copy(bf16[2,2048,1024]{1,2,0:T(8,128)(2,1)} %convert_bitcast_fusion) | data formatting | bytes 16777216 | tf_op jit(solution)/shard_map/convert_element_type | solution.py:278
  664.5 4.5 bitcast_convert_fusion
  673.6 2.9 collective-permute-start.36
  676.6 4.5 collective-permute-done.25
  682.2 6.2 collective-permute-done.38
  688.4 19.8 %collective-permute-done.37 = bf16[128,2048]{1,0:T(8,128)(2,1)} collective-permute-done((bf16[128,2048]{1,0:T(8,128)(2,1)}, bf16[128,2048]{1,0:T(8,128)(2,1)}, u32[]{:S(2)}, u32[]{:S(2)}) %collective-permute-start.37) | collective-permute-done | bytes 524320 | tf_op jit(solution)/shard_map/ppermute | solution.py:71
  714.6 52.2 %psum.7 = f32[16,272]{1,0:T(8,128)S(1)} all-reduce(f32[16,272]{1,0:T(8,128)S(1)} %pad_maximum_fusion.19), channel_id=1, replica_groups=mesh['dp'=4,'ctx'=4,'tensor'=2] {'dp','ctx','tensor'}, use_global_device_ids=true, to_apply=%region_15.16 | all-reduce | flops 4352 | bytes 34816 | tf_op jit(solution)/shard_map/psum | solution.py:331
  775.1 8.4 collective-permute-done.41
  796.4 44.6 %reduce-scatter.14.cloned.1.call-done = bf16[512,768]{1,0:T(8,128)(2,1)} async-done(((bf16[4096,768]{1,0:T(8,128)(2,1)}), bf16[512,768]{1,0:T(8,128)(2,1)}) %reduce-scatter.14.cloned.1.call-update) | async-done | bytes 786448 | tf_op jit(solution)/shard_map/reduce_scatter | solution.py:129
  844.7 2.4 collective-permute-start.51
  849.9 3.0 collective-permute-done.46
  861.4 26.6 %collective-permute-done.50 = bf16[128,768]{1,0:T(8,128)(2,1)} collective-permute-done((bf16[128,768]{1,0:T(8,128)(2,1)}, bf16[128,768]{1,0:T(8,128)(2,1)}, u32[]{:S(2)}, u32[]{:S(2)}) %collective-permute-start.50) | collective-permute-done | bytes 196640 | tf_op jit(solution)/shard_map/ppermute | solution.py:71
  891.4 153.2 %reduce-scatter.8.cloned.1.call-done = bf16[128,1024]{1,0:T(8,128)(2,1)} async-done(((bf16[4096,1024]{1,0:T(8,128)(2,1)}), bf16[128,1024]{1,0:T(8,128)(2,1)}) %reduce-scatter.8.cloned.1.call-update) | async-done | bytes 262160 | tf_op jit(solution)/shard_map/reduce_scatter | solution.py:280
  (393 shorter events, 146.8 us)
Async XLA Ops:
  7.2 253.6 %all-gather.9.cloned.1.call-start = ((), (), s32[]{:S(2)}) async-start(), calls=%async_computation.5 | async-start | bytes 4718592 | tf_op jit(solution)/shard_map/all_gather | solution.py:120
  10.7 9.0 collective-permute-start.5
  15.8 11.2 %collective-permute-start.4 = (bf16[128,512]{0,1:T(8,128)(2,1)S(1)}, bf16[128,512]{0,1:T(8,128)(2,1)S(1)}, u32[]{:S(2)}, u32[]{:S(2)}) collective-permute-start(bf16[128,512]{0,1:T(8,128)(2,1)S(1)} %get-tuple-element.138), channel_id=1, source_target_pairs={{0,4},{2,6},{4,0},{6,2},{1,5},{3,7},{5,1},{7,3},{8,12},{10,14},{12... | collective-permute-start | bytes 393224 | tf_op jit(solution)/shard_map/ppermute | solution.py:71
  15.9 11.2 %collective-permute-start.3 = (bf16[128,512]{0,1:T(8,128)(2,1)S(1)}, bf16[128,512]{0,1:T(8,128)(2,1)S(1)}, u32[]{:S(2)}, u32[]{:S(2)}) collective-permute-start(bf16[128,512]{0,1:T(8,128)(2,1)S(1)} %get-tuple-element.137), channel_id=1, source_target_pairs={{0,2},{2,4},{4,6},{6,0},{1,3},{3,5},{5,7},{7,1},{8,10},{10,12},{12... | collective-permute-start | bytes 393224 | tf_op jit(solution)/shard_map/ppermute | solution.py:71
  28.5 293.2 %all-gather.11.cloned.1.call-start = ((), (), s32[]{:S(2)}) async-start(), calls=%async_computation.6 | async-start | bytes 8650752 | tf_op jit(solution)/shard_map/all_gather | solution.py:181
  29.3 361.5 %all-gather.13.cloned.1.call-start = ((), (), s32[]{:S(2)}) async-start(), calls=%async_computation.7 | async-start | bytes 7077888 | tf_op jit(solution)/shard_map/all_gather | solution.py:120
  30.1 6.9 collective-permute-start.12
  31.7 18.1 %collective-permute-start.11 = (bf16[128,768]{0,1:T(8,128)(2,1)S(1)}, bf16[128,768]{0,1:T(8,128)(2,1)S(1)}, u32[]{:S(2)}, u32[]{:S(2)}) collective-permute-start(bf16[128,768]{0,1:T(8,128)(2,1)S(1)} %get-tuple-element.116), channel_id=1, source_target_pairs={{0,4},{2,6},{4,0},{6,2},{1,5},{3,7},{5,1},{7,3},{8,12},{10,14},{12... | collective-permute-start | bytes 589832 | tf_op jit(solution)/shard_map/ppermute | solution.py:71
  32.8 16.9 %collective-permute-start.10 = (bf16[128,768]{0,1:T(8,128)(2,1)S(1)}, bf16[128,768]{0,1:T(8,128)(2,1)S(1)}, u32[]{:S(2)}, u32[]{:S(2)}) collective-permute-start(bf16[128,768]{0,1:T(8,128)(2,1)S(1)} %get-tuple-element.115), channel_id=1, source_target_pairs={{0,2},{2,4},{4,6},{6,0},{1,3},{3,5},{5,7},{7,1},{8,10},{10,12},{12... | collective-permute-start | bytes 589832 | tf_op jit(solution)/shard_map/ppermute | solution.py:71
  51.6 347.8 %all-gather.15.cloned.1.call-start = ((), (), s32[]{:S(2)}) async-start(), calls=%async_computation.8 | async-start | bytes 7077888 | tf_op jit(solution)/shard_map/all_gather | solution.py:120
  52.7 6.7 collective-permute-start.21
  52.7 19.7 %collective-permute-start.20 = (bf16[128,768]{0,1:T(8,128)(2,1)S(1)}, bf16[128,768]{0,1:T(8,128)(2,1)S(1)}, u32[]{:S(2)}, u32[]{:S(2)}) collective-permute-start(bf16[128,768]{0,1:T(8,128)(2,1)S(1)} %get-tuple-element.112), channel_id=1, source_target_pairs={{0,4},{2,6},{4,0},{6,2},{1,5},{3,7},{5,1},{7,3},{8,12},{10,14},{12... | collective-permute-start | bytes 589832 | tf_op jit(solution)/shard_map/ppermute | solution.py:71
  53.4 19.0 %collective-permute-start.19 = (bf16[128,768]{0,1:T(8,128)(2,1)S(1)}, bf16[128,768]{0,1:T(8,128)(2,1)S(1)}, u32[]{:S(2)}, u32[]{:S(2)}) collective-permute-start(bf16[128,768]{0,1:T(8,128)(2,1)S(1)} %get-tuple-element.111), channel_id=1, source_target_pairs={{0,2},{2,4},{4,6},{6,0},{1,3},{3,5},{5,7},{7,1},{8,10},{10,12},{12... | collective-permute-start | bytes 589832 | tf_op jit(solution)/shard_map/ppermute | solution.py:71
  56.8 15.7 %collective-permute-start.18 = (bf16[128,768]{0,1:T(8,128)(2,1)S(1)}, bf16[128,768]{0,1:T(8,128)(2,1)S(1)}, u32[]{:S(2)}, u32[]{:S(2)}) collective-permute-start(bf16[128,768]{0,1:T(8,128)(2,1)S(1)} %get-tuple-element.122), channel_id=1, source_target_pairs={{0,6},{2,0},{4,2},{6,4},{1,7},{3,1},{5,3},{7,5},{8,14},{10,8},{12,... | collective-permute-start | bytes 589832 | tf_op jit(solution)/shard_map/ppermute | solution.py:71
  58.6 29.5 %collective-permute-start.17 = (bf16[128,768]{0,1:T(8,128)(2,1)S(1)}, bf16[128,768]{0,1:T(8,128)(2,1)S(1)}, u32[]{:S(2)}, u32[]{:S(2)}) collective-permute-start(bf16[128,768]{0,1:T(8,128)(2,1)S(1)} %get-tuple-element.120), channel_id=1, source_target_pairs={{0,4},{2,6},{4,0},{6,2},{1,5},{3,7},{5,1},{7,3},{8,12},{10,14},{12... | collective-permute-start | bytes 589832 | tf_op jit(solution)/shard_map/ppermute | solution.py:71
  59.3 28.8 %collective-permute-start.16 = (bf16[128,768]{0,1:T(8,128)(2,1)S(1)}, bf16[128,768]{0,1:T(8,128)(2,1)S(1)}, u32[]{:S(2)}, u32[]{:S(2)}) collective-permute-start(bf16[128,768]{0,1:T(8,128)(2,1)S(1)} %get-tuple-element.119), channel_id=1, source_target_pairs={{0,2},{2,4},{4,6},{6,0},{1,3},{3,5},{5,7},{7,1},{8,10},{10,12},{12... | collective-permute-start | bytes 589832 | tf_op jit(solution)/shard_map/ppermute | solution.py:71
  92.5 315.4 %all-gather.17.cloned.1.call-start = ((), (), s32[]{:S(2)}) async-start(), calls=%async_computation.9 | async-start | bytes 7077888 | tf_op jit(solution)/shard_map/all_gather | solution.py:120
  164.1 93.2 %copy-start.42 = (f32[128]{0:T(128)}, f32[128]{0:T(128)S(1)}, u32[]{:S(2)}) copy-start(f32[128]{0:T(128)S(1)} %fusion.107) | copy-start | bytes 1540
  164.1 93.2 %copy-start.29 = (f32[2048]{0:T(1024)}, f32[2048]{0:T(1024)S(1)}, u32[]{:S(2)}) copy-start(f32[2048]{0:T(1024)S(1)} %get-tuple-element.146) | copy-start | bytes 24580
  165.1 92.3 %collective-permute-start.2 = (bf16[128,2048]{1,0:T(8,128)(2,1)}, bf16[128,2048]{1,0:T(8,128)(2,1)}, u32[]{:S(2)}, u32[]{:S(2)}) collective-permute-start(bf16[128,2048]{1,0:T(8,128)(2,1)} %fusion.39), channel_id=1, source_target_pairs={{0,6},{2,0},{4,2},{6,4},{1,7},{3,1},{5,3},{7,5},{8,14},{10,8},{12,... | collective-permute-start | bytes 1572872 | tf_op jit(solution)/shard_map/ppermute | solution.py:71
  166.4 91.2 %collective-permute-start.1 = (bf16[128,2048]{1,0:T(8,128)(2,1)}, bf16[128,2048]{1,0:T(8,128)(2,1)}, u32[]{:S(2)}, u32[]{:S(2)}) collective-permute-start(bf16[128,2048]{1,0:T(8,128)(2,1)} %fusion.39), channel_id=1, source_target_pairs={{0,4},{2,6},{4,0},{6,2},{1,5},{3,7},{5,1},{7,3},{8,12},{10,14},{12... | collective-permute-start | bytes 1572872 | tf_op jit(solution)/shard_map/ppermute | solution.py:71
  168.6 89.0 %collective-permute-start = (bf16[128,2048]{1,0:T(8,128)(2,1)}, bf16[128,2048]{1,0:T(8,128)(2,1)}, u32[]{:S(2)}, u32[]{:S(2)}) collective-permute-start(bf16[128,2048]{1,0:T(8,128)(2,1)} %fusion.39), channel_id=1, source_target_pairs={{0,2},{2,4},{4,6},{6,0},{1,3},{3,5},{5,7},{7,1},{8,10},{10,12},{12... | collective-permute-start | bytes 1572872 | tf_op jit(solution)/shard_map/ppermute | solution.py:71
  169.5 174.1 %collective-permute-start.28 = (bf16[128,2048]{1,0:T(8,128)(2,1)}, bf16[128,2048]{1,0:T(8,128)(2,1)}, u32[]{:S(2)}, u32[]{:S(2)}) collective-permute-start(bf16[128,2048]{1,0:T(8,128)(2,1)} %fusion.155), channel_id=1, source_target_pairs={{0,6},{2,0},{4,2},{6,4},{1,7},{3,1},{5,3},{7,5},{8,14},{10,8},{12,... | collective-permute-start | bytes 1572872 | tf_op jit(solution)/shard_map/ppermute | solution.py:71
  173.3 172.4 %collective-permute-start.27 = (bf16[128,2048]{1,0:T(8,128)(2,1)}, bf16[128,2048]{1,0:T(8,128)(2,1)}, u32[]{:S(2)}, u32[]{:S(2)}) collective-permute-start(bf16[128,2048]{1,0:T(8,128)(2,1)} %fusion.155), channel_id=1, source_target_pairs={{0,4},{2,6},{4,0},{6,2},{1,5},{3,7},{5,1},{7,3},{8,12},{10,14},{12... | collective-permute-start | bytes 1572872 | tf_op jit(solution)/shard_map/ppermute | solution.py:71
  257.4 510.8 %reduce-scatter.6.cloned.1.call-start = ((), (), s32[]{:S(2)}) async-start(), calls=%async_computation.10 | async-start | bytes 4718592 | tf_op jit(solution)/shard_map/reduce_scatter | solution.py:129
  257.4 88.3 %collective-permute-start.26 = (bf16[128,2048]{1,0:T(8,128)(2,1)}, bf16[128,2048]{1,0:T(8,128)(2,1)}, u32[]{:S(2)}, u32[]{:S(2)}) collective-permute-start(bf16[128,2048]{1,0:T(8,128)(2,1)} %fusion.155), channel_id=1, source_target_pairs={{0,2},{2,4},{4,6},{6,0},{1,3},{3,5},{5,7},{7,1},{8,10},{10,12},{12... | collective-permute-start | bytes 1572872 | tf_op jit(solution)/shard_map/ppermute | solution.py:71
  268.3 20.3 %collective-permute-start.6 = (bf16[2,512,2,128]{1,3,2,0:T(8,128)(2,1)}, bf16[2,512,2,128]{1,3,2,0:T(8,128)(2,1)}, u32[]{:S(2)}, u32[]{:S(2)}) collective-permute-start(bf16[2,512,2,128]{1,3,2,0:T(8,128)(2,1)} %pad_maximum_fusion.12), channel_id=1, source_target_pairs={{0,1},{1,0},{2,3},{3,2},{4,5},{5,4},{6,7},{7,6},{8,9},{9,8},{10,11... | collective-permute-start | bytes 1572872 | tf_op jit(solution)/shard_map/ppermute | solution.py:71
  305.2 7.3 collective-permute-start.7
  309.4 10.6 %collective-permute-start.8 = (bf16[128,2,256]{0,2,1:T(8,128)(2,1)S(1)}, bf16[128,2,256]{0,2,1:T(8,128)(2,1)S(1)}, u32[]{:S(2)}, u32[]{:S(2)}) collective-permute-start(bf16[128,2,256]{0,2,1:T(8,128)(2,1)S(1)} %bitcast.503), channel_id=1, source_target_pairs={{0,4},{2,6},{4,0},{6,2},{1,5},{3,7},{5,1},{7,3},{8,12},{10,14},{12... | collective-permute-start | bytes 393224 | tf_op jit(solution)/shard_map/ppermute | solution.py:71
  312.4 7.6 collective-permute-start.9
  340.4 15.0 %collective-permute-start.15 = (bf16[128,2048]{1,0:T(8,128)(2,1)S(1)}, bf16[128,2048]{1,0:T(8,128)(2,1)S(1)}, u32[]{:S(2)}, u32[]{:S(2)}) collective-permute-start(bf16[128,2048]{1,0:T(8,128)(2,1)S(1)} %multiply_convert_fusion), channel_id=1, source_target_pairs={{0,6},{2,0},{4,2},{6,4},{1,7},{3,1},{5,3},{7,5},{8,14},{10,8},{12,... | collective-permute-start | bytes 1572872 | tf_op jit(solution)/shard_map/ppermute | solution.py:71
  343.0 46.2 %collective-permute-start.14 = (bf16[128,2048]{1,0:T(8,128)(2,1)S(1)}, bf16[128,2048]{1,0:T(8,128)(2,1)S(1)}, u32[]{:S(2)}, u32[]{:S(2)}) collective-permute-start(bf16[128,2048]{1,0:T(8,128)(2,1)S(1)} %multiply_convert_fusion), channel_id=1, source_target_pairs={{0,4},{2,6},{4,0},{6,2},{1,5},{3,7},{5,1},{7,3},{8,12},{10,14},{12... | collective-permute-start | bytes 1572872 | tf_op jit(solution)/shard_map/ppermute | solution.py:71
  343.6 45.7 %collective-permute-start.13 = (bf16[128,2048]{1,0:T(8,128)(2,1)S(1)}, bf16[128,2048]{1,0:T(8,128)(2,1)S(1)}, u32[]{:S(2)}, u32[]{:S(2)}) collective-permute-start(bf16[128,2048]{1,0:T(8,128)(2,1)S(1)} %multiply_convert_fusion), channel_id=1, source_target_pairs={{0,2},{2,4},{4,6},{6,0},{1,3},{3,5},{5,7},{7,1},{8,10},{10,12},{12... | collective-permute-start | bytes 1572872 | tf_op jit(solution)/shard_map/ppermute | solution.py:71
  429.9 16.7 %collective-permute-start.31 = (bf16[128,2048]{1,0:T(8,128)(2,1)S(1)}, bf16[128,2048]{1,0:T(8,128)(2,1)S(1)}, u32[]{:S(2)}, u32[]{:S(2)}) collective-permute-start(bf16[128,2048]{1,0:T(8,128)(2,1)S(1)} %get-tuple-element.80), channel_id=1, source_target_pairs={{0,2},{2,4},{4,6},{6,0},{1,3},{3,5},{5,7},{7,1},{8,10},{10,12},{12... | collective-permute-start | bytes 1572872 | tf_op jit(solution)/shard_map/ppermute | solution.py:71
  430.0 39.2 %collective-permute-start.30 = (bf16[128,2048]{1,0:T(8,128)(2,1)S(1)}, bf16[128,2048]{1,0:T(8,128)(2,1)S(1)}, u32[]{:S(2)}, u32[]{:S(2)}) collective-permute-start(bf16[128,2048]{1,0:T(8,128)(2,1)S(1)} %get-tuple-element.81), channel_id=1, source_target_pairs={{0,4},{2,6},{4,0},{6,2},{1,5},{3,7},{5,1},{7,3},{8,12},{10,14},{12... | collective-permute-start | bytes 1572872 | tf_op jit(solution)/shard_map/ppermute | solution.py:71
  430.8 38.3 %collective-permute-start.29 = (bf16[128,2048]{1,0:T(8,128)(2,1)S(1)}, bf16[128,2048]{1,0:T(8,128)(2,1)S(1)}, u32[]{:S(2)}, u32[]{:S(2)}) collective-permute-start(bf16[128,2048]{1,0:T(8,128)(2,1)S(1)} %get-tuple-element.79), channel_id=1, source_target_pairs={{0,6},{2,0},{4,2},{6,4},{1,7},{3,1},{5,3},{7,5},{8,14},{10,8},{12,... | collective-permute-start | bytes 1572872 | tf_op jit(solution)/shard_map/ppermute | solution.py:71
  437.6 42.8 %collective-permute-start.24 = (bf16[128,2048]{1,0:T(8,128)(2,1)S(1)}, bf16[128,2048]{1,0:T(8,128)(2,1)S(1)}, u32[]{:S(2)}, u32[]{:S(2)}) collective-permute-start(bf16[128,2048]{1,0:T(8,128)(2,1)S(1)} %get-tuple-element.83), channel_id=1, source_target_pairs={{0,2},{2,4},{4,6},{6,0},{1,3},{3,5},{5,7},{7,1},{8,10},{10,12},{12... | collective-permute-start | bytes 1572872 | tf_op jit(solution)/shard_map/ppermute | solution.py:71
  438.3 74.3 %collective-permute-start.23 = (bf16[128,2048]{1,0:T(8,128)(2,1)S(1)}, bf16[128,2048]{1,0:T(8,128)(2,1)S(1)}, u32[]{:S(2)}, u32[]{:S(2)}) collective-permute-start(bf16[128,2048]{1,0:T(8,128)(2,1)S(1)} %get-tuple-element.84), channel_id=1, source_target_pairs={{0,4},{2,6},{4,0},{6,2},{1,5},{3,7},{5,1},{7,3},{8,12},{10,14},{12... | collective-permute-start | bytes 1572872 | tf_op jit(solution)/shard_map/ppermute | solution.py:71
  446.6 65.9 %collective-permute-start.22 = (bf16[128,2048]{1,0:T(8,128)(2,1)S(1)}, bf16[128,2048]{1,0:T(8,128)(2,1)S(1)}, u32[]{:S(2)}, u32[]{:S(2)}) collective-permute-start(bf16[128,2048]{1,0:T(8,128)(2,1)S(1)} %get-tuple-element.82), channel_id=1, source_target_pairs={{0,6},{2,0},{4,2},{6,4},{1,7},{3,1},{5,3},{7,5},{8,14},{10,8},{12,... | collective-permute-start | bytes 1572872 | tf_op jit(solution)/shard_map/ppermute | solution.py:71
  516.1 15.5 %collective-permute-start.34 = (bf16[128,2,256]{2,0,1:T(8,128)(2,1)S(1)}, bf16[128,2,256]{2,0,1:T(8,128)(2,1)S(1)}, u32[]{:S(2)}, u32[]{:S(2)}) collective-permute-start(bf16[128,2,256]{2,0,1:T(8,128)(2,1)S(1)} %get-tuple-element.132), channel_id=1, source_target_pairs={{0,6},{2,0},{4,2},{6,4},{1,7},{3,1},{5,3},{7,5},{8,14},{10,8},{12,... | collective-permute-start | bytes 393224 | tf_op jit(solution)/shard_map/ppermute | solution.py:71
  527.7 11.8 %collective-permute-start.33 = (bf16[128,2,256]{2,0,1:T(8,128)(2,1)S(1)}, bf16[128,2,256]{2,0,1:T(8,128)(2,1)S(1)}, u32[]{:S(2)}, u32[]{:S(2)}) collective-permute-start(bf16[128,2,256]{2,0,1:T(8,128)(2,1)S(1)} %get-tuple-element.130), channel_id=1, source_target_pairs={{0,4},{2,6},{4,0},{6,2},{1,5},{3,7},{5,1},{7,3},{8,12},{10,14},{12... | collective-permute-start | bytes 393224 | tf_op jit(solution)/shard_map/ppermute | solution.py:71
  528.5 11.0 %collective-permute-start.32 = (bf16[128,2,256]{2,0,1:T(8,128)(2,1)S(1)}, bf16[128,2,256]{2,0,1:T(8,128)(2,1)S(1)}, u32[]{:S(2)}, u32[]{:S(2)}) collective-permute-start(bf16[128,2,256]{2,0,1:T(8,128)(2,1)S(1)} %get-tuple-element.131), channel_id=1, source_target_pairs={{0,2},{2,4},{4,6},{6,0},{1,3},{3,5},{5,7},{7,1},{8,10},{10,12},{12... | collective-permute-start | bytes 393224 | tf_op jit(solution)/shard_map/ppermute | solution.py:71
  562.5 12.9 %collective-permute-start.35 = (bf16[2,512,2,128]{1,3,2,0:T(8,128)(2,1)}, bf16[2,512,2,128]{1,3,2,0:T(8,128)(2,1)}, u32[]{:S(2)}, u32[]{:S(2)}) collective-permute-start(bf16[2,512,2,128]{1,3,2,0:T(8,128)(2,1)} %fusion.51), channel_id=1, source_target_pairs={{0,1},{1,0},{2,3},{3,2},{4,5},{5,4},{6,7},{7,6},{8,9},{9,8},{10,11... | collective-permute-start | bytes 1572872 | tf_op jit(solution)/shard_map/ppermute | solution.py:71
  594.4 192.9 %reduce-scatter.10.cloned.1.call-start = ((), (), s32[]{:S(2)}) async-start(), calls=%async_computation.12 | async-start | bytes 7077888 | tf_op jit(solution)/shard_map/reduce_scatter | solution.py:129
  611.5 180.7 %reduce-scatter.12.cloned.1.call-start = ((), (), s32[]{:S(2)}) async-start(), calls=%async_computation.13 | async-start | bytes 7077888 | tf_op jit(solution)/shard_map/reduce_scatter | solution.py:129
  626.8 214.1 %reduce-scatter.14.cloned.1.call-start = ((), (), s32[]{:S(2)}) async-start(), calls=%async_computation.14 | async-start | bytes 7077888 | tf_op jit(solution)/shard_map/reduce_scatter | solution.py:129
  643.9 400.7 %reduce-scatter.8.cloned.1.call-start = ((), (), s32[]{:S(2)}) async-start(), calls=%async_computation.11 | async-start | bytes 8650752 | tf_op jit(solution)/shard_map/reduce_scatter | solution.py:280
  664.1 17.0 %collective-permute-start.25 = (bf16[128,2048]{1,0:T(8,128)(2,1)S(1)}, bf16[128,2048]{1,0:T(8,128)(2,1)}, u32[]{:S(2)}, u32[]{:S(2)}) collective-permute-start(bf16[128,2048]{1,0:T(8,128)(2,1)S(1)} %copy-done.14), channel_id=1, source_target_pairs={{0,1},{1,0},{2,3},{3,2},{4,5},{5,4},{6,7},{7,6},{8,9},{9,8},{10,11... | collective-permute-start | bytes 1572872 | tf_op jit(solution)/shard_map/ppermute | solution.py:71
  671.6 16.9 %collective-permute-start.38 = (bf16[128,2048]{1,0:T(8,128)(2,1)}, bf16[128,2048]{1,0:T(8,128)(2,1)S(1)}, u32[]{:S(2)}, u32[]{:S(2)}) collective-permute-start(bf16[128,2048]{1,0:T(8,128)(2,1)} %get-tuple-element.77), channel_id=1, source_target_pairs={{0,2},{2,4},{4,6},{6,0},{1,3},{3,5},{5,7},{7,1},{8,10},{10,12},{12... | collective-permute-start | bytes 1572872 | tf_op jit(solution)/shard_map/ppermute | solution.py:71
  671.6 36.7 %collective-permute-start.37 = (bf16[128,2048]{1,0:T(8,128)(2,1)}, bf16[128,2048]{1,0:T(8,128)(2,1)}, u32[]{:S(2)}, u32[]{:S(2)}) collective-permute-start(bf16[128,2048]{1,0:T(8,128)(2,1)} %get-tuple-element.78), channel_id=1, source_target_pairs={{0,4},{2,6},{4,0},{6,2},{1,5},{3,7},{5,1},{7,3},{8,12},{10,14},{12... | collective-permute-start | bytes 1572872 | tf_op jit(solution)/shard_map/ppermute | solution.py:71
  673.6 34.7 %collective-permute-start.36 = (bf16[128,2048]{1,0:T(8,128)(2,1)}, bf16[128,2048]{1,0:T(8,128)(2,1)}, u32[]{:S(2)}, u32[]{:S(2)}) collective-permute-start(bf16[128,2048]{1,0:T(8,128)(2,1)} %get-tuple-element.76), channel_id=1, source_target_pairs={{0,6},{2,0},{4,2},{6,4},{1,7},{3,1},{5,3},{7,5},{8,14},{10,8},{12,... | collective-permute-start | bytes 1572872 | tf_op jit(solution)/shard_map/ppermute | solution.py:71
  711.9 56.1 %collective-permute-start.39 = (bf16[128,2048]{1,0:T(8,128)(2,1)S(1)}, bf16[128,2048]{1,0:T(8,128)(2,1)S(1)}, u32[]{:S(2)}, u32[]{:S(2)}) collective-permute-start(bf16[128,2048]{1,0:T(8,128)(2,1)S(1)} %fusion.48), channel_id=1, source_target_pairs={{0,1},{1,0},{2,3},{3,2},{4,5},{5,4},{6,7},{7,6},{8,9},{9,8},{10,11... | collective-permute-start | bytes 1572872 | tf_op jit(solution)/shard_map/ppermute | solution.py:71
  769.4 5.7 collective-permute-start.42
  771.0 12.6 %collective-permute-start.41 = (bf16[128,512]{1,0:T(8,128)(2,1)S(1)}, bf16[128,512]{1,0:T(8,128)(2,1)S(1)}, u32[]{:S(2)}, u32[]{:S(2)}) collective-permute-start(bf16[128,512]{1,0:T(8,128)(2,1)S(1)} %get-tuple-element.126), channel_id=1, source_target_pairs={{0,4},{2,6},{4,0},{6,2},{1,5},{3,7},{5,1},{7,3},{8,12},{10,14},{12... | collective-permute-start | bytes 393224 | tf_op jit(solution)/shard_map/ppermute | solution.py:71
  772.7 10.9 %collective-permute-start.40 = (bf16[128,512]{1,0:T(8,128)(2,1)S(1)}, bf16[128,512]{1,0:T(8,128)(2,1)S(1)}, u32[]{:S(2)}, u32[]{:S(2)}) collective-permute-start(bf16[128,512]{1,0:T(8,128)(2,1)S(1)} %get-tuple-element.125), channel_id=1, source_target_pairs={{0,2},{2,4},{4,6},{6,0},{1,3},{3,5},{5,7},{7,1},{8,10},{10,12},{12... | collective-permute-start | bytes 393224 | tf_op jit(solution)/shard_map/ppermute | solution.py:71
  788.9 54.4 %collective-permute-start.45 = (bf16[128,768]{1,0:T(8,128)(2,1)S(1)}, bf16[128,768]{1,0:T(8,128)(2,1)S(1)}, u32[]{:S(2)}, u32[]{:S(2)}) collective-permute-start(bf16[128,768]{1,0:T(8,128)(2,1)S(1)} %get-tuple-element.108), channel_id=1, source_target_pairs={{0,6},{2,0},{4,2},{6,4},{1,7},{3,1},{5,3},{7,5},{8,14},{10,8},{12,... | collective-permute-start | bytes 589832 | tf_op jit(solution)/shard_map/ppermute | solution.py:71
  788.9 55.8 %collective-permute-start.44 = (bf16[128,768]{1,0:T(8,128)(2,1)S(1)}, bf16[128,768]{1,0:T(8,128)(2,1)S(1)}, u32[]{:S(2)}, u32[]{:S(2)}) collective-permute-start(bf16[128,768]{1,0:T(8,128)(2,1)S(1)} %get-tuple-element.106), channel_id=1, source_target_pairs={{0,4},{2,6},{4,0},{6,2},{1,5},{3,7},{5,1},{7,3},{8,12},{10,14},{12... | collective-permute-start | bytes 589832 | tf_op jit(solution)/shard_map/ppermute | solution.py:71
  790.2 56.8 %collective-permute-start.43 = (bf16[128,768]{1,0:T(8,128)(2,1)S(1)}, bf16[128,768]{1,0:T(8,128)(2,1)S(1)}, u32[]{:S(2)}, u32[]{:S(2)}) collective-permute-start(bf16[128,768]{1,0:T(8,128)(2,1)S(1)} %get-tuple-element.105), channel_id=1, source_target_pairs={{0,2},{2,4},{4,6},{6,0},{1,3},{3,5},{5,7},{7,1},{8,10},{10,12},{12... | collective-permute-start | bytes 589832 | tf_op jit(solution)/shard_map/ppermute | solution.py:71
  794.4 53.9 %collective-permute-start.48 = (bf16[128,768]{1,0:T(8,128)(2,1)}, bf16[128,768]{1,0:T(8,128)(2,1)S(1)}, u32[]{:S(2)}, u32[]{:S(2)}) collective-permute-start(bf16[128,768]{1,0:T(8,128)(2,1)} %get-tuple-element.104), channel_id=1, source_target_pairs={{0,6},{2,0},{4,2},{6,4},{1,7},{3,1},{5,3},{7,5},{8,14},{10,8},{12,... | collective-permute-start | bytes 589832 | tf_op jit(solution)/shard_map/ppermute | solution.py:71
  796.4 53.6 %collective-permute-start.47 = (bf16[128,768]{1,0:T(8,128)(2,1)S(1)}, bf16[128,768]{1,0:T(8,128)(2,1)}, u32[]{:S(2)}, u32[]{:S(2)}) collective-permute-start(bf16[128,768]{1,0:T(8,128)(2,1)S(1)} %get-tuple-element.102), channel_id=1, source_target_pairs={{0,4},{2,6},{4,0},{6,2},{1,5},{3,7},{5,1},{7,3},{8,12},{10,14},{12... | collective-permute-start | bytes 589832 | tf_op jit(solution)/shard_map/ppermute | solution.py:71
  843.2 9.7 collective-permute-start.46
  844.7 16.7 %collective-permute-start.51 = (bf16[128,768]{1,0:T(8,128)(2,1)}, bf16[128,768]{1,0:T(8,128)(2,1)}, u32[]{:S(2)}, u32[]{:S(2)}) collective-permute-start(bf16[128,768]{1,0:T(8,128)(2,1)} %get-tuple-element.100), channel_id=1, source_target_pairs={{0,6},{2,0},{4,2},{6,4},{1,7},{3,1},{5,3},{7,5},{8,14},{10,8},{12,... | collective-permute-start | bytes 589832 | tf_op jit(solution)/shard_map/ppermute | solution.py:71
  847.1 40.9 %collective-permute-start.50 = (bf16[128,768]{1,0:T(8,128)(2,1)}, bf16[128,768]{1,0:T(8,128)(2,1)}, u32[]{:S(2)}, u32[]{:S(2)}) collective-permute-start(bf16[128,768]{1,0:T(8,128)(2,1)} %get-tuple-element.98), channel_id=1, source_target_pairs={{0,4},{2,6},{4,0},{6,2},{1,5},{3,7},{5,1},{7,3},{8,12},{10,14},{12... | collective-permute-start | bytes 589832 | tf_op jit(solution)/shard_map/ppermute | solution.py:71
  848.3 39.7 %collective-permute-start.49 = (bf16[128,768]{1,0:T(8,128)(2,1)}, bf16[128,768]{1,0:T(8,128)(2,1)}, u32[]{:S(2)}, u32[]{:S(2)}) collective-permute-start(bf16[128,768]{1,0:T(8,128)(2,1)} %get-tuple-element.97), channel_id=1, source_target_pairs={{0,2},{2,4},{4,6},{6,0},{1,3},{3,5},{5,7},{7,1},{8,10},{10,12},{12... | collective-permute-start | bytes 589832 | tf_op jit(solution)/shard_map/ppermute | solution.py:71
  (61 other events, 993.6 us)
Sparse Core Ops, SparseCore 0:
  28.6 36.8 all-gather.8
  68.4 93.8 all-gather.10
  164.7 43.2 all-gather.12
  210.4 45.3 all-gather.14
  258.1 52.4 all-gather.16
  594.5 49.4 reduce-scatter.5
  647.4 63.0 reduce-scatter.9
  713.8 61.9 reduce-scatter.11
  779.2 61.7 reduce-scatter.13
  843.1 201.4 reduce-scatter.7

commit v2 on v1

--- a/solution.py
+++ b/solution.py
@@ -3,11 +3,15 @@
 import jax
 import jax.numpy as jnp
 from jax import lax
+from jax.experimental import pallas as pl
+from jax.experimental.pallas import tpu as pltpu
 from jax.sharding import PartitionSpec as P
 
 HEAD_DIM = 128
 BF16 = jnp.bfloat16
 F32 = jnp.float32
+MESH = pl.DeviceIdType.MESH
+TILE = (8, 128)
 
 epsilon = 1e-06
 rope_base = 1000000.0
@@ -110,6 +114,120 @@
     count = lax.axis_size("ctx")
     ahead = take_ring(blocks, lax.axis_index("ctx"))
     return jnp.stack([ahead[0]] + [shift(ahead[d], "ctx", d) for d in range(1, count)])
+
+
+def greet(peers):
+    barrier = pltpu.get_barrier_semaphore()
+    for peer in peers:
+        pl.semaphore_signal(barrier, inc=1, device_id=peer, device_id_type=MESH)
+    pl.semaphore_wait(barrier, len(peers))
+
+
+def remote(source, target, send_sem, recv_sem, peer):
+    copy = pltpu.make_async_remote_copy(
+        src_ref=source,
+        dst_ref=target,
+        send_sem=send_sem,
+        recv_sem=recv_sem,
+        device_id=peer,
+        device_id_type=MESH,
+    )
+    copy.start()
+    return copy
+
+
+def to_tile(values):
+    return jnp.pad(values, (0, math.prod(TILE) - values.shape[0])).reshape(TILE)
+
+
+def spread_small(gains, marks):
+    count, pairs = lax.axis_size("ctx"), lax.axis_size("dp")
+    owners = count * pairs
+
+    def kernel(gain_ref, mark_ref, gains_ref, marks_ref, gain_send, gain_recv, mark_send, mark_recv):
+        rank = lax.axis_index("ctx")
+        me = lax.axis_index("dp") * count + rank
+        far = [lax.rem(me + k, owners) for k in range(1, owners)]
+        far = [{"dp": lax.div(t, count), "ctx": lax.rem(t, count)} for t in far]
+        near = [{"ctx": lax.rem(rank + k, count)} for k in range(1, count)]
+        greet(far)
+        copies = [
+            remote(mark_ref, marks_ref.at[rank], mark_send.at[k], mark_recv.at[k], peer)
+            for k, peer in enumerate(near)
+        ]
+        copies += [
+            remote(gain_ref, gains_ref.at[me], gain_send.at[k], gain_recv.at[k], peer)
+            for k, peer in enumerate(far)
+        ]
+        gains_ref[me] = gain_ref[...]
+        marks_ref[rank] = mark_ref[...]
+        for copy in copies:
+            copy.wait()
+
+    sems = pltpu.SemaphoreType.DMA
+    return pl.pallas_call(
+        kernel,
+        out_shape=(
+            jax.ShapeDtypeStruct((owners, *TILE), F32),
+            jax.ShapeDtypeStruct((count, *TILE), jnp.int32),
+        ),
+        in_specs=[pl.BlockSpec(memory_space=pltpu.VMEM)] * 2,
+        out_specs=(pl.BlockSpec(memory_space=pltpu.VMEM),) * 2,
+        scratch_shapes=[
+            sems((owners - 1,)),
+            sems((owners - 1,)),
+            sems((count - 1,)),
+            sems((count - 1,)),
+        ],
+        compiler_params=pltpu.CompilerParams(collective_id=0, has_side_effects=True),
+        name="spread_small",
+    )(gains, marks)
+
+
+def owner_sums(tiles):
+    count, pairs, tensors = lax.axis_size("ctx"), lax.axis_size("dp"), lax.axis_size("tensor")
+    total = count * pairs * tensors
+
+    def kernel(tiles_ref, sum_ref, got, send_sem, recv_sem):
+        owner = lax.axis_index("dp") * count + lax.axis_index("ctx")
+        me = owner * tensors + lax.axis_index("tensor")
+        targets = [lax.rem(me + k, total) for k in range(1, total)]
+        peers = [
+            {
+                "dp": lax.div(t, count * tensors),
+                "ctx": lax.rem(lax.div(t, tensors), count),
+                "tensor": lax.rem(t, tensors),
+            }
+            for t in targets
+        ]
+        greet(peers)
+        copies = [
+            remote(
+                tiles_ref.at[lax.div(t, tensors)], got.at[me], send_sem.at[k], recv_sem.at[k], peer
+            )
+            for k, (t, peer) in enumerate(zip(targets, peers))
+        ]
+        got[me] = tiles_ref[owner]
+        for copy in copies:
+            copy.wait()
+        value = got[0]
+        for source in range(1, total):
+            value = value + got[source]
+        sum_ref[...] = value
+
+    return pl.pallas_call(
+        kernel,
+        out_shape=jax.ShapeDtypeStruct(TILE, F32),
+        in_specs=[pl.BlockSpec(memory_space=pltpu.VMEM)],
+        out_specs=pl.BlockSpec(memory_space=pltpu.VMEM),
+        scratch_shapes=[
+            pltpu.VMEM((total, *TILE), F32),
+            pltpu.SemaphoreType.DMA((total - 1,)),
+            pltpu.SemaphoreType.DMA((total - 1,)),
+        ],
+        compiler_params=pltpu.CompilerParams(collective_id=1, has_side_effects=True),
+        name="owner_sums",
+    )(tiles)
 
 
 def slices_of(shard):
@@ -185,18 +303,17 @@
     up_weight = slices_of(w_up)
     down_weight = slices_of(w_down.T)
 
-    gains = lax.all_gather(
-        jnp.concatenate([attn_gain, mlp_gain, q_gain, k_gain]), ("dp", "ctx"), axis=0
-    )
     piece = attn_gain.shape[0]
     small = q_gain.shape[0]
-    attn_scale = gains[:, :piece].reshape(-1).astype(F32)
-    mlp_scale = gains[:, piece : 2 * piece].reshape(-1).astype(F32)
-    query_scale = gains[:, 2 * piece : 2 * piece + small].reshape(-1).astype(F32)
-    key_scale = gains[:, 2 * piece + small :].reshape(-1).astype(F32)
-
-    marks = lax.all_gather(jnp.stack([segment_ids[0], positions[0]]), "ctx", axis=0)
-    marks = marks.reshape(count, 2, tensors, own_rows)
+    own_gains = jnp.concatenate([attn_gain, mlp_gain, q_gain, k_gain]).astype(F32)
+    own_marks = jnp.concatenate([segment_ids[0], positions[0]])
+    gains, marks = spread_small(to_tile(own_gains), to_tile(own_marks))
+    gains = gains.reshape(gains.shape[0], -1)
+    attn_scale = gains[:, :piece].reshape(-1)
+    mlp_scale = gains[:, piece : 2 * piece].reshape(-1)
+    query_scale = gains[:, 2 * piece : 2 * piece + small].reshape(-1)
+    key_scale = gains[:, 2 * piece + small : 2 * (piece + small)].reshape(-1)
+    marks = marks.reshape(count, -1)[:, : 2 * tok_count].reshape(count, 2, tensors, own_rows)
     behind = (rank - jnp.arange(count)) % count
     marks = marks[behind]
     starts = behind * tok_count
@@ -275,17 +392,9 @@
     middle_norm_grad, mlp_gain_grad = mlp_norm_pullback(mid_grad)
     middle_grad = grad_own.astype(F32) + middle_norm_grad
     branch_grad = middle_grad.astype(BF16)
-    out_weight_grad = dot32(branch_grad, attended_own, "mk,mtr->tkr").astype(BF16)
-    out_weight_grad = (
-        lax.psum_scatter(
-            out_weight_grad.reshape(tensors * width, head_rows),
-            ("tensor", "dp", "ctx"),
-            scatter_dimension=0,
-            tiled=True,
-        )
-        .astype(F32)
-        .T
-    )
+    branch_all = gather_behind(branch_grad).reshape(rows, width)
+    attended_low = attended_heads.reshape(rows, tensors, q_cols)
+    out_weight_grad = shards_of(dot32(branch_all, attended_low, "mk,mtr->tkr")).T
     attended_grad = dot32(branch_grad, out_weight, "mk,tkr->mtr").astype(BF16)
     attended_grad = attended_grad.reshape(own_rows, tensors, count, q_cols).transpose(2, 0, 1, 3)
     attended_grad = swap_to_behind(attended_grad).reshape(rows, kv_heads, group, HEAD_DIM)
@@ -328,9 +437,7 @@
         ],
         axis=1,
     )
-    gain_grads = lax.psum(gain_grads, ("dp", "ctx", "tensor"))
-    owner = lax.axis_index("dp") * count + rank
-    gain_grads = lax.dynamic_index_in_dim(gain_grads, owner, 0, keepdims=False)
+    gain_grads = owner_sums(jax.vmap(to_tile)(gain_grads)).reshape(-1)
     return (
         output,
         input_grad,
@@ -339,7 +446,7 @@
         key_weight_grad,
         value_weight_grad,
         gain_grads[2 * piece : 2 * piece + small],
-        gain_grads[2 * piece + small :],
+        gain_grads[2 * piece + small : 2 * (piece + small)],
         out_weight_grad,
         gain_grads[piece : 2 * piece],
         gate_weight_grad,
@@ -355,6 +462,7 @@
         and inputs.shape[0] == mesh.shape["dp"]
         and (inputs.shape[1] // count) % (16 * tensors) == 0
         and w_key.shape[1] % (tensors * count * HEAD_DIM) == 0
+        and inputs.shape[1] // count * 2 <= math.prod(TILE)
         and w_gate.shape[1] % (tensors * count * 128) == 0
     )
 

time: 1060 us -> 924 us (0.87)
  blocking collectives: 200 us -> 0 us
  Pallas kernels: 0 us -> 66.5 us
  starting transfers between devices: 77.8 us -> 132 us
  waiting for transfers between devices: 476 us -> 426 us
    reduce_scatter x1 -> x0, waiting for transfers between devices: 153 us -> none  [on_device_sliced(): lax.psum_scatter(out_weight_grad.reshape(tensors * width, head_rows), ('t...]
    all_gather x1 -> x0, blocking collectives: 78.2 us -> none  [on_device_sliced(): lax.all_gather(jnp.stack([segment_ids[0], positions[0]]), 'ctx', axis=0)]
    unnamed x1 -> x0, blocking collectives: 69.7 us -> none
    pallas_call x0 -> x2, Pallas kernels: none -> 66.5 us  [the longest x1 48.8 us: spread_small(): pl.pallas_call(kernel, out_shape=(jax.ShapeDtypeStruct((owners, *TILE), F...]
    reduce_scatter x4 -> x5, waiting for transfers between devices: 44.6 us -> 102 us  [shards_of(): lax.psum_scatter(flat, ('tensor', 'dp'), scatter_dimension=0, tiled=True)]
    ppermute x52 -> x58, starting transfers between devices: 77.2 us -> 131 us  [shift(): return lax.ppermute(value, axis, pairs)]
    psum x1 -> x0, blocking collectives: 52.2 us -> none  [on_device_sliced(): gain_grads = lax.psum(gain_grads, ('dp', 'ctx', 'tensor'))]
    ppermute x52 -> x58, waiting for transfers between devices: 278 us -> 312 us  [shift(): return lax.ppermute(value, axis, pairs)]
  transfers between devices with their start and end apart: 62 -> 68, of which waited for: 28 -> 35; matrix products, arithmetic and copies ran while one was open for 19% -> 24% of each run, Pallas kernels for 0% -> 7%
where the time goes in v2:
time: 924 us; the launch traced here: 913 us
  waiting for transfers between devices  426 us (46%)
  starting transfers between devices  132 us (14%)
  matrix products  118 us (13%)
  local copies, waits for them, and re-layouts  103 us (11%)
  Pallas kernels  66.5 us (7%)
  other arithmetic  50.6 us (5%)
  between operations  15.9 us (2%)
    ppermute x58, waiting for transfers between devices, shift(): return lax.ppermute(value, axis, pairs)  312 us
    ppermute x58, starting transfers between devices, shift(): return lax.ppermute(value, axis, pairs)  131 us
    dot_general x20, matrix products, dot32(): return jnp.einsum(spec, left, right, preferred_element_type=F32)  109 us
    reduce_scatter x5, waiting for transfers between devices, shards_of(): lax.psum_scatter(flat, ('tensor', 'dp'), scatter_dimension=0, tiled=True)  102 us
    pallas_call x1, Pallas kernels, spread_small(): pl.pallas_call(kernel, out_shape=(jax.ShapeDtypeStruct((owners, *TILE), F...  48.8 us
    convert_element_type x5, local copies, waits for them, and re-layouts, shards_of(): flat = partial.astype(BF16).reshape(-1, width)  36.1 us
    unnamed x154, local copies, waits for them, and re-layouts  23 us
  transfers between devices with their start and end apart: 68, of which 35 were waited for; matrix products, arithmetic and copies ran while one was open for 24% of the time, Pallas kernels for 7%

profile of v2, /device:TPU:0, one launch (start us, length us, event | category | flops | bytes accessed | tf_op | source)
XLA Modules:
  0.0 913.0 jit_solution(15023286865883382051)
XLA Ops:
  10.7 3.1 collective-permute-start.3
  20.3 4.8 collective-permute-done.4
  28.1 3.3 collective-permute-start.16
  38.9 7.9 collective-permute-done.17
  51.0 11.1 %collective-permute-done.20 = bf16[128,768]{0,1:T(8,128)(2,1)S(1)} collective-permute-done((bf16[128,768]{0,1:T(8,128)(2,1)S(1)}, bf16[128,768]{0,1:T(8,128)(2,1)S(1)}, u32[]{:S(2)}, u32[]{:S(2)}) %collective-permute-start.20) | collective-permute-done | bytes 196640 | tf_op jit(solution)/shard_map/ppermute | solution.py:75
  68.0 4.8 collective-permute-start.10
  75.3 4.9 collective-permute-done.10
  80.2 7.2 collective-permute-done.11
  91.2 3.7 collective-permute-start.27
  98.7 48.8 %spread_small.1 = (f32[16,8,128]{2,1,0:T(8,128)}, s32[4,8,128]{2,1,0:T(8,128)}) custom-call(f32[8,128]{1,0:T(8,128)} %fusion.107.gain_ref, s32[8,128]{1,0:T(8,128)} %pad_bitcast_fusion.mark_ref), custom_call_target="tpu_custom_call" | custom-call | tf_op jit(solution)/shard_map/spread_small/pallas_call | solution.py:168
  158.3 18.1 %collective-permute-done.2 = bf16[128,2048]{1,0:T(8,128)(2,1)S(1)} collective-permute-done((bf16[128,2048]{1,0:T(8,128)(2,1)S(1)}, bf16[128,2048]{1,0:T(8,128)(2,1)S(1)}, u32[]{:S(2)}, u32[]{:S(2)}) %collective-permute-start.2) | collective-permute-done | bytes 524320 | tf_op jit(solution)/shard_map/ppermute | solution.py:75
  178.7 48.4 %collective-permute-done.1 = bf16[128,2048]{1,0:T(8,128)(2,1)} collective-permute-done((bf16[128,2048]{1,0:T(8,128)(2,1)S(1)}, bf16[128,2048]{1,0:T(8,128)(2,1)}, u32[]{:S(2)}, u32[]{:S(2)}) %collective-permute-start.1) | collective-permute-done | bytes 524320 | tf_op jit(solution)/shard_map/ppermute | solution.py:75
  230.3 4.6 fusion.131
  241.3 14.5 %collective-permute-done.6 = bf16[2,512,2,128]{1,3,2,0:T(8,128)(2,1)} collective-permute-done((bf16[2,512,2,128]{1,3,2,0:T(8,128)(2,1)}, bf16[2,512,2,128]{1,3,2,0:T(8,128)(2,1)}, u32[]{:S(2)}, u32[]{:S(2)}) %collective-permute-start.6) | collective-permute-done | bytes 524320 | tf_op jit(solution)/shard_map/ppermute | solution.py:75
  257.0 9.4 %fusion.130 = (f32[2,2,512]{2,1,0:T(2,128)S(1)}, f32[2,2,512,1024]{2,3,1,0:T(8,128)}) fusion(pred[512,1024]{0,1:T(8,128)(4,1)} %compare_and_fusion, bf16[2,1024,2,128]{1,3,2,0:T(8,128)(2,1)S(1)} %pad_maximum_fusion.5, bf16[512,2,2,64]{3,0,2,1:T(8,128)(2,1)} %bitcast.483, bf16[512,2,2,64]{3,0,2,1:T(8,128)(2,1)} %bitcast.481), kind=kOutput, calls=%fused_computation.356 | convolution fusion | flops 548406272 | bytes 11018240 | tf_op jit(solution)/shard_map/sub | solution.py:360
  266.5 5.4 fusion.32
  272.9 14.0 %collective-permute-start.8 = (bf16[128,2,256]{0,2,1:T(8,128)(2,1)S(1)}, bf16[128,2,256]{0,2,1:T(8,128)(2,1)S(1)}, u32[]{:S(2)}, u32[]{:S(2)}) collective-permute-start(bf16[128,2,256]{0,2,1:T(8,128)(2,1)S(1)} %bitcast.546), channel_id=1, source_target_pairs={{0,4},{2,6},{4,0},{6,2},{1,5},{3,7},{5,1},{7,3},{8,12},{10,14},{12... | collective-permute-start | bytes 393224 | tf_op jit(solution)/shard_map/ppermute | solution.py:75
  288.1 8.5 collective-permute-start.9
  300.8 11.9 %copy.174 = bf16[4096,1024]{1,0:T(8,128)(2,1)} copy(bf16[4096,1024]{0,1:T(8,128)(2,1)} %all-gather.8.cloned.1.call-done) | data formatting | bytes 16777216 | tf_op jit(solution)/shard_map/all_gather | solution.py:299
  312.8 6.9 multiply_reduce_fusion.4
  328.9 23.4 %collective-permute-done.14 = bf16[128,2048]{1,0:T(8,128)(2,1)S(1)} collective-permute-done((bf16[128,2048]{1,0:T(8,128)(2,1)S(1)}, bf16[128,2048]{1,0:T(8,128)(2,1)S(1)}, u32[]{:S(2)}, u32[]{:S(2)}) %collective-permute-start.14) | collective-permute-done | bytes 524320 | tf_op jit(solution)/shard_map/ppermute | solution.py:75
  356.4 8.6 fusion.133
  365.0 8.6 fusion.132
  373.5 10.8 %all-gather.14.cloned.1.call-done = bf16[4096,768]{1,0:T(8,128)(2,1)} async-done(((bf16[512,768]{1,0:T(8,128)(2,1)}), bf16[4096,768]{1,0:T(8,128)(2,1)}) %all-gather.14.cloned.1.call-update) | async-done | bytes 6291472 | tf_op jit(solution)/shard_map/all_gather | solution.py:238
  384.4 10.5 %fusion.14 = (bf16[2,512,768]{1,2,0:T(8,128)(2,1)S(1)}, bf16[2,512,768]{1,2,0:T(8,128)(2,1)S(1)}, bf16[2,512,768]{1,2,0:T(8,128)(2,1)S(1)}) fusion(f32[2,768,512]{2,1,0:T(8,128)} %fusion.132, f32[2,768,512]{2,1,0:T(8,128)} %fusion.133, bf16[2,2048,768]{2,1,0:T(8,128)(2,1)} %bitcast.567, bf16[512,2048,1]{1,0,2:T(8,128)(2,1)} %bitcast.491), kind=kOutput, calls=%fused_computation.29 | convolution fusion | flops 3233808384 | bytes 19398656 | tf_op jit(solution)/shard_map/mk,tkc->tmc/dot_general | solution.py:69
  394.9 3.5 fusion.134
  398.4 6.8 fusion.7
  405.4 3.4 collective-permute-start.29
  409.9 3.7 bitcast_convert_fusion.1
  417.2 3.9 collective-permute-done.29
  422.6 10.8 %collective-permute-done.31 = bf16[128,2048]{1,0:T(8,128)(2,1)S(1)} collective-permute-done((bf16[128,2048]{1,0:T(8,128)(2,1)S(1)}, bf16[128,2048]{1,0:T(8,128)(2,1)S(1)}, u32[]{:S(2)}, u32[]{:S(2)}) %collective-permute-start.31) | collective-permute-done | bytes 524320 | tf_op jit(solution)/shard_map/ppermute | solution.py:75
  433.4 21.9 %collective-permute-done.30 = bf16[128,2048]{1,0:T(8,128)(2,1)S(1)} collective-permute-done((bf16[128,2048]{1,0:T(8,128)(2,1)S(1)}, bf16[128,2048]{1,0:T(8,128)(2,1)S(1)}, u32[]{:S(2)}, u32[]{:S(2)}) %collective-permute-start.30) | collective-permute-done | bytes 524320 | tf_op jit(solution)/shard_map/ppermute | solution.py:75
  456.4 10.7 %collective-permute-done.24 = bf16[128,2048]{1,0:T(8,128)(2,1)S(1)} collective-permute-done((bf16[128,2048]{1,0:T(8,128)(2,1)S(1)}, bf16[128,2048]{1,0:T(8,128)(2,1)S(1)}, u32[]{:S(2)}, u32[]{:S(2)}) %collective-permute-start.24) | collective-permute-done | bytes 524320 | tf_op jit(solution)/shard_map/ppermute | solution.py:75
  467.1 31.9 %collective-permute-done.23 = bf16[128,2048]{1,0:T(8,128)(2,1)S(1)} collective-permute-done((bf16[128,2048]{1,0:T(8,128)(2,1)S(1)}, bf16[128,2048]{1,0:T(8,128)(2,1)S(1)}, u32[]{:S(2)}, u32[]{:S(2)}) %collective-permute-start.23) | collective-permute-done | bytes 524320 | tf_op jit(solution)/shard_map/ppermute | solution.py:75
  503.8 3.2 collective-permute-start.32
  510.6 4.3 collective-permute-done.33
  514.9 19.5 %collective-permute-start.43 = (bf16[128,2048]{1,0:T(8,128)(2,1)}, bf16[128,2048]{1,0:T(8,128)(2,1)}, u32[]{:S(2)}, u32[]{:S(2)}) collective-permute-start(bf16[128,2048]{1,0:T(8,128)(2,1)} %get-tuple-element.51), channel_id=1, source_target_pairs={{0,2},{2,4},{4,6},{6,0},{1,3},{3,5},{5,7},{7,1},{8,10},{10,12},{12... | collective-permute-start | bytes 1572872 | tf_op jit(solution)/shard_map/ppermute | solution.py:75
  535.1 6.0 fusion.25
  541.1 4.8 fusion.1
  551.6 11.1 %collective-permute-done.44 = bf16[128,2048]{1,0:T(8,128)(2,1)} collective-permute-done((bf16[128,2048]{1,0:T(8,128)(2,1)}, bf16[128,2048]{1,0:T(8,128)(2,1)}, u32[]{:S(2)}, u32[]{:S(2)}) %collective-permute-start.44) | collective-permute-done | bytes 524320 | tf_op jit(solution)/shard_map/ppermute | solution.py:75
  567.1 3.9 copy.207
  578.6 9.1 collective-permute-done.35
  594.4 6.3 convert_bitcast_fusion.3
  600.7 6.3 copy.203
  608.6 6.8 convert_bitcast_fusion
  615.4 8.7 copy.213
  625.9 6.8 convert_bitcast_fusion.1
  632.6 8.5 copy.211
  641.2 6.8 convert_bitcast_fusion.2
  647.9 8.7 copy.209
  659.0 4.9 bitcast_convert_fusion
  667.3 9.2 %collective-permute-done.25 = bf16[128,2048]{1,0:T(8,128)(2,1)S(1)} collective-permute-done((bf16[128,2048]{1,0:T(8,128)(2,1)S(1)}, bf16[128,2048]{1,0:T(8,128)(2,1)S(1)}, u32[]{:S(2)}, u32[]{:S(2)}) %collective-permute-start.25) | collective-permute-done | bytes 524320 | tf_op jit(solution)/shard_map/ppermute | solution.py:75
  677.8 13.5 %collective-permute-done.36 = bf16[128,2048]{1,0:T(8,128)(2,1)S(1)} collective-permute-done((bf16[128,2048]{1,0:T(8,128)(2,1)}, bf16[128,2048]{1,0:T(8,128)(2,1)S(1)}, u32[]{:S(2)}, u32[]{:S(2)}) %collective-permute-start.36) | collective-permute-done | bytes 524320 | tf_op jit(solution)/shard_map/ppermute | solution.py:75
  691.3 19.1 %collective-permute-done.37 = bf16[128,2048]{1,0:T(8,128)(2,1)} collective-permute-done((bf16[128,2048]{1,0:T(8,128)(2,1)}, bf16[128,2048]{1,0:T(8,128)(2,1)}, u32[]{:S(2)}, u32[]{:S(2)}) %collective-permute-start.37) | collective-permute-done | bytes 524320 | tf_op jit(solution)/shard_map/ppermute | solution.py:75
  715.7 17.7 %owner_sums.1 = f32[8,128]{1,0:T(8,128)} custom-call(f32[16,8,128]{2,1,0:T(8,128)} %bitcast.520), custom_call_target="tpu_custom_call" | custom-call | tf_op jit(solution)/shard_map/owner_sums/pallas_call | solution.py:218
  750.1 3.1 collective-permute-done.40
  753.2 4.0 collective-permute-done.41
  762.5 3.0 collective-permute-start.55
  767.9 43.5 %reduce-scatter.12.cloned.1.call-done = bf16[512,768]{1,0:T(8,128)(2,1)} async-done(((bf16[4096,768]{1,0:T(8,128)(2,1)}), bf16[512,768]{1,0:T(8,128)(2,1)}) %reduce-scatter.12.cloned.1.call-update) | async-done | bytes 786448 | tf_op jit(solution)/shard_map/reduce_scatter | solution.py:247
  817.6 58.9 %reduce-scatter.10.cloned.1.call-done = bf16[512,768]{1,0:T(8,128)(2,1)} async-done(((bf16[4096,768]{1,0:T(8,128)(2,1)}), bf16[512,768]{1,0:T(8,128)(2,1)}) %reduce-scatter.10.cloned.1.call-update) | async-done | bytes 786448 | tf_op jit(solution)/shard_map/reduce_scatter | solution.py:247
  878.7 3.4 collective-permute-start.54
  892.4 3.0 copy.219
  895.4 4.2 collective-permute-done.50
  903.0 3.0 copy.218
  (419 shorter events, 186.0 us)
Async XLA Ops:
  7.2 221.8 %all-gather.6.cloned.1.call-start = ((), (), s32[]{:S(2)}) async-start(), calls=%async_computation.5 | async-start | bytes 4718592 | tf_op jit(solution)/shard_map/all_gather | solution.py:238
  10.7 9.6 %collective-permute-start.3 = (bf16[128,512]{0,1:T(8,128)(2,1)S(1)}, bf16[128,512]{0,1:T(8,128)(2,1)S(1)}, u32[]{:S(2)}, u32[]{:S(2)}) collective-permute-start(bf16[128,512]{0,1:T(8,128)(2,1)S(1)} %get-tuple-element.116), channel_id=1, source_target_pairs={{0,2},{2,4},{4,6},{6,0},{1,3},{3,5},{5,7},{7,1},{8,10},{10,12},{12... | collective-permute-start | bytes 393224 | tf_op jit(solution)/shard_map/ppermute | solution.py:75
  13.8 11.2 %collective-permute-start.4 = (bf16[128,512]{0,1:T(8,128)(2,1)S(1)}, bf16[128,512]{0,1:T(8,128)(2,1)S(1)}, u32[]{:S(2)}, u32[]{:S(2)}) collective-permute-start(bf16[128,512]{0,1:T(8,128)(2,1)S(1)} %get-tuple-element.117), channel_id=1, source_target_pairs={{0,4},{2,6},{4,0},{6,2},{1,5},{3,7},{5,1},{7,3},{8,12},{10,14},{12... | collective-permute-start | bytes 393224 | tf_op jit(solution)/shard_map/ppermute | solution.py:75
  26.5 274.3 %all-gather.8.cloned.1.call-start = ((), (), s32[]{:S(2)}) async-start(), calls=%async_computation.6 | async-start | bytes 8650752 | tf_op jit(solution)/shard_map/all_gather | solution.py:299
  27.3 329.1 %all-gather.12.cloned.1.call-start = ((), (), s32[]{:S(2)}) async-start(), calls=%async_computation.8 | async-start | bytes 7077888 | tf_op jit(solution)/shard_map/all_gather | solution.py:238
  28.1 10.2 %collective-permute-start.16 = (bf16[128,768]{0,1:T(8,128)(2,1)S(1)}, bf16[128,768]{0,1:T(8,128)(2,1)S(1)}, u32[]{:S(2)}, u32[]{:S(2)}) collective-permute-start(bf16[128,768]{0,1:T(8,128)(2,1)S(1)} %get-tuple-element.98), channel_id=1, source_target_pairs={{0,2},{2,4},{4,6},{6,0},{1,3},{3,5},{5,7},{7,1},{8,10},{10,12},{12... | collective-permute-start | bytes 589832 | tf_op jit(solution)/shard_map/ppermute | solution.py:75
  31.4 15.4 %collective-permute-start.17 = (bf16[128,768]{0,1:T(8,128)(2,1)S(1)}, bf16[128,768]{0,1:T(8,128)(2,1)S(1)}, u32[]{:S(2)}, u32[]{:S(2)}) collective-permute-start(bf16[128,768]{0,1:T(8,128)(2,1)S(1)} %get-tuple-element.99), channel_id=1, source_target_pairs={{0,4},{2,6},{4,0},{6,2},{1,5},{3,7},{5,1},{7,3},{8,12},{10,14},{12... | collective-permute-start | bytes 589832 | tf_op jit(solution)/shard_map/ppermute | solution.py:75
  33.0 15.9 %collective-permute-start.18 = (bf16[128,768]{0,1:T(8,128)(2,1)S(1)}, bf16[128,768]{0,1:T(8,128)(2,1)S(1)}, u32[]{:S(2)}, u32[]{:S(2)}) collective-permute-start(bf16[128,768]{0,1:T(8,128)(2,1)S(1)} %get-tuple-element.101), channel_id=1, source_target_pairs={{0,6},{2,0},{4,2},{6,4},{1,7},{3,1},{5,3},{7,5},{8,14},{10,8},{12,... | collective-permute-start | bytes 589832 | tf_op jit(solution)/shard_map/ppermute | solution.py:75
  34.2 16.8 %collective-permute-start.19 = (bf16[128,768]{0,1:T(8,128)(2,1)S(1)}, bf16[128,768]{0,1:T(8,128)(2,1)S(1)}, u32[]{:S(2)}, u32[]{:S(2)}) collective-permute-start(bf16[128,768]{0,1:T(8,128)(2,1)S(1)} %get-tuple-element.90), channel_id=1, source_target_pairs={{0,2},{2,4},{4,6},{6,0},{1,3},{3,5},{5,7},{7,1},{8,10},{10,12},{12... | collective-permute-start | bytes 589832 | tf_op jit(solution)/shard_map/ppermute | solution.py:75
  35.5 26.6 %collective-permute-start.20 = (bf16[128,768]{0,1:T(8,128)(2,1)S(1)}, bf16[128,768]{0,1:T(8,128)(2,1)S(1)}, u32[]{:S(2)}, u32[]{:S(2)}) collective-permute-start(bf16[128,768]{0,1:T(8,128)(2,1)S(1)} %get-tuple-element.91), channel_id=1, source_target_pairs={{0,4},{2,6},{4,0},{6,2},{1,5},{3,7},{5,1},{7,3},{8,12},{10,14},{12... | collective-permute-start | bytes 589832 | tf_op jit(solution)/shard_map/ppermute | solution.py:75
  38.3 23.8 %collective-permute-start.21 = (bf16[128,768]{0,1:T(8,128)(2,1)S(1)}, bf16[128,768]{0,1:T(8,128)(2,1)}, u32[]{:S(2)}, u32[]{:S(2)}) collective-permute-start(bf16[128,768]{0,1:T(8,128)(2,1)S(1)} %get-tuple-element.93), channel_id=1, source_target_pairs={{0,6},{2,0},{4,2},{6,4},{1,7},{3,1},{5,3},{7,5},{8,14},{10,8},{12,... | collective-permute-start | bytes 589832 | tf_op jit(solution)/shard_map/ppermute | solution.py:75
  67.2 297.7 %all-gather.10.cloned.1.call-start = ((), (), s32[]{:S(2)}) async-start(), calls=%async_computation.7 | async-start | bytes 7077888 | tf_op jit(solution)/shard_map/all_gather | solution.py:238
  68.0 12.1 %collective-permute-start.10 = (bf16[128,768]{0,1:T(8,128)(2,1)S(1)}, bf16[128,768]{0,1:T(8,128)(2,1)S(1)}, u32[]{:S(2)}, u32[]{:S(2)}) collective-permute-start(bf16[128,768]{0,1:T(8,128)(2,1)S(1)} %get-tuple-element.94), channel_id=1, source_target_pairs={{0,2},{2,4},{4,6},{6,0},{1,3},{3,5},{5,7},{7,1},{8,10},{10,12},{12... | collective-permute-start | bytes 589832 | tf_op jit(solution)/shard_map/ppermute | solution.py:75
  72.9 14.5 %collective-permute-start.11 = (bf16[128,768]{0,1:T(8,128)(2,1)S(1)}, bf16[128,768]{0,1:T(8,128)(2,1)S(1)}, u32[]{:S(2)}, u32[]{:S(2)}) collective-permute-start(bf16[128,768]{0,1:T(8,128)(2,1)S(1)} %get-tuple-element.95), channel_id=1, source_target_pairs={{0,4},{2,6},{4,0},{6,2},{1,5},{3,7},{5,1},{7,3},{8,12},{10,14},{12... | collective-permute-start | bytes 589832 | tf_op jit(solution)/shard_map/ppermute | solution.py:75
  74.9 12.5 %collective-permute-start.12 = (bf16[128,768]{0,1:T(8,128)(2,1)S(1)}, bf16[128,768]{0,1:T(8,128)(2,1)S(1)}, u32[]{:S(2)}, u32[]{:S(2)}) collective-permute-start(bf16[128,768]{0,1:T(8,128)(2,1)S(1)} %get-tuple-element.97), channel_id=1, source_target_pairs={{0,6},{2,0},{4,2},{6,4},{1,7},{3,1},{5,3},{7,5},{8,14},{10,8},{12,... | collective-permute-start | bytes 589832 | tf_op jit(solution)/shard_map/ppermute | solution.py:75
  89.3 295.1 %all-gather.14.cloned.1.call-start = ((), (), s32[]{:S(2)}) async-start(), calls=%async_computation.9 | async-start | bytes 7077888 | tf_op jit(solution)/shard_map/all_gather | solution.py:238
  91.2 231.8 %collective-permute-start.27 = (bf16[128,2048]{1,0:T(8,128)(2,1)}, bf16[128,2048]{1,0:T(8,128)(2,1)}, u32[]{:S(2)}, u32[]{:S(2)}) collective-permute-start(bf16[128,2048]{1,0:T(8,128)(2,1)} %fusion.166), channel_id=1, source_target_pairs={{0,4},{2,6},{4,0},{6,2},{1,5},{3,7},{5,1},{7,3},{8,12},{10,14},{12... | collective-permute-start | bytes 1572872 | tf_op jit(solution)/shard_map/ppermute | solution.py:75
  94.9 230.9 %collective-permute-start.26 = (bf16[128,2048]{1,0:T(8,128)(2,1)}, bf16[128,2048]{1,0:T(8,128)(2,1)}, u32[]{:S(2)}, u32[]{:S(2)}) collective-permute-start(bf16[128,2048]{1,0:T(8,128)(2,1)} %fusion.166), channel_id=1, source_target_pairs={{0,2},{2,4},{4,6},{6,0},{1,3},{3,5},{5,7},{7,1},{8,10},{10,12},{12... | collective-permute-start | bytes 1572872 | tf_op jit(solution)/shard_map/ppermute | solution.py:75
  148.8 27.7 %collective-permute-start.2 = (bf16[128,2048]{1,0:T(8,128)(2,1)S(1)}, bf16[128,2048]{1,0:T(8,128)(2,1)S(1)}, u32[]{:S(2)}, u32[]{:S(2)}) collective-permute-start(bf16[128,2048]{1,0:T(8,128)(2,1)S(1)} %fusion.37), channel_id=1, source_target_pairs={{0,6},{2,0},{4,2},{6,4},{1,7},{3,1},{5,3},{7,5},{8,14},{10,8},{12,... | collective-permute-start | bytes 1572872 | tf_op jit(solution)/shard_map/ppermute | solution.py:75
  150.7 76.4 %collective-permute-start.1 = (bf16[128,2048]{1,0:T(8,128)(2,1)S(1)}, bf16[128,2048]{1,0:T(8,128)(2,1)}, u32[]{:S(2)}, u32[]{:S(2)}) collective-permute-start(bf16[128,2048]{1,0:T(8,128)(2,1)S(1)} %fusion.37), channel_id=1, source_target_pairs={{0,4},{2,6},{4,0},{6,2},{1,5},{3,7},{5,1},{7,3},{8,12},{10,14},{12... | collective-permute-start | bytes 1572872 | tf_op jit(solution)/shard_map/ppermute | solution.py:75
  151.0 76.1 %collective-permute-start = (bf16[128,2048]{1,0:T(8,128)(2,1)S(1)}, bf16[128,2048]{1,0:T(8,128)(2,1)}, u32[]{:S(2)}, u32[]{:S(2)}) collective-permute-start(bf16[128,2048]{1,0:T(8,128)(2,1)S(1)} %fusion.37), channel_id=1, source_target_pairs={{0,2},{2,4},{4,6},{6,0},{1,3},{3,5},{5,7},{7,1},{8,10},{10,12},{12... | collective-permute-start | bytes 1572872 | tf_op jit(solution)/shard_map/ppermute | solution.py:75
  158.3 578.9 %reduce-scatter.8.cloned.1.call-start = ((), (), s32[]{:S(2)}) async-start(), calls=%async_computation.11 | async-start | bytes 2359296 | tf_op jit(solution)/shard_map/reduce_scatter | solution.py:247
  176.5 149.3 %collective-permute-start.28 = (bf16[128,2048]{1,0:T(8,128)(2,1)}, bf16[128,2048]{1,0:T(8,128)(2,1)}, u32[]{:S(2)}, u32[]{:S(2)}) collective-permute-start(bf16[128,2048]{1,0:T(8,128)(2,1)} %fusion.166), channel_id=1, source_target_pairs={{0,6},{2,0},{4,2},{6,4},{1,7},{3,1},{5,3},{7,5},{8,14},{10,8},{12,... | collective-permute-start | bytes 1572872 | tf_op jit(solution)/shard_map/ppermute | solution.py:75
  237.2 18.6 %collective-permute-start.6 = (bf16[2,512,2,128]{1,3,2,0:T(8,128)(2,1)}, bf16[2,512,2,128]{1,3,2,0:T(8,128)(2,1)}, u32[]{:S(2)}, u32[]{:S(2)}) collective-permute-start(bf16[2,512,2,128]{1,3,2,0:T(8,128)(2,1)} %pad_maximum_fusion.13), channel_id=1, source_target_pairs={{0,1},{1,0},{2,3},{3,2},{4,5},{5,4},{6,7},{7,6},{8,9},{9,8},{10,11... | collective-permute-start | bytes 1572872 | tf_op jit(solution)/shard_map/ppermute | solution.py:75
  272.0 16.1 %collective-permute-start.7 = (bf16[128,2,256]{0,2,1:T(8,128)(2,1)S(1)}, bf16[128,2,256]{0,2,1:T(8,128)(2,1)S(1)}, u32[]{:S(2)}, u32[]{:S(2)}) collective-permute-start(bf16[128,2,256]{0,2,1:T(8,128)(2,1)S(1)} %bitcast.547), channel_id=1, source_target_pairs={{0,6},{2,0},{4,2},{6,4},{1,7},{3,1},{5,3},{7,5},{8,14},{10,8},{12,... | collective-permute-start | bytes 393224 | tf_op jit(solution)/shard_map/ppermute | solution.py:75
  272.9 24.6 %collective-permute-start.8 = (bf16[128,2,256]{0,2,1:T(8,128)(2,1)S(1)}, bf16[128,2,256]{0,2,1:T(8,128)(2,1)S(1)}, u32[]{:S(2)}, u32[]{:S(2)}) collective-permute-start(bf16[128,2,256]{0,2,1:T(8,128)(2,1)S(1)} %bitcast.546), channel_id=1, source_target_pairs={{0,4},{2,6},{4,0},{6,2},{1,5},{3,7},{5,1},{7,3},{8,12},{10,14},{12... | collective-permute-start | bytes 393224 | tf_op jit(solution)/shard_map/ppermute | solution.py:75
  288.1 11.1 %collective-permute-start.9 = (bf16[128,2,256]{0,2,1:T(8,128)(2,1)S(1)}, bf16[128,2,256]{0,2,1:T(8,128)(2,1)S(1)}, u32[]{:S(2)}, u32[]{:S(2)}) collective-permute-start(bf16[128,2,256]{0,2,1:T(8,128)(2,1)S(1)} %bitcast.545), channel_id=1, source_target_pairs={{0,2},{2,4},{4,6},{6,0},{1,3},{3,5},{5,7},{7,1},{8,10},{10,12},{12... | collective-permute-start | bytes 393224 | tf_op jit(solution)/shard_map/ppermute | solution.py:75
  319.8 32.5 %collective-permute-start.14 = (bf16[128,2048]{1,0:T(8,128)(2,1)S(1)}, bf16[128,2048]{1,0:T(8,128)(2,1)S(1)}, u32[]{:S(2)}, u32[]{:S(2)}) collective-permute-start(bf16[128,2048]{1,0:T(8,128)(2,1)S(1)} %multiply_convert_fusion), channel_id=1, source_target_pairs={{0,4},{2,6},{4,0},{6,2},{1,5},{3,7},{5,1},{7,3},{8,12},{10,14},{12... | collective-permute-start | bytes 1572872 | tf_op jit(solution)/shard_map/ppermute | solution.py:75
  321.5 30.8 %collective-permute-start.13 = (bf16[128,2048]{1,0:T(8,128)(2,1)S(1)}, bf16[128,2048]{1,0:T(8,128)(2,1)S(1)}, u32[]{:S(2)}, u32[]{:S(2)}) collective-permute-start(bf16[128,2048]{1,0:T(8,128)(2,1)S(1)} %multiply_convert_fusion), channel_id=1, source_target_pairs={{0,2},{2,4},{4,6},{6,0},{1,3},{3,5},{5,7},{7,1},{8,10},{10,12},{12... | collective-permute-start | bytes 1572872 | tf_op jit(solution)/shard_map/ppermute | solution.py:75
  323.0 31.8 %collective-permute-start.15 = (bf16[128,2048]{1,0:T(8,128)(2,1)S(1)}, bf16[128,2048]{1,0:T(8,128)(2,1)S(1)}, u32[]{:S(2)}, u32[]{:S(2)}) collective-permute-start(bf16[128,2048]{1,0:T(8,128)(2,1)S(1)} %multiply_convert_fusion), channel_id=1, source_target_pairs={{0,6},{2,0},{4,2},{6,4},{1,7},{3,1},{5,3},{7,5},{8,14},{10,8},{12,... | collective-permute-start | bytes 1572872 | tf_op jit(solution)/shard_map/ppermute | solution.py:75
  405.4 15.7 %collective-permute-start.29 = (bf16[128,2048]{1,0:T(8,128)(2,1)S(1)}, bf16[128,2048]{1,0:T(8,128)(2,1)S(1)}, u32[]{:S(2)}, u32[]{:S(2)}) collective-permute-start(bf16[128,2048]{1,0:T(8,128)(2,1)S(1)} %get-tuple-element.59), channel_id=1, source_target_pairs={{0,6},{2,0},{4,2},{6,4},{1,7},{3,1},{5,3},{7,5},{8,14},{10,8},{12,... | collective-permute-start | bytes 1572872 | tf_op jit(solution)/shard_map/ppermute | solution.py:75
  408.7 24.6 %collective-permute-start.31 = (bf16[128,2048]{1,0:T(8,128)(2,1)S(1)}, bf16[128,2048]{1,0:T(8,128)(2,1)S(1)}, u32[]{:S(2)}, u32[]{:S(2)}) collective-permute-start(bf16[128,2048]{1,0:T(8,128)(2,1)S(1)} %get-tuple-element.60), channel_id=1, source_target_pairs={{0,2},{2,4},{4,6},{6,0},{1,3},{3,5},{5,7},{7,1},{8,10},{10,12},{12... | collective-permute-start | bytes 1572872 | tf_op jit(solution)/shard_map/ppermute | solution.py:75
  408.7 46.6 %collective-permute-start.30 = (bf16[128,2048]{1,0:T(8,128)(2,1)S(1)}, bf16[128,2048]{1,0:T(8,128)(2,1)S(1)}, u32[]{:S(2)}, u32[]{:S(2)}) collective-permute-start(bf16[128,2048]{1,0:T(8,128)(2,1)S(1)} %get-tuple-element.61), channel_id=1, source_target_pairs={{0,4},{2,6},{4,0},{6,2},{1,5},{3,7},{5,1},{7,3},{8,12},{10,14},{12... | collective-permute-start | bytes 1572872 | tf_op jit(solution)/shard_map/ppermute | solution.py:75
  413.8 42.7 %collective-permute-start.22 = (bf16[128,2048]{1,0:T(8,128)(2,1)S(1)}, bf16[128,2048]{1,0:T(8,128)(2,1)S(1)}, u32[]{:S(2)}, u32[]{:S(2)}) collective-permute-start(bf16[128,2048]{1,0:T(8,128)(2,1)S(1)} %get-tuple-element.62), channel_id=1, source_target_pairs={{0,6},{2,0},{4,2},{6,4},{1,7},{3,1},{5,3},{7,5},{8,14},{10,8},{12,... | collective-permute-start | bytes 1572872 | tf_op jit(solution)/shard_map/ppermute | solution.py:75
  416.6 50.6 %collective-permute-start.24 = (bf16[128,2048]{1,0:T(8,128)(2,1)S(1)}, bf16[128,2048]{1,0:T(8,128)(2,1)S(1)}, u32[]{:S(2)}, u32[]{:S(2)}) collective-permute-start(bf16[128,2048]{1,0:T(8,128)(2,1)S(1)} %get-tuple-element.63), channel_id=1, source_target_pairs={{0,2},{2,4},{4,6},{6,0},{1,3},{3,5},{5,7},{7,1},{8,10},{10,12},{12... | collective-permute-start | bytes 1572872 | tf_op jit(solution)/shard_map/ppermute | solution.py:75
  421.1 78.0 %collective-permute-start.23 = (bf16[128,2048]{1,0:T(8,128)(2,1)S(1)}, bf16[128,2048]{1,0:T(8,128)(2,1)S(1)}, u32[]{:S(2)}, u32[]{:S(2)}) collective-permute-start(bf16[128,2048]{1,0:T(8,128)(2,1)S(1)} %get-tuple-element.64), channel_id=1, source_target_pairs={{0,4},{2,6},{4,0},{6,2},{1,5},{3,7},{5,1},{7,3},{8,12},{10,14},{12... | collective-permute-start | bytes 1572872 | tf_op jit(solution)/shard_map/ppermute | solution.py:75
  503.7 11.2 %collective-permute-start.33 = (bf16[128,2,256]{2,0,1:T(8,128)(2,1)S(1)}, bf16[128,2,256]{2,0,1:T(8,128)(2,1)S(1)}, u32[]{:S(2)}, u32[]{:S(2)}) collective-permute-start(bf16[128,2,256]{2,0,1:T(8,128)(2,1)S(1)} %get-tuple-element.109), channel_id=1, source_target_pairs={{0,4},{2,6},{4,0},{6,2},{1,5},{3,7},{5,1},{7,3},{8,12},{10,14},{12... | collective-permute-start | bytes 393224 | tf_op jit(solution)/shard_map/ppermute | solution.py:75
  503.8 30.7 %collective-permute-start.32 = (bf16[128,2,256]{2,0,1:T(8,128)(2,1)S(1)}, bf16[128,2,256]{2,0,1:T(8,128)(2,1)S(1)}, u32[]{:S(2)}, u32[]{:S(2)}) collective-permute-start(bf16[128,2,256]{2,0,1:T(8,128)(2,1)S(1)} %get-tuple-element.110), channel_id=1, source_target_pairs={{0,2},{2,4},{4,6},{6,0},{1,3},{3,5},{5,7},{7,1},{8,10},{10,12},{12... | collective-permute-start | bytes 393224 | tf_op jit(solution)/shard_map/ppermute | solution.py:75
  507.0 27.5 %collective-permute-start.34 = (bf16[128,2,256]{2,0,1:T(8,128)(2,1)S(1)}, bf16[128,2,256]{2,0,1:T(8,128)(2,1)S(1)}, u32[]{:S(2)}, u32[]{:S(2)}) collective-permute-start(bf16[128,2,256]{2,0,1:T(8,128)(2,1)S(1)} %get-tuple-element.111), channel_id=1, source_target_pairs={{0,6},{2,0},{4,2},{6,4},{1,7},{3,1},{5,3},{7,5},{8,14},{10,8},{12,... | collective-permute-start | bytes 393224 | tf_op jit(solution)/shard_map/ppermute | solution.py:75
  507.6 44.0 %collective-permute-start.45 = (bf16[128,2048]{1,0:T(8,128)(2,1)}, bf16[128,2048]{1,0:T(8,128)(2,1)}, u32[]{:S(2)}, u32[]{:S(2)}) collective-permute-start(bf16[128,2048]{1,0:T(8,128)(2,1)} %get-tuple-element.51), channel_id=1, source_target_pairs={{0,6},{2,0},{4,2},{6,4},{1,7},{3,1},{5,3},{7,5},{8,14},{10,8},{12,... | collective-permute-start | bytes 1572872 | tf_op jit(solution)/shard_map/ppermute | solution.py:75
  508.7 54.0 %collective-permute-start.44 = (bf16[128,2048]{1,0:T(8,128)(2,1)}, bf16[128,2048]{1,0:T(8,128)(2,1)}, u32[]{:S(2)}, u32[]{:S(2)}) collective-permute-start(bf16[128,2048]{1,0:T(8,128)(2,1)} %get-tuple-element.51), channel_id=1, source_target_pairs={{0,4},{2,6},{4,0},{6,2},{1,5},{3,7},{5,1},{7,3},{8,12},{10,14},{12... | collective-permute-start | bytes 1572872 | tf_op jit(solution)/shard_map/ppermute | solution.py:75
  514.9 47.8 %collective-permute-start.43 = (bf16[128,2048]{1,0:T(8,128)(2,1)}, bf16[128,2048]{1,0:T(8,128)(2,1)}, u32[]{:S(2)}, u32[]{:S(2)}) collective-permute-start(bf16[128,2048]{1,0:T(8,128)(2,1)} %get-tuple-element.51), channel_id=1, source_target_pairs={{0,2},{2,4},{4,6},{6,0},{1,3},{3,5},{5,7},{7,1},{8,10},{10,12},{12... | collective-permute-start | bytes 1572872 | tf_op jit(solution)/shard_map/ppermute | solution.py:75
  571.1 172.5 %reduce-scatter.6.cloned.1.call-start = ((), (), s32[]{:S(2)}) async-start(), calls=%async_computation.10 | async-start | bytes 4718592 | tf_op jit(solution)/shard_map/reduce_scatter | solution.py:247
  573.6 14.2 %collective-permute-start.35 = (bf16[2,512,2,128]{1,3,2,0:T(8,128)(2,1)}, bf16[2,512,2,128]{1,3,2,0:T(8,128)(2,1)}, u32[]{:S(2)}, u32[]{:S(2)}) collective-permute-start(bf16[2,512,2,128]{1,3,2,0:T(8,128)(2,1)} %fusion.49), channel_id=1, source_target_pairs={{0,1},{1,0},{2,3},{3,2},{4,5},{5,4},{6,7},{7,6},{8,9},{9,8},{10,11... | collective-permute-start | bytes 1572872 | tf_op jit(solution)/shard_map/ppermute | solution.py:75
  607.0 153.9 %reduce-scatter.14.cloned.1.call-start = ((), (), s32[]{:S(2)}) async-start(), calls=%async_computation.14 | async-start | bytes 7077888 | tf_op jit(solution)/shard_map/reduce_scatter | solution.py:247
  624.1 187.3 %reduce-scatter.12.cloned.1.call-start = ((), (), s32[]{:S(2)}) async-start(), calls=%async_computation.13 | async-start | bytes 7077888 | tf_op jit(solution)/shard_map/reduce_scatter | solution.py:247
  641.1 235.3 %reduce-scatter.10.cloned.1.call-start = ((), (), s32[]{:S(2)}) async-start(), calls=%async_computation.12 | async-start | bytes 7077888 | tf_op jit(solution)/shard_map/reduce_scatter | solution.py:247
  657.7 18.9 %collective-permute-start.25 = (bf16[128,2048]{1,0:T(8,128)(2,1)S(1)}, bf16[128,2048]{1,0:T(8,128)(2,1)S(1)}, u32[]{:S(2)}, u32[]{:S(2)}) collective-permute-start(bf16[128,2048]{1,0:T(8,128)(2,1)S(1)} %copy-done.12), channel_id=1, source_target_pairs={{0,1},{1,0},{2,3},{3,2},{4,5},{5,4},{6,7},{7,6},{8,9},{9,8},{10,11... | collective-permute-start | bytes 1572872 | tf_op jit(solution)/shard_map/ppermute | solution.py:75
  665.1 26.2 %collective-permute-start.36 = (bf16[128,2048]{1,0:T(8,128)(2,1)}, bf16[128,2048]{1,0:T(8,128)(2,1)S(1)}, u32[]{:S(2)}, u32[]{:S(2)}) collective-permute-start(bf16[128,2048]{1,0:T(8,128)(2,1)} %get-tuple-element.56), channel_id=1, source_target_pairs={{0,6},{2,0},{4,2},{6,4},{1,7},{3,1},{5,3},{7,5},{8,14},{10,8},{12,... | collective-permute-start | bytes 1572872 | tf_op jit(solution)/shard_map/ppermute | solution.py:75
  665.2 26.2 %collective-permute-start.38 = (bf16[128,2048]{1,0:T(8,128)(2,1)}, bf16[128,2048]{1,0:T(8,128)(2,1)S(1)}, u32[]{:S(2)}, u32[]{:S(2)}) collective-permute-start(bf16[128,2048]{1,0:T(8,128)(2,1)} %get-tuple-element.57), channel_id=1, source_target_pairs={{0,2},{2,4},{4,6},{6,0},{1,3},{3,5},{5,7},{7,1},{8,10},{10,12},{12... | collective-permute-start | bytes 1572872 | tf_op jit(solution)/shard_map/ppermute | solution.py:75
  667.3 43.1 %collective-permute-start.37 = (bf16[128,2048]{1,0:T(8,128)(2,1)}, bf16[128,2048]{1,0:T(8,128)(2,1)}, u32[]{:S(2)}, u32[]{:S(2)}) collective-permute-start(bf16[128,2048]{1,0:T(8,128)(2,1)} %get-tuple-element.58), channel_id=1, source_target_pairs={{0,4},{2,6},{4,0},{6,2},{1,5},{3,7},{5,1},{7,3},{8,12},{10,14},{12... | collective-permute-start | bytes 1572872 | tf_op jit(solution)/shard_map/ppermute | solution.py:75
  714.3 21.7 %collective-permute-start.39 = (bf16[128,2048]{1,0:T(8,128)(2,1)S(1)}, bf16[128,2048]{1,0:T(8,128)(2,1)S(1)}, u32[]{:S(2)}, u32[]{:S(2)}) collective-permute-start(bf16[128,2048]{1,0:T(8,128)(2,1)S(1)} %fusion.46), channel_id=1, source_target_pairs={{0,1},{1,0},{2,3},{3,2},{4,5},{5,4},{6,7},{7,6},{8,9},{9,8},{10,11... | collective-permute-start | bytes 1572872 | tf_op jit(solution)/shard_map/ppermute | solution.py:75
  739.7 9.1 collective-permute-start.47
  745.5 11.6 %collective-permute-start.41 = (bf16[128,512]{1,0:T(8,128)(2,1)S(1)}, bf16[128,512]{1,0:T(8,128)(2,1)S(1)}, u32[]{:S(2)}, u32[]{:S(2)}) collective-permute-start(bf16[128,512]{1,0:T(8,128)(2,1)S(1)} %get-tuple-element.105), channel_id=1, source_target_pairs={{0,4},{2,6},{4,0},{6,2},{1,5},{3,7},{5,1},{7,3},{8,12},{10,14},{12... | collective-permute-start | bytes 393224 | tf_op jit(solution)/shard_map/ppermute | solution.py:75
  746.1 11.1 %collective-permute-start.42 = (bf16[128,512]{1,0:T(8,128)(2,1)S(1)}, bf16[128,512]{1,0:T(8,128)(2,1)S(1)}, u32[]{:S(2)}, u32[]{:S(2)}) collective-permute-start(bf16[128,512]{1,0:T(8,128)(2,1)S(1)} %get-tuple-element.107), channel_id=1, source_target_pairs={{0,6},{2,0},{4,2},{6,4},{1,7},{3,1},{5,3},{7,5},{8,14},{10,8},{12,... | collective-permute-start | bytes 393224 | tf_op jit(solution)/shard_map/ppermute | solution.py:75
  762.5 116.3 %collective-permute-start.55 = (bf16[128,768]{1,0:T(8,128)(2,1)S(1)}, bf16[128,768]{1,0:T(8,128)(2,1)S(1)}, u32[]{:S(2)}, u32[]{:S(2)}) collective-permute-start(bf16[128,768]{1,0:T(8,128)(2,1)S(1)} %get-tuple-element.76), channel_id=1, source_target_pairs={{0,2},{2,4},{4,6},{6,0},{1,3},{3,5},{5,7},{7,1},{8,10},{10,12},{12... | collective-permute-start | bytes 589832 | tf_op jit(solution)/shard_map/ppermute | solution.py:75
  765.5 116.6 %collective-permute-start.56 = (bf16[128,768]{1,0:T(8,128)(2,1)S(1)}, bf16[128,768]{1,0:T(8,128)(2,1)S(1)}, u32[]{:S(2)}, u32[]{:S(2)}) collective-permute-start(bf16[128,768]{1,0:T(8,128)(2,1)S(1)} %get-tuple-element.77), channel_id=1, source_target_pairs={{0,4},{2,6},{4,0},{6,2},{1,5},{3,7},{5,1},{7,3},{8,12},{10,14},{12... | collective-permute-start | bytes 589832 | tf_op jit(solution)/shard_map/ppermute | solution.py:75
  767.2 114.9 %collective-permute-start.57 = (bf16[128,768]{1,0:T(8,128)(2,1)S(1)}, bf16[128,768]{1,0:T(8,128)(2,1)S(1)}, u32[]{:S(2)}, u32[]{:S(2)}) collective-permute-start(bf16[128,768]{1,0:T(8,128)(2,1)S(1)} %get-tuple-element.79), channel_id=1, source_target_pairs={{0,6},{2,0},{4,2},{6,4},{1,7},{3,1},{5,3},{7,5},{8,14},{10,8},{12,... | collective-permute-start | bytes 589832 | tf_op jit(solution)/shard_map/ppermute | solution.py:75
  813.6 70.2 %collective-permute-start.52 = (bf16[128,768]{1,0:T(8,128)(2,1)}, bf16[128,768]{1,0:T(8,128)(2,1)S(1)}, u32[]{:S(2)}, u32[]{:S(2)}) collective-permute-start(bf16[128,768]{1,0:T(8,128)(2,1)} %get-tuple-element.80), channel_id=1, source_target_pairs={{0,2},{2,4},{4,6},{6,0},{1,3},{3,5},{5,7},{7,1},{8,10},{10,12},{12... | collective-permute-start | bytes 589832 | tf_op jit(solution)/shard_map/ppermute | solution.py:75
  815.1 71.6 %collective-permute-start.53 = (bf16[128,768]{1,0:T(8,128)(2,1)}, bf16[128,768]{1,0:T(8,128)(2,1)}, u32[]{:S(2)}, u32[]{:S(2)}) collective-permute-start(bf16[128,768]{1,0:T(8,128)(2,1)} %get-tuple-element.81), channel_id=1, source_target_pairs={{0,4},{2,6},{4,0},{6,2},{1,5},{3,7},{5,1},{7,3},{8,12},{10,14},{12... | collective-permute-start | bytes 589832 | tf_op jit(solution)/shard_map/ppermute | solution.py:75
  878.7 8.7 collective-permute-start.54
  882.1 13.3 %collective-permute-start.49 = (bf16[128,768]{1,0:T(8,128)(2,1)}, bf16[128,768]{1,0:T(8,128)(2,1)S(1)}, u32[]{:S(2)}, u32[]{:S(2)}) collective-permute-start(bf16[128,768]{1,0:T(8,128)(2,1)} %get-tuple-element.84), channel_id=1, source_target_pairs={{0,2},{2,4},{4,6},{6,0},{1,3},{3,5},{5,7},{7,1},{8,10},{10,12},{12... | collective-permute-start | bytes 589832 | tf_op jit(solution)/shard_map/ppermute | solution.py:75
  882.1 17.5 %collective-permute-start.50 = (bf16[128,768]{1,0:T(8,128)(2,1)}, bf16[128,768]{1,0:T(8,128)(2,1)}, u32[]{:S(2)}, u32[]{:S(2)}) collective-permute-start(bf16[128,768]{1,0:T(8,128)(2,1)} %get-tuple-element.85), channel_id=1, source_target_pairs={{0,4},{2,6},{4,0},{6,2},{1,5},{3,7},{5,1},{7,3},{8,12},{10,14},{12... | collective-permute-start | bytes 589832 | tf_op jit(solution)/shard_map/ppermute | solution.py:75
  883.8 15.8 %collective-permute-start.51 = (bf16[128,768]{1,0:T(8,128)(2,1)}, bf16[128,768]{1,0:T(8,128)(2,1)}, u32[]{:S(2)}, u32[]{:S(2)}) collective-permute-start(bf16[128,768]{1,0:T(8,128)(2,1)} %get-tuple-element.87), channel_id=1, source_target_pairs={{0,6},{2,0},{4,2},{6,4},{1,7},{3,1},{5,3},{7,5},{8,14},{10,8},{12,... | collective-permute-start | bytes 589832 | tf_op jit(solution)/shard_map/ppermute | solution.py:75
  (71 other events, 1021.4 us)
Sparse Core Ops, SparseCore 0:
  26.6 38.5 all-gather.5
  68.1 161.3 all-gather.7
  232.0 56.8 all-gather.11
  291.2 45.3 all-gather.9
  338.9 45.3 all-gather.13
  571.2 38.3 reduce-scatter.7
  613.0 61.7 reduce-scatter.5
  678.1 68.1 reduce-scatter.13
  749.7 61.7 reduce-scatter.11
  814.7 61.7 reduce-scatter.9

commit v3 on v2

--- a/solution.py
+++ b/solution.py
@@ -79,41 +79,32 @@
     return lax.dynamic_slice_in_dim(jnp.concatenate([blocks, blocks]), first, blocks.shape[0], 0)
 
 
-def reversed_ring(blocks):
-    return jnp.concatenate([blocks[:1], blocks[:0:-1]])
-
-
-def gather_behind(block):
+def block_ahead(blocks, steps):
     count = lax.axis_size("ctx")
-    return jnp.stack([block] + [shift(block, "ctx", d) for d in range(1, count)])
+    place = (lax.axis_index("ctx") + steps) % count
+    return lax.dynamic_index_in_dim(blocks, place, 0, keepdims=False)
+
+
+def gather_ctx(block):
+    count = lax.axis_size("ctx")
+    rank = lax.axis_index("ctx")
+    got = jnp.stack([block] + [shift(block, "ctx", -d) for d in range(1, count)])
+    return take_ring(got, (count - rank) % count)
 
 
 def scatter_sum(blocks):
-    total = blocks[0].astype(F32)
+    total = block_ahead(blocks, 0).astype(F32)
     for d in range(1, blocks.shape[0]):
-        total = total + shift(blocks[d], "ctx", -d).astype(F32)
+        total = total + shift(block_ahead(blocks, d), "ctx", d).astype(F32)
     return total
 
 
 def swap_by_target(blocks):
     count = lax.axis_size("ctx")
     rank = lax.axis_index("ctx")
-    ahead = take_ring(blocks, rank)
-    got = jnp.stack([ahead[0]] + [shift(ahead[d], "ctx", d) for d in range(1, count)])
-    return take_ring(reversed_ring(got), (count - rank) % count)
-
-
-def swap_behind(blocks):
-    count = lax.axis_size("ctx")
-    rank = lax.axis_index("ctx")
-    got = jnp.stack([blocks[0]] + [shift(blocks[d], "ctx", -d) for d in range(1, count)])
+    got = [shift(block_ahead(blocks, d), "ctx", d) for d in range(1, count)]
+    got = jnp.stack([block_ahead(blocks, 0)] + got[::-1])
     return take_ring(got, (count - rank) % count)
-
-
-def swap_to_behind(blocks):
-    count = lax.axis_size("ctx")
-    ahead = take_ring(blocks, lax.axis_index("ctx"))
-    return jnp.stack([ahead[0]] + [shift(ahead[d], "ctx", d) for d in range(1, count)])
 
 
 def greet(peers):
@@ -140,48 +131,391 @@
     return jnp.pad(values, (0, math.prod(TILE) - values.shape[0])).reshape(TILE)
 
 
-def spread_small(gains, marks):
+def place():
+    pair, rank, half = lax.axis_index("dp"), lax.axis_index("ctx"), lax.axis_index("tensor")
+    core = lax.rem(pair, 2)
+    return {
+        "pair": pair,
+        "rank": rank,
+        "half": half,
+        "sibling": pair + 1 - 2 * core,
+        "across": lax.rem(pair + 2, 4),
+        "twin": 1 - half,
+    }
+
+
+class Relay:
+    KINDS = 9
+
+    def __init__(self, here, source, view, rows, send_sem, recv_sem):
+        self.here, self.source, self.view, self.rows = here, source, view, rows
+        self.send_sem, self.recv_sem = send_sem, recv_sem
+        self.copies = {}
+
+    def go(self, kind, source, target, peer):
+        self.copies[kind] = remote(
+            source, target, self.send_sem.at[kind], self.recv_sem.at[kind], peer
+        )
+
+    def first(self):
+        p = self.here
+        target = self.view(p["half"], p["pair"], 0, self.rows)
+        self.go(1, self.source, target, {"dp": p["across"]})
+        self.go(2, self.source, target, {"tensor": p["twin"]})
+        self.go(0, self.source, target, {"dp": p["sibling"]})
+
+    def second(self):
+        p, part = self.here, self.rows // 2
+        self.copies[1].wait_recv()
+        low = self.view(p["half"], p["across"], 0, part)
+        self.go(4, low, low, {"tensor": p["twin"]})
+        whole = self.view(p["half"], p["across"], 0, self.rows)
+        self.go(3, whole, whole, {"dp": p["sibling"]})
+        self.copies[2].wait_recv()
+        high = self.view(p["twin"], p["pair"], part, part)
+        self.go(6, high, high, {"dp": p["across"]})
+        whole = self.view(p["twin"], p["pair"], 0, self.rows)
+        self.go(5, whole, whole, {"dp": p["sibling"]})
+
+    def third(self):
+        p, part = self.here, self.rows // 2
+        self.copies[4].wait_recv()
+        low = self.view(p["twin"], p["across"], 0, part)
+        self.go(7, low, low, {"dp": p["sibling"]})
+        self.copies[6].wait_recv()
+        high = self.view(p["twin"], p["across"], part, part)
+        self.go(8, high, high, {"dp": p["sibling"]})
+
+    def last(self):
+        for kind in (0, 3, 5, 7, 8):
+            self.copies[kind].wait_recv()
+        for copy in self.copies.values():
+            copy.wait_send()
+
+
+class Chain:
+    def __init__(self, rank, count, source, result, send_sem, recv_sem):
+        self.rank, self.count, self.source, self.result = rank, count, source, result
+        self.send_sem, self.recv_sem = send_sem, recv_sem
+
+    def copy(self, way, step):
+        step_to = self.rank + (1 if way == 0 else -1)
+        owner = self.rank - step if way == 0 else self.rank + step
+        owner = jnp.clip(owner, 0, self.count - 1)
+        return pltpu.make_async_remote_copy(
+            src_ref=self.source if step == 0 else self.result.at[owner],
+            dst_ref=self.result.at[owner],
+            send_sem=self.send_sem.at[way, step],
+            recv_sem=self.recv_sem.at[way, step],
+            device_id={"ctx": jnp.clip(step_to, 0, self.count - 1)},
+            device_id_type=MESH,
+        )
+
+    def sends(self, way, step):
+        if way == 0:
+            return (self.rank >= step) & (self.rank < self.count - 1)
+        return (self.rank + step < self.count) & (self.rank > 0)
+
+    def receives(self, way, step):
+        return self.rank > step if way == 0 else self.rank + step < self.count - 1
+
+    def start(self, step):
+        for way in (0, 1):
+            if step > 0:
+
+                @pl.when(self.receives(way, step - 1))
+                def _():
+                    self.copy(way, step - 1).wait_recv()
+
+            @pl.when(self.sends(way, step))
+            def _():
+                self.copy(way, step).start()
+
+    def finish(self):
+        last = self.count - 2
+        for way in (0, 1):
+
+            @pl.when(self.receives(way, last))
+            def _():
+                self.copy(way, last).wait_recv()
+
+            for step in range(self.count - 1):
+
+                @pl.when(self.sends(way, step))
+                def _():
+                    self.copy(way, step).wait_send()
+
+
+SEMS = pltpu.SemaphoreType.DMA
+ANYWHERE = pl.BlockSpec(memory_space=pl.ANY)
+ON_CHIP = pl.BlockSpec(memory_space=pltpu.VMEM)
+
+
+def enter(gains, marks, block, w_query, w_key, w_value):
     count, pairs = lax.axis_size("ctx"), lax.axis_size("dp")
     owners = count * pairs
-
-    def kernel(gain_ref, mark_ref, gains_ref, marks_ref, gain_send, gain_recv, mark_send, mark_recv):
-        rank = lax.axis_index("ctx")
-        me = lax.axis_index("dp") * count + rank
+    depth = w_query.shape[0]
+    widths = [w.shape[1] // count for w in (w_query, w_key, w_value)]
+    width = sum(widths)
+    spots = [sum(widths[:i]) for i in range(3)]
+    rows = block.shape[0]
+
+    def kernel(
+        gain_ref, mark_ref, block_ref, wq_ref, wk_ref, wv_ref,
+        gains_ref, marks_ref, rows_ref, weight_ref,
+        held, gain_send, gain_recv, mark_send, mark_recv,
+        swap_send, swap_recv, chain_send, chain_recv, relay_send, relay_recv, local_sem,
+    ):
+        here = place()
+        rank, pair, half = here["rank"], here["pair"], here["half"]
+        me = pair * count + rank
         far = [lax.rem(me + k, owners) for k in range(1, owners)]
         far = [{"dp": lax.div(t, count), "ctx": lax.rem(t, count)} for t in far]
         near = [{"ctx": lax.rem(rank + k, count)} for k in range(1, count)]
-        greet(far)
-        copies = [
+        greet(far + [{"tensor": here["twin"]}])
+
+        def view(owner_rank):
+            def at(t, p, start, size):
+                first = pl.multiple_of((p * count + owner_rank) * depth + start, 64)
+                return weight_ref.at[pl.ds(first, size), pl.ds(pl.multiple_of(t * width, 128), width)]
+
+            return at
+
+        def columns(ref, i, target):
+            return ref.at[:, pl.ds(pl.multiple_of(target * widths[i], 128), widths[i])]
+
+        sources = (wq_ref, wk_ref, wv_ref)
+        takes = [
+            pltpu.make_async_copy(
+                columns(ref, i, rank), held.at[:, pl.ds(spots[i], widths[i])], local_sem.at[i]
+            )
+            for i, ref in enumerate(sources)
+        ]
+        for take in takes:
+            take.start()
+        small = [
             remote(mark_ref, marks_ref.at[rank], mark_send.at[k], mark_recv.at[k], peer)
             for k, peer in enumerate(near)
         ]
-        copies += [
+        small += [
             remote(gain_ref, gains_ref.at[me], gain_send.at[k], gain_recv.at[k], peer)
             for k, peer in enumerate(far)
         ]
+        own_rows = pl.ds(pl.multiple_of(me * depth, depth), depth)
+        swaps = []
+        for k, peer in enumerate(near):
+            swaps.append([])
+            for i, ref in enumerate(sources):
+                spot = pl.ds(pl.multiple_of(half * width + spots[i], 128), widths[i])
+                swaps[k].append(
+                    remote(
+                        columns(ref, i, peer["ctx"]),
+                        weight_ref.at[own_rows, spot],
+                        swap_send.at[k, i],
+                        swap_recv.at[k, i],
+                        peer,
+                    )
+                )
+        chain = Chain(rank, count, block_ref, rows_ref, chain_send, chain_recv)
+        chain.start(0)
         gains_ref[me] = gain_ref[...]
         marks_ref[rank] = mark_ref[...]
-        for copy in copies:
+        for take in takes:
+            take.wait()
+        keep = pltpu.make_async_copy(held, view(rank)(half, pair, 0, depth), local_sem.at[3])
+        keep.start()
+        relays = [Relay(here, held, view(rank), depth, relay_send.at[0], relay_recv.at[0])]
+        relays[0].first()
+        for k in range(1, count):
+            owner = lax.rem(rank - k + count, count)
+            for swap in swaps[k - 1]:
+                swap.wait_recv()
+            at = view(owner)
+            relays.append(
+                Relay(here, at(half, pair, 0, depth), at, depth, relay_send.at[k], relay_recv.at[k])
+            )
+            relays[k].first()
+            relays[k - 1].second()
+            if k > 1:
+                relays[k - 2].third()
+            if k < count - 1:
+                chain.start(k)
+        relays[-1].second()
+        relays[-2].third()
+        relays[-1].third()
+        for relay in relays:
+            relay.last()
+        keep.wait()
+        chain.finish()
+        for swap in swaps:
+            for copy in swap:
+                copy.wait_send()
+        for copy in small:
             copy.wait()
 
-    sems = pltpu.SemaphoreType.DMA
     return pl.pallas_call(
         kernel,
         out_shape=(
             jax.ShapeDtypeStruct((owners, *TILE), F32),
             jax.ShapeDtypeStruct((count, *TILE), jnp.int32),
+            jax.ShapeDtypeStruct((count, rows, block.shape[1]), block.dtype),
+            jax.ShapeDtypeStruct((owners * depth, 2 * width), w_query.dtype),
         ),
-        in_specs=[pl.BlockSpec(memory_space=pltpu.VMEM)] * 2,
-        out_specs=(pl.BlockSpec(memory_space=pltpu.VMEM),) * 2,
+        in_specs=[ON_CHIP] * 2 + [ANYWHERE] * 4,
+        out_specs=(ON_CHIP, ON_CHIP, ANYWHERE, ANYWHERE),
         scratch_shapes=[
-            sems((owners - 1,)),
-            sems((owners - 1,)),
-            sems((count - 1,)),
-            sems((count - 1,)),
+            pltpu.VMEM((depth, width), w_query.dtype),
+            SEMS((owners - 1,)),
+            SEMS((owners - 1,)),
+            SEMS((count - 1,)),
+            SEMS((count - 1,)),
+            SEMS((count - 1, 3)),
+            SEMS((count - 1, 3)),
+            SEMS((2, count - 1)),
+            SEMS((2, count - 1)),
+            SEMS((count, Relay.KINDS)),
+            SEMS((count, Relay.KINDS)),
+            SEMS((4,)),
         ],
         compiler_params=pltpu.CompilerParams(collective_id=0, has_side_effects=True),
-        name="spread_small",
-    )(gains, marks)
+        name="enter",
+    )(gains, marks, block, w_query, w_key, w_value)
+
+
+def spread_mlp(first, second, pieces):
+    count, pairs = lax.axis_size("ctx"), lax.axis_size("dp")
+    kinds, depth, width = pieces[0].shape
+    rows, features = first.shape
+
+    def kernel(first_ref, second_ref, *rest):
+        piece_refs, rest = rest[:count], rest[count:]
+        firsts_ref, seconds_ref = rest[:2]
+        weight_refs, rest = rest[2 : 2 + kinds], rest[2 + kinds :]
+        held, chain_send, chain_recv, relay_send, relay_recv, take_sem, keep_sem = rest
+        here = place()
+        rank, pair, half = here["rank"], here["pair"], here["half"]
+        greet(
+            [{"ctx": lax.rem(rank + k, count)} for k in range(1, count)]
+            + [{"dp": here["sibling"]}, {"dp": here["across"]}, {"tensor": here["twin"]}]
+        )
+        takes = []
+        for i in range(kinds):
+            for d, ref in enumerate(piece_refs):
+                owner = lax.rem(rank - d + count, count)
+                take = pltpu.make_async_copy(
+                    ref.at[i],
+                    held.at[i, pl.ds(pl.multiple_of(owner * depth, depth), depth)],
+                    take_sem.at[i, d],
+                )
+                take.start()
+                takes.append(take)
+        chains = [
+            Chain(rank, count, first_ref, firsts_ref, chain_send.at[0], chain_recv.at[0]),
+            Chain(rank, count, second_ref, seconds_ref, chain_send.at[1], chain_recv.at[1]),
+        ]
+        chains[0].start(0)
+        block = count * depth
+
+        def view(i):
+            def at(t, p, start, size):
+                first = pl.multiple_of(p * block + start, 64)
+                return weight_refs[i].at[
+                    pl.ds(first, size), pl.ds(pl.multiple_of(t * width, 128), width)
+                ]
+
+            return at
+
+        relays, keeps = [], []
+        for i in range(kinds):
+            for take in takes[i * count : (i + 1) * count]:
+                take.wait()
+            keeps.append(
+                pltpu.make_async_copy(held.at[i], view(i)(half, pair, 0, block), keep_sem.at[i])
+            )
+            keeps[i].start()
+            relays.append(
+                Relay(here, held.at[i], view(i), block, relay_send.at[i], relay_recv.at[i])
+            )
+            relays[i].first()
+        chains[0].start(1)
+        relays[0].second()
+        chains[0].start(2)
+        chains[1].start(0)
+        relays[0].third()
+        relays[1].second()
+        chains[1].start(1)
+        relays[1].third()
+        relays[2].second()
+        chains[1].start(2)
+        relays[2].third()
+        for relay in relays:
+            relay.last()
+        for keep in keeps:
+            keep.wait()
+        for chain in chains:
+            chain.finish()
+
+    return pl.pallas_call(
+        kernel,
+        out_shape=(
+            jax.ShapeDtypeStruct((count, rows, features), first.dtype),
+            jax.ShapeDtypeStruct((count, rows, features), second.dtype),
+        )
+        + (jax.ShapeDtypeStruct((pairs * count * depth, 2 * width), pieces[0].dtype),) * kinds,
+        in_specs=[ANYWHERE] * (2 + count),
+        out_specs=(ANYWHERE,) * (2 + kinds),
+        scratch_shapes=[
+            pltpu.VMEM((kinds, count * depth, width), pieces[0].dtype),
+            SEMS((2, 2, count - 1)),
+            SEMS((2, 2, count - 1)),
+            SEMS((kinds, Relay.KINDS)),
+            SEMS((kinds, Relay.KINDS)),
+            SEMS((kinds, count)),
+            SEMS((kinds,)),
+        ],
+        compiler_params=pltpu.CompilerParams(
+            collective_id=2, has_side_effects=True, vmem_limit_bytes=16 * 1024 * 1024
+        ),
+        name="spread_mlp",
+    )(first, second, *pieces)
+
+
+def swap_ctx(blocks, collective_id):
+    count = lax.axis_size("ctx")
+
+    def kernel(blocks_ref, got_ref, held, send_sem, recv_sem, local_sem):
+        rank = lax.axis_index("ctx")
+        peers = [lax.rem(rank + k, count) for k in range(1, count)]
+        greet([{"ctx": peer} for peer in peers])
+        copies = [
+            remote(
+                blocks_ref.at[peer], got_ref.at[rank], send_sem.at[k], recv_sem.at[k], {"ctx": peer}
+            )
+            for k, peer in enumerate(peers)
+        ]
+        take = pltpu.make_async_copy(blocks_ref.at[rank], held, local_sem.at[0])
+        take.start()
+        take.wait()
+        keep = pltpu.make_async_copy(held, got_ref.at[rank], local_sem.at[1])
+        keep.start()
+        keep.wait()
+        for copy in copies:
+            copy.wait()
+
+    return pl.pallas_call(
+        kernel,
+        out_shape=jax.ShapeDtypeStruct(blocks.shape, blocks.dtype),
+        in_specs=[ANYWHERE],
+        out_specs=ANYWHERE,
+        scratch_shapes=[
+            pltpu.VMEM(blocks.shape[1:], blocks.dtype),
+            SEMS((count - 1,)),
+            SEMS((count - 1,)),
+            SEMS((2,)),
+        ],
+        compiler_params=pltpu.CompilerParams(collective_id=collective_id, has_side_effects=True),
+        name=f"swap_ctx_{collective_id}",
+    )(blocks)
 
 
 def owner_sums(tiles):
@@ -230,14 +564,17 @@
     )(tiles)
 
 
-def slices_of(shard):
-    count = lax.axis_size("ctx")
-    rows, width = shard.shape
-    mine = swap_by_target(shard.reshape(rows, count, width // count).transpose(1, 0, 2))
-    mine = mine.reshape(count * rows, width // count)
-    full = lax.all_gather(mine, ("tensor", "dp"), axis=0, tiled=True)
+def weight_partial(rows_side, columns_side):
     tensors = lax.axis_size("tensor")
-    return full.reshape(tensors, full.shape[0] // tensors, full.shape[1])
+    cols = columns_side.shape[1] // tensors
+    return jnp.stack(
+        [
+            jnp.dot(
+                rows_side.T, columns_side[:, t * cols : (t + 1) * cols], preferred_element_type=F32
+            ).astype(BF16)
+            for t in range(tensors)
+        ]
+    )
 
 
 def shards_of(partial):
@@ -285,39 +622,41 @@
     q_cols = w_query.shape[1] // count
     k_cols = w_key.shape[1] // count
     local_kv = k_cols // HEAD_DIM
+    kv_heads = tensors * local_kv
     group = q_cols // k_cols
     in_width = q_cols + 2 * k_cols
-    in_shard = jnp.concatenate(
-        [
-            w_query.reshape(-1, count, q_cols),
-            w_key.reshape(-1, count, k_cols),
-            w_value.reshape(-1, count, k_cols),
-        ],
-        axis=2,
-    ).reshape(w_query.shape[0], count * in_width)
-    in_weight = slices_of(in_shard)
+    piece = attn_gain.shape[0]
+    small = q_gain.shape[0]
+
+    input_own = lax.dynamic_slice_in_dim(inputs[0], half * own_rows, own_rows, 0)
+    grad_own = lax.dynamic_slice_in_dim(out_grad[0], half * own_rows, own_rows, 0)
+    own_gains = jnp.concatenate([attn_gain, mlp_gain, q_gain, k_gain]).astype(F32)
+    own_marks = jnp.concatenate([segment_ids[0], positions[0]])
+    gains, marks, input_all, in_weight = enter(
+        to_tile(own_gains), to_tile(own_marks), input_own, w_query, w_key, w_value
+    )
     out_weight = lax.all_gather(w_out.T, ("tensor", "dp", "ctx"), axis=0, tiled=True).reshape(
         tensors, width, head_rows
     )
-    gate_weight = slices_of(w_gate)
-    up_weight = slices_of(w_up)
-    down_weight = slices_of(w_down.T)
-
-    piece = attn_gain.shape[0]
-    small = q_gain.shape[0]
-    own_gains = jnp.concatenate([attn_gain, mlp_gain, q_gain, k_gain]).astype(F32)
-    own_marks = jnp.concatenate([segment_ids[0], positions[0]])
-    gains, marks = spread_small(to_tile(own_gains), to_tile(own_marks))
     gains = gains.reshape(gains.shape[0], -1)
     attn_scale = gains[:, :piece].reshape(-1)
     mlp_scale = gains[:, piece : 2 * piece].reshape(-1)
     query_scale = gains[:, 2 * piece : 2 * piece + small].reshape(-1)
     key_scale = gains[:, 2 * piece + small : 2 * (piece + small)].reshape(-1)
+
+    mlp_shards = jnp.stack([w_gate, w_up, w_down.T]).reshape(3, -1, count, w_gate.shape[1] // count)
+    mlp_shards, in_weight = lax.optimization_barrier((mlp_shards, in_weight))
+    mlp_pieces = [
+        shift(
+            lax.dynamic_index_in_dim(mlp_shards, (rank + d) % count, 2, keepdims=False), "ctx", d
+        )
+        if d
+        else lax.dynamic_index_in_dim(mlp_shards, rank, 2, keepdims=False)
+        for d in range(count)
+    ]
+
     marks = marks.reshape(count, -1)[:, : 2 * tok_count].reshape(count, 2, tensors, own_rows)
-    behind = (rank - jnp.arange(count)) % count
-    marks = marks[behind]
-    starts = behind * tok_count
-    offsets = starts[:, None] + jnp.arange(own_rows)[None, :]
+    offsets = jnp.arange(count)[:, None] * tok_count + jnp.arange(own_rows)[None, :]
 
     def marks_of(which):
         segs = lax.dynamic_index_in_dim(marks[:, 0], which, 1, keepdims=False).reshape(rows)
@@ -326,18 +665,20 @@
     own_segs, own_index = marks_of(half)
     twin_segs, twin_index = marks_of(1 - half)
     own_positions = lax.dynamic_index_in_dim(marks[:, 1], half, 1, keepdims=False).reshape(rows)
-    key_segs = jnp.concatenate([own_segs, twin_segs])
-    key_index = jnp.concatenate([own_index, twin_index])
-    allowed = (key_index[None, :] <= own_index[:, None]) & (key_segs[None, :] == own_segs[:, None])
-
-    stream = lax.dynamic_slice_in_dim(inputs[0], half * own_rows, own_rows, 0).astype(F32)
-    grad_own = lax.dynamic_slice_in_dim(out_grad[0], half * own_rows, own_rows, 0)
-    normed_attn, attn_norm_pullback = jax.vjp(rms_norm, stream, attn_scale)
-    normed_low = gather_behind(normed_attn.astype(BF16)).reshape(rows, width)
-    raw = dot32(normed_low, in_weight, "mk,tkc->mtc")
-    query_raw = raw[..., :q_cols].reshape(rows, tensors * local_kv * group, HEAD_DIM)
-    key_raw = raw[..., q_cols : q_cols + k_cols].reshape(rows, tensors * local_kv, HEAD_DIM)
-    kv_heads = tensors * local_kv
+
+    def allowed_of(key_segs, key_index):
+        return (key_index[None, :] <= own_index[:, None]) & (key_segs[None, :] == own_segs[:, None])
+
+    allowed = (allowed_of(own_segs, own_index), allowed_of(twin_segs, twin_index))
+
+    stream = input_own.astype(F32)
+    input_all = lax.dynamic_update_index_in_dim(input_all, input_own, rank, 0)
+    normed_low = rms_norm(input_all.reshape(rows, width).astype(F32), attn_scale).astype(BF16)
+    _, attn_norm_pullback = jax.vjp(rms_norm, stream, attn_scale)
+    raw = jnp.dot(normed_low, in_weight, preferred_element_type=F32)
+    raw = raw.reshape(rows, tensors, in_width)
+    query_raw = raw[..., :q_cols].reshape(rows, kv_heads * group, HEAD_DIM)
+    key_raw = raw[..., q_cols : q_cols + k_cols].reshape(rows, kv_heads, HEAD_DIM)
     value_low = raw[..., q_cols + k_cols :].astype(BF16).reshape(rows, kv_heads, HEAD_DIM)
     cosine_table, sine_table = rope_tables(own_positions, HEAD_DIM)
     cosine_table = cosine_table[:, None, :]
@@ -346,68 +687,89 @@
     def norm_rope(raw_heads, gain_vector):
         return head_norm(raw_heads, gain_vector, cosine_table, sine_table)
 
-    query_rot, query_pullback = jax.vjp(norm_rope, query_raw, query_scale)
     key_rot, key_pullback = jax.vjp(norm_rope, key_raw, key_scale)
-    query_low = query_rot.astype(BF16).reshape(rows, kv_heads, group, HEAD_DIM)
     key_low = key_rot.astype(BF16)
     kv_own = jnp.stack([key_low, value_low])
-    kv_all = jnp.concatenate([kv_own, shift(kv_own, "tensor", 1)], axis=1)
-    keys, values = kv_all[0], kv_all[1]
-
-    scores = dot32(query_low, keys, "mkgd,nkd->kgmn") * score_scale
-    masked = jnp.where(allowed, scores, masked_value)
-    best = jnp.max(masked, axis=-1, keepdims=True)
-    weights = jnp.where(allowed, jnp.exp(masked - best), 0.0)
-    total = jnp.sum(weights, axis=-1, keepdims=True)
-    prob = weights / total
-    prob_low = prob.astype(BF16)
-    attended = dot32(prob_low, values, "kgmn,nkd->mkgd")
-    attended_heads = attended.astype(BF16).reshape(count, own_rows, tensors, q_cols)
-    attended_own = swap_behind(attended_heads)
+    kv_twin = shift(kv_own, "tensor", 1)
+    query_rot, query_pullback = jax.vjp(norm_rope, query_raw, query_scale)
+    query_low = query_rot.astype(BF16).reshape(rows, kv_heads, group, HEAD_DIM)
+    keys = (kv_own[0], kv_twin[0])
+    values = (kv_own[1], kv_twin[1])
+
+    scores = [
+        jnp.where(ok, dot32(query_low, key, "mkgd,nkd->kgmn") * score_scale, masked_value)
+        for ok, key in zip(allowed, keys)
+    ]
+    best = jnp.maximum(*[jnp.max(s, axis=-1, keepdims=True) for s in scores])
+    weights = [jnp.where(ok, jnp.exp(s - best), 0.0) for ok, s in zip(allowed, scores)]
+    total = sum(jnp.sum(w, axis=-1, keepdims=True) for w in weights)
+    prob = [w / total for w in weights]
+    prob_low = [p.astype(BF16) for p in prob]
+    attended = sum(dot32(p, v, "kgmn,nkd->mkgd") for p, v in zip(prob_low, values))
+    attended_low = attended.astype(BF16).reshape(rows, tensors * q_cols)
+    attended_own = swap_ctx(attended_low.reshape(count, own_rows, tensors * q_cols), 3)
+    attended_own = attended_own.reshape(count, own_rows, tensors, q_cols)
     attended_own = attended_own.transpose(1, 2, 0, 3).reshape(own_rows, tensors, head_rows)
     middle = stream + dot32(attended_own, out_weight, "mtr,tkr->mk")
     normed_mid, mlp_norm_pullback = jax.vjp(rms_norm, middle, mlp_scale)
-    mid_low = gather_behind(normed_mid.astype(BF16)).reshape(rows, width)
-    grad_low = gather_behind(grad_own).reshape(rows, width)
-
-    gate = dot32(mid_low, gate_weight, "mk,tkc->tmc")
-    upward = dot32(mid_low, up_weight, "mk,tkc->tmc")
+    mid_own = normed_mid.astype(BF16)
+    mid_low, grad_low, gate_weight, up_weight, down_weight = spread_mlp(
+        mid_own, grad_own, mlp_pieces
+    )
+    mid_low = lax.dynamic_update_index_in_dim(mid_low, mid_own, rank, 0).reshape(rows, width)
+    grad_low = lax.dynamic_update_index_in_dim(grad_low, grad_own, rank, 0).reshape(rows, width)
+
+    gate = jnp.dot(mid_low, gate_weight, preferred_element_type=F32)
+    upward = jnp.dot(mid_low, up_weight, preferred_element_type=F32)
     hidden, silu_pullback = jax.vjp(silu_product, gate, upward)
     hidden_low = hidden.astype(BF16)
-    hidden_grad = dot32(grad_low, down_weight, "mk,tkc->tmc")
+    hidden_grad = jnp.dot(grad_low, down_weight, preferred_element_type=F32)
     gate_grad, upward_grad = silu_pullback(hidden_grad)
     gate_grad_low = gate_grad.astype(BF16)
     upward_grad_low = upward_grad.astype(BF16)
-    mid_grad_part = dot32(gate_grad_low, gate_weight, "tmc,tkc->mk") + dot32(
-        upward_grad_low, up_weight, "tmc,tkc->mk"
+    mid_grad_part = jnp.dot(gate_grad_low, gate_weight.T, preferred_element_type=F32) + jnp.dot(
+        upward_grad_low, up_weight.T, preferred_element_type=F32
     )
     mid_grad = scatter_sum(mid_grad_part.astype(BF16).reshape(count, own_rows, width))
-    down_part = dot32(hidden_low, down_weight, "tmc,tkc->mk")
-    down_sum = scatter_sum(down_part.astype(BF16).reshape(count, own_rows, width))
-    output = with_twin((middle + down_sum).astype(BF16))[None]
-    down_weight_grad = shards_of(dot32(grad_low, hidden_low, "mk,tmc->tkc")).T
-    gate_weight_grad = shards_of(dot32(mid_low, gate_grad_low, "mk,tmc->tkc"))
-    up_weight_grad = shards_of(dot32(mid_low, upward_grad_low, "mk,tmc->tkc"))
+    mlp_grads = [
+        weight_partial(mid_low, gate_grad_low),
+        weight_partial(mid_low, upward_grad_low),
+        weight_partial(grad_low, hidden_low),
+    ]
+    down_part = jnp.dot(hidden_low, down_weight.T, preferred_element_type=F32).astype(BF16)
+    mid_grad, down_part, mlp_grads = lax.optimization_barrier((mid_grad, down_part, mlp_grads))
+    gate_weight_grad, up_weight_grad, down_weight_grad = [shards_of(g) for g in mlp_grads]
+    down_weight_grad = down_weight_grad.T
 
     middle_norm_grad, mlp_gain_grad = mlp_norm_pullback(mid_grad)
     middle_grad = grad_own.astype(F32) + middle_norm_grad
     branch_grad = middle_grad.astype(BF16)
-    branch_all = gather_behind(branch_grad).reshape(rows, width)
-    attended_low = attended_heads.reshape(rows, tensors, q_cols)
-    out_weight_grad = shards_of(dot32(branch_all, attended_low, "mk,mtr->tkr")).T
     attended_grad = dot32(branch_grad, out_weight, "mk,tkr->mtr").astype(BF16)
     attended_grad = attended_grad.reshape(own_rows, tensors, count, q_cols).transpose(2, 0, 1, 3)
-    attended_grad = swap_to_behind(attended_grad).reshape(rows, kv_heads, group, HEAD_DIM)
-    prob_grad = dot32(attended_grad, values, "mkgd,nkd->kgmn")
-    delta = jnp.sum(prob * prob_grad, axis=-1, keepdims=True)
-    score_grad = (prob * (prob_grad - delta)).astype(BF16)
-    query_grad = dot32(score_grad, keys, "kgmn,nkd->mkgd") * score_scale
-    key_grad_all = dot32(score_grad, query_low, "kgmn,mkgd->nkd")
-    value_grad_all = dot32(prob_low, attended_grad, "kgmn,mkgd->nkd")
-    kv_grad_all = jnp.stack([key_grad_all, value_grad_all])
-    kv_grad = kv_grad_all[:, :rows] + shift(
-        kv_grad_all[:, rows:].astype(BF16), "tensor", 1
-    ).astype(F32)
+    attended_grad = swap_ctx(attended_grad.reshape(count, own_rows, tensors * q_cols), 4)
+    branch_grad, down_part, attended_grad = lax.optimization_barrier(
+        (branch_grad, down_part, attended_grad)
+    )
+    down_sum = scatter_sum(down_part.reshape(count, own_rows, width))
+    output = with_twin((middle + down_sum).astype(BF16))[None]
+    branch_all = gather_ctx(branch_grad).reshape(rows, width)
+    out_weight_grad = shards_of(weight_partial(branch_all, attended_low)).T
+    attended_grad = attended_grad.reshape(rows, kv_heads, group, HEAD_DIM)
+    prob_grad = [dot32(attended_grad, v, "mkgd,nkd->kgmn") for v in values]
+    delta = sum(jnp.sum(p * g, axis=-1, keepdims=True) for p, g in zip(prob, prob_grad))
+    score_grad = [(p * (g - delta)).astype(BF16) for p, g in zip(prob, prob_grad)]
+
+    def key_side(i):
+        return jnp.stack(
+            [
+                dot32(score_grad[i], query_low, "kgmn,mkgd->nkd"),
+                dot32(prob_low[i], attended_grad, "kgmn,mkgd->nkd"),
+            ]
+        )
+
+    kv_back = shift(key_side(1).astype(BF16), "tensor", 1)
+    kv_grad = key_side(0) + kv_back.astype(F32)
+    query_grad = sum(dot32(g, k, "kgmn,nkd->mkgd") for g, k in zip(score_grad, keys)) * score_scale
     query_raw_grad, query_gain_grad = query_pullback(query_grad.reshape(query_raw.shape))
     key_raw_grad, key_gain_grad = key_pullback(kv_grad[0] * score_scale)
     raw_grad_low = jnp.concatenate(
@@ -417,10 +779,821 @@
             kv_grad[1].astype(BF16).reshape(rows, tensors, k_cols),
         ],
         axis=2,
-    )
-    normed_grad_part = dot32(raw_grad_low, in_weight, "mtc,tkc->mk")
+    ).reshape(rows, tensors * in_width)
+    normed_grad_part = jnp.dot(raw_grad_low, in_weight.T, preferred_element_type=F32)
     normed_grad = scatter_sum(normed_grad_part.astype(BF16).reshape(count, own_rows, width))
-    in_weight_grad = shards_of(dot32(normed_low, raw_grad_low, "mk,mtc->tkc"))
+    in_weight_grad = shards_of(weight_partial(normed_low, raw_grad_low))
+    in_weight_grad = in_weight_grad.reshape(-1, count, in_width)
+    query_weight_grad = in_weight_grad[..., :q_cols].reshape(w_query.shape)
+    key_weight_grad = in_weight_grad[..., q_cols : q_cols + k_cols].reshape(w_key.shape)
+    value_weight_grad = in_weight_grad[..., q_cols + k_cols :].reshape(w_value.shape)
+    stream_norm_grad, attn_gain_grad = attn_norm_pullback(normed_grad)
+    input_grad = with_twin((middle_grad + stream_norm_grad).astype(BF16))[None]
+
+    gain_grads = jnp.concatenate(
+        [
+            attn_gain_grad.reshape(-1, piece),
+            mlp_gain_grad.reshape(-1, piece),
+            query_gain_grad.reshape(-1, small),
+            key_gain_grad.reshape(-1, small),
+        ],
+        axis=1,
+    )
+    gain_grads = owner_sums(jax.vmap(to_tile)(gain_grads)).reshape(-1)
+    return (
+        output,
+        input_grad,
+        gain_grads[:piece],
+        query_weight_grad,
+        key_weight_grad,
+        value_weight_grad,
+        gain_grads[2 * piece : 2 * piece + small],
+        gain_grads[2 * piece + small : 2 * (piece + small)],
+        out_weight_grad,
+        gain_grads[piece : 2 * piece],
+        gate_weight_grad,
+        up_weight_grad,
+        down_weight_grad,
+    )
+
+
+def can_slice(mesh, inputs, w_key, w_gate):
+    tensors, count = mesh.shape["tensor"], mesh.shape["ctx"]
+    return (
+        (mesh.shape["dp"], count, tensors) == (4, 4, 2)
+        and inputs.shape[0] == mesh.shape["dp"]
+        and (inputs.shape[1] // count) % (16 * tensors) == 0
+        and w_key.shape[1] % (tensors * count * HEAD_DIM) == 0
+        and inputs.shape[1] // count * 2 <= math.prod(TILE)
+        and w_gate.shape[1] % (tensors * count * 128) == 0
+    )
+
+
+def from_behind(value, axis, steps):
+    count = lax.axis_size(axis)
+    pairs = [(source, (source + steps) % count) for source in range(count)]
+    return lax.ppermute(value, axis, pairs)
+
+
+def rope_tables(positions, head_size):
+    half_dim = head_size // 2
+    frequency = rope_base ** (-(jnp.arange(half_dim, dtype=jnp.float32) * 2.0) / head_size)
+    angles = positions.astype(jnp.float32)[..., None] * frequency
+    return (jnp.cos(angles), jnp.sin(angles))
+
+
+def rotate(values, cosine_table, sine_table):
+    half_dim = values.shape[-1] // 2
+    first_half = values[..., :half_dim]
+    second_half = values[..., half_dim:]
+    return jnp.concatenate(
+        [
+            first_half * cosine_table - second_half * sine_table,
+            second_half * cosine_table + first_half * sine_table,
+        ],
+        axis=-1,
+    )
+
+
+def head_norm(raw_heads, gain_vector, cosine_table, sine_table):
+    scaled = (
+        raw_heads
+        * lax.rsqrt(jnp.mean(raw_heads * raw_heads, axis=-1, keepdims=True) + epsilon)
+        * gain_vector
+    )
+    return rotate(scaled, cosine_table, sine_table)
+
+
+def rms_norm(stream, gain_vector):
+    return (
+        stream
+        * lax.rsqrt(jnp.mean(stream * stream, axis=-1, keepdims=True) + epsilon)
+        * gain_vector
+    )
+
+
+def silu_product(gate, upward):
+    return jax.nn.silu(gate) * upward
+
+
+def dot32(left, right, spec):
+    return jnp.einsum(spec, left, right, preferred_element_type=F32)
+
+
+def shift(value, axis, steps):
+    count = lax.axis_size(axis)
+    pairs = [(source, (source + steps) % count) for source in range(count)]
+    return lax.ppermute(value, axis, pairs)
+
+
+def take_ring(blocks, first):
+    return lax.dynamic_slice_in_dim(jnp.concatenate([blocks, blocks]), first, blocks.shape[0], 0)
+
+
+def block_ahead(blocks, steps):
+    count = lax.axis_size("ctx")
+    place = (lax.axis_index("ctx") + steps) % count
+    return lax.dynamic_index_in_dim(blocks, place, 0, keepdims=False)
+
+
+def gather_ctx(block):
+    count = lax.axis_size("ctx")
+    rank = lax.axis_index("ctx")
+    got = jnp.stack([block] + [shift(block, "ctx", -d) for d in range(1, count)])
+    return take_ring(got, (count - rank) % count)
+
+
+def scatter_sum(blocks):
+    total = block_ahead(blocks, 0).astype(F32)
+    for d in range(1, blocks.shape[0]):
+        total = total + shift(block_ahead(blocks, d), "ctx", d).astype(F32)
+    return total
+
+
+def swap_by_target(blocks):
+    count = lax.axis_size("ctx")
+    rank = lax.axis_index("ctx")
+    got = [shift(block_ahead(blocks, d), "ctx", d) for d in range(1, count)]
+    got = jnp.stack([block_ahead(blocks, 0)] + got[::-1])
+    return take_ring(got, (count - rank) % count)
+
+
+def greet(peers):
+    barrier = pltpu.get_barrier_semaphore()
+    for peer in peers:
+        pl.semaphore_signal(barrier, inc=1, device_id=peer, device_id_type=MESH)
+    pl.semaphore_wait(barrier, len(peers))
+
+
+def remote(source, target, send_sem, recv_sem, peer):
+    copy = pltpu.make_async_remote_copy(
+        src_ref=source,
+        dst_ref=target,
+        send_sem=send_sem,
+        recv_sem=recv_sem,
+        device_id=peer,
+        device_id_type=MESH,
+    )
+    copy.start()
+    return copy
+
+
+def to_tile(values):
+    return jnp.pad(values, (0, math.prod(TILE) - values.shape[0])).reshape(TILE)
+
+
+def place():
+    pair, rank, half = lax.axis_index("dp"), lax.axis_index("ctx"), lax.axis_index("tensor")
+    core = lax.rem(pair, 2)
+    return {
+        "pair": pair,
+        "rank": rank,
+        "half": half,
+        "sibling": pair + 1 - 2 * core,
+        "across": lax.rem(pair + 2, 4),
+        "twin": 1 - half,
+    }
+
+
+class Relay:
+    KINDS = 9
+
+    def __init__(self, here, source, view, rows, send_sem, recv_sem):
+        self.here, self.source, self.view, self.rows = here, source, view, rows
+        self.send_sem, self.recv_sem = send_sem, recv_sem
+        self.copies = {}
+
+    def go(self, kind, source, target, peer):
+        self.copies[kind] = remote(
+            source, target, self.send_sem.at[kind], self.recv_sem.at[kind], peer
+        )
+
+    def first(self):
+        p = self.here
+        target = self.view(p["half"], p["pair"], 0, self.rows)
+        self.go(1, self.source, target, {"dp": p["across"]})
+        self.go(2, self.source, target, {"tensor": p["twin"]})
+        self.go(0, self.source, target, {"dp": p["sibling"]})
+
+    def second(self):
+        p, part = self.here, self.rows // 2
+        self.copies[1].wait_recv()
+        low = self.view(p["half"], p["across"], 0, part)
+        self.go(4, low, low, {"tensor": p["twin"]})
+        whole = self.view(p["half"], p["across"], 0, self.rows)
+        self.go(3, whole, whole, {"dp": p["sibling"]})
+        self.copies[2].wait_recv()
+        high = self.view(p["twin"], p["pair"], part, part)
+        self.go(6, high, high, {"dp": p["across"]})
+        whole = self.view(p["twin"], p["pair"], 0, self.rows)
+        self.go(5, whole, whole, {"dp": p["sibling"]})
+
+    def third(self):
+        p, part = self.here, self.rows // 2
+        self.copies[4].wait_recv()
+        low = self.view(p["twin"], p["across"], 0, part)
+        self.go(7, low, low, {"dp": p["sibling"]})
+        self.copies[6].wait_recv()
+        high = self.view(p["twin"], p["across"], part, part)
+        self.go(8, high, high, {"dp": p["sibling"]})
+
+    def last(self):
+        for kind in (0, 3, 5, 7, 8):
+            self.copies[kind].wait_recv()
+        for copy in self.copies.values():
+            copy.wait_send()
+
+
+class Chain:
+    def __init__(self, rank, count, source, result, send_sem, recv_sem):
+        self.rank, self.count, self.source, self.result = rank, count, source, result
+        self.send_sem, self.recv_sem = send_sem, recv_sem
+
+    def copy(self, way, step):
+        step_to = self.rank + (1 if way == 0 else -1)
+        owner = self.rank - step if way == 0 else self.rank + step
+        owner = jnp.clip(owner, 0, self.count - 1)
+        return pltpu.make_async_remote_copy(
+            src_ref=self.source if step == 0 else self.result.at[owner],
+            dst_ref=self.result.at[owner],
+            send_sem=self.send_sem.at[way, step],
+            recv_sem=self.recv_sem.at[way, step],
+            device_id={"ctx": jnp.clip(step_to, 0, self.count - 1)},
+            device_id_type=MESH,
+        )
+
+    def sends(self, way, step):
+        if way == 0:
+            return (self.rank >= step) & (self.rank < self.count - 1)
+        return (self.rank + step < self.count) & (self.rank > 0)
+
+    def receives(self, way, step):
+        return self.rank > step if way == 0 else self.rank + step < self.count - 1
+
+    def start(self, step):
+        for way in (0, 1):
+            if step > 0:
+
+                @pl.when(self.receives(way, step - 1))
+                def _():
+                    self.copy(way, step - 1).wait_recv()
+
+            @pl.when(self.sends(way, step))
+            def _():
+                self.copy(way, step).start()
+
+    def finish(self):
+        last = self.count - 2
+        for way in (0, 1):
+
+            @pl.when(self.receives(way, last))
+            def _():
+                self.copy(way, last).wait_recv()
+
+            for step in range(self.count - 1):
+
+                @pl.when(self.sends(way, step))
+                def _():
+                    self.copy(way, step).wait_send()
+
+
+SEMS = pltpu.SemaphoreType.DMA
+ANYWHERE = pl.BlockSpec(memory_space=pl.ANY)
+ON_CHIP = pl.BlockSpec(memory_space=pltpu.VMEM)
+
+
+def enter(gains, marks, block, w_query, w_key, w_value):
+    count, pairs = lax.axis_size("ctx"), lax.axis_size("dp")
+    owners = count * pairs
+    depth = w_query.shape[0]
+    widths = [w.shape[1] // count for w in (w_query, w_key, w_value)]
+    width = sum(widths)
+    spots = [sum(widths[:i]) for i in range(3)]
+    rows = block.shape[0]
+
+    def kernel(
+        gain_ref, mark_ref, block_ref, wq_ref, wk_ref, wv_ref,
+        gains_ref, marks_ref, rows_ref, weight_ref,
+        held, gain_send, gain_recv, mark_send, mark_recv,
+        swap_send, swap_recv, chain_send, chain_recv, relay_send, relay_recv, local_sem,
+    ):
+        here = place()
+        rank, pair, half = here["rank"], here["pair"], here["half"]
+        me = pair * count + rank
+        far = [lax.rem(me + k, owners) for k in range(1, owners)]
+        far = [{"dp": lax.div(t, count), "ctx": lax.rem(t, count)} for t in far]
+        near = [{"ctx": lax.rem(rank + k, count)} for k in range(1, count)]
+        greet(far + [{"tensor": here["twin"]}])
+
+        def view(owner_rank):
+            def at(t, p, start, size):
+                first = pl.multiple_of((p * count + owner_rank) * depth + start, 64)
+                return weight_ref.at[pl.ds(first, size), pl.ds(pl.multiple_of(t * width, 128), width)]
+
+            return at
+
+        def columns(ref, i, target):
+            return ref.at[:, pl.ds(pl.multiple_of(target * widths[i], 128), widths[i])]
+
+        sources = (wq_ref, wk_ref, wv_ref)
+        takes = [
+            pltpu.make_async_copy(
+                columns(ref, i, rank), held.at[:, pl.ds(spots[i], widths[i])], local_sem.at[i]
+            )
+            for i, ref in enumerate(sources)
+        ]
+        for take in takes:
+            take.start()
+        small = [
+            remote(mark_ref, marks_ref.at[rank], mark_send.at[k], mark_recv.at[k], peer)
+            for k, peer in enumerate(near)
+        ]
+        small += [
+            remote(gain_ref, gains_ref.at[me], gain_send.at[k], gain_recv.at[k], peer)
+            for k, peer in enumerate(far)
+        ]
+        own_rows = pl.ds(pl.multiple_of(me * depth, depth), depth)
+        swaps = []
+        for k, peer in enumerate(near):
+            swaps.append([])
+            for i, ref in enumerate(sources):
+                spot = pl.ds(pl.multiple_of(half * width + spots[i], 128), widths[i])
+                swaps[k].append(
+                    remote(
+                        columns(ref, i, peer["ctx"]),
+                        weight_ref.at[own_rows, spot],
+                        swap_send.at[k, i],
+                        swap_recv.at[k, i],
+                        peer,
+                    )
+                )
+        chain = Chain(rank, count, block_ref, rows_ref, chain_send, chain_recv)
+        chain.start(0)
+        gains_ref[me] = gain_ref[...]
+        marks_ref[rank] = mark_ref[...]
+        for take in takes:
+            take.wait()
+        keep = pltpu.make_async_copy(held, view(rank)(half, pair, 0, depth), local_sem.at[3])
+        keep.start()
+        relays = [Relay(here, held, view(rank), depth, relay_send.at[0], relay_recv.at[0])]
+        relays[0].first()
+        for k in range(1, count):
+            owner = lax.rem(rank - k + count, count)
+            for swap in swaps[k - 1]:
+                swap.wait_recv()
+            at = view(owner)
+            relays.append(
+                Relay(here, at(half, pair, 0, depth), at, depth, relay_send.at[k], relay_recv.at[k])
+            )
+            relays[k].first()
+            relays[k - 1].second()
+            if k > 1:
+                relays[k - 2].third()
+            if k < count - 1:
+                chain.start(k)
+        relays[-1].second()
+        relays[-2].third()
+        relays[-1].third()
+        for relay in relays:
+            relay.last()
+        keep.wait()
+        chain.finish()
+        for swap in swaps:
+            for copy in swap:
+                copy.wait_send()
+        for copy in small:
+            copy.wait()
+
+    return pl.pallas_call(
+        kernel,
+        out_shape=(
+            jax.ShapeDtypeStruct((owners, *TILE), F32),
+            jax.ShapeDtypeStruct((count, *TILE), jnp.int32),
+            jax.ShapeDtypeStruct((count, rows, block.shape[1]), block.dtype),
+            jax.ShapeDtypeStruct((owners * depth, 2 * width), w_query.dtype),
+        ),
+        in_specs=[ON_CHIP] * 2 + [ANYWHERE] * 4,
+        out_specs=(ON_CHIP, ON_CHIP, ANYWHERE, ANYWHERE),
+        scratch_shapes=[
+            pltpu.VMEM((depth, width), w_query.dtype),
+            SEMS((owners - 1,)),
+            SEMS((owners - 1,)),
+            SEMS((count - 1,)),
+            SEMS((count - 1,)),
+            SEMS((count - 1, 3)),
+            SEMS((count - 1, 3)),
+            SEMS((2, count - 1)),
+            SEMS((2, count - 1)),
+            SEMS((count, Relay.KINDS)),
+            SEMS((count, Relay.KINDS)),
+            SEMS((4,)),
+        ],
+        compiler_params=pltpu.CompilerParams(collective_id=0, has_side_effects=True),
+        name="enter",
+    )(gains, marks, block, w_query, w_key, w_value)
+
+
+def spread_mlp(first, second, pieces):
+    count, pairs = lax.axis_size("ctx"), lax.axis_size("dp")
+    kinds, depth, width = pieces[0].shape
+    rows, features = first.shape
+
+    def kernel(first_ref, second_ref, *rest):
+        piece_refs, rest = rest[:count], rest[count:]
+        firsts_ref, seconds_ref = rest[:2]
+        weight_refs, rest = rest[2 : 2 + kinds], rest[2 + kinds :]
+        held, chain_send, chain_recv, relay_send, relay_recv, take_sem, keep_sem = rest
+        here = place()
+        rank, pair, half = here["rank"], here["pair"], here["half"]
+        greet(
+            [{"ctx": lax.rem(rank + k, count)} for k in range(1, count)]
+            + [{"dp": here["sibling"]}, {"dp": here["across"]}, {"tensor": here["twin"]}]
+        )
+        takes = []
+        for i in range(kinds):
+            for d, ref in enumerate(piece_refs):
+                owner = lax.rem(rank - d + count, count)
+                take = pltpu.make_async_copy(
+                    ref.at[i],
+                    held.at[i, pl.ds(pl.multiple_of(owner * depth, depth), depth)],
+                    take_sem.at[i, d],
+                )
+                take.start()
+                takes.append(take)
+        chains = [
+            Chain(rank, count, first_ref, firsts_ref, chain_send.at[0], chain_recv.at[0]),
+            Chain(rank, count, second_ref, seconds_ref, chain_send.at[1], chain_recv.at[1]),
+        ]
+        chains[0].start(0)
+        block = count * depth
+
+        def view(i):
+            def at(t, p, start, size):
+                first = pl.multiple_of(p * block + start, 64)
+                return weight_refs[i].at[
+                    pl.ds(first, size), pl.ds(pl.multiple_of(t * width, 128), width)
+                ]
+
+            return at
+
+        relays, keeps = [], []
+        for i in range(kinds):
+            for take in takes[i * count : (i + 1) * count]:
+                take.wait()
+            keeps.append(
+                pltpu.make_async_copy(held.at[i], view(i)(half, pair, 0, block), keep_sem.at[i])
+            )
+            keeps[i].start()
+            relays.append(
+                Relay(here, held.at[i], view(i), block, relay_send.at[i], relay_recv.at[i])
+            )
+            relays[i].first()
+        chains[0].start(1)
+        relays[0].second()
+        chains[0].start(2)
+        chains[1].start(0)
+        relays[0].third()
+        relays[1].second()
+        chains[1].start(1)
+        relays[1].third()
+        relays[2].second()
+        chains[1].start(2)
+        relays[2].third()
+        for relay in relays:
+            relay.last()
+        for keep in keeps:
+            keep.wait()
+        for chain in chains:
+            chain.finish()
+
+    return pl.pallas_call(
+        kernel,
+        out_shape=(
+            jax.ShapeDtypeStruct((count, rows, features), first.dtype),
+            jax.ShapeDtypeStruct((count, rows, features), second.dtype),
+        )
+        + (jax.ShapeDtypeStruct((pairs * count * depth, 2 * width), pieces[0].dtype),) * kinds,
+        in_specs=[ANYWHERE] * (2 + count),
+        out_specs=(ANYWHERE,) * (2 + kinds),
+        scratch_shapes=[
+            pltpu.VMEM((kinds, count * depth, width), pieces[0].dtype),
+            SEMS((2, 2, count - 1)),
+            SEMS((2, 2, count - 1)),
+            SEMS((kinds, Relay.KINDS)),
+            SEMS((kinds, Relay.KINDS)),
+            SEMS((kinds, count)),
+            SEMS((kinds,)),
+        ],
+        compiler_params=pltpu.CompilerParams(
+            collective_id=2, has_side_effects=True, vmem_limit_bytes=16 * 1024 * 1024
+        ),
+        name="spread_mlp",
+    )(first, second, *pieces)
+
+
+def swap_ctx(blocks, collective_id):
+    count = lax.axis_size("ctx")
+
+    def kernel(blocks_ref, got_ref, held, send_sem, recv_sem, local_sem):
+        rank = lax.axis_index("ctx")
+        peers = [lax.rem(rank + k, count) for k in range(1, count)]
+        greet([{"ctx": peer} for peer in peers])
+        copies = [
+            remote(
+                blocks_ref.at[peer], got_ref.at[rank], send_sem.at[k], recv_sem.at[k], {"ctx": peer}
+            )
+            for k, peer in enumerate(peers)
+        ]
+        take = pltpu.make_async_copy(blocks_ref.at[rank], held, local_sem.at[0])
+        take.start()
+        take.wait()
+        keep = pltpu.make_async_copy(held, got_ref.at[rank], local_sem.at[1])
+        keep.start()
+        keep.wait()
+        for copy in copies:
+            copy.wait()
+
+    return pl.pallas_call(
+        kernel,
+        out_shape=jax.ShapeDtypeStruct(blocks.shape, blocks.dtype),
+        in_specs=[ANYWHERE],
+        out_specs=ANYWHERE,
+        scratch_shapes=[
+            pltpu.VMEM(blocks.shape[1:], blocks.dtype),
+            SEMS((count - 1,)),
+            SEMS((count - 1,)),
+            SEMS((2,)),
+        ],
+        compiler_params=pltpu.CompilerParams(collective_id=collective_id, has_side_effects=True),
+        name=f"swap_ctx_{collective_id}",
+    )(blocks)
+
+
+def owner_sums(tiles):
+    count, pairs, tensors = lax.axis_size("ctx"), lax.axis_size("dp"), lax.axis_size("tensor")
+    total = count * pairs * tensors
+
+    def kernel(tiles_ref, sum_ref, got, send_sem, recv_sem):
+        owner = lax.axis_index("dp") * count + lax.axis_index("ctx")
+        me = owner * tensors + lax.axis_index("tensor")
+        targets = [lax.rem(me + k, total) for k in range(1, total)]
+        peers = [
+            {
+                "dp": lax.div(t, count * tensors),
+                "ctx": lax.rem(lax.div(t, tensors), count),
+                "tensor": lax.rem(t, tensors),
+            }
+            for t in targets
+        ]
+        greet(peers)
+        copies = [
+            remote(
+                tiles_ref.at[lax.div(t, tensors)], got.at[me], send_sem.at[k], recv_sem.at[k], peer
+            )
+            for k, (t, peer) in enumerate(zip(targets, peers))
+        ]
+        got[me] = tiles_ref[owner]
+        for copy in copies:
+            copy.wait()
+        value = got[0]
+        for source in range(1, total):
+            value = value + got[source]
+        sum_ref[...] = value
+
+    return pl.pallas_call(
+        kernel,
+        out_shape=jax.ShapeDtypeStruct(TILE, F32),
+        in_specs=[pl.BlockSpec(memory_space=pltpu.VMEM)],
+        out_specs=pl.BlockSpec(memory_space=pltpu.VMEM),
+        scratch_shapes=[
+            pltpu.VMEM((total, *TILE), F32),
+            pltpu.SemaphoreType.DMA((total - 1,)),
+            pltpu.SemaphoreType.DMA((total - 1,)),
+        ],
+        compiler_params=pltpu.CompilerParams(collective_id=1, has_side_effects=True),
+        name="owner_sums",
+    )(tiles)
+
+
+def weight_partial(rows_side, columns_side):
+    tensors = lax.axis_size("tensor")
+    cols = columns_side.shape[1] // tensors
+    return jnp.stack(
+        [
+            jnp.dot(
+                rows_side.T, columns_side[:, t * cols : (t + 1) * cols], preferred_element_type=F32
+            ).astype(BF16)
+            for t in range(tensors)
+        ]
+    )
+
+
+def shards_of(partial):
+    count = lax.axis_size("ctx")
+    width = partial.shape[2]
+    flat = partial.astype(BF16).reshape(-1, width)
+    mine = lax.psum_scatter(flat, ("tensor", "dp"), scatter_dimension=0, tiled=True)
+    got = swap_by_target(mine.reshape(count, mine.shape[0] // count, width))
+    return got.transpose(1, 0, 2).reshape(got.shape[1], count * width).astype(F32)
+
+
+def with_twin(own):
+    other = shift(own, "tensor", 1)
+    first = lax.axis_index("tensor") == 0
+    return jnp.concatenate([jnp.where(first, own, other), jnp.where(first, other, own)])
+
+
+def on_device_sliced(
+    inputs,
+    segment_ids,
+    positions,
+    out_grad,
+    attn_gain,
+    w_query,
+    w_key,
+    w_value,
+    q_gain,
+    k_gain,
+    w_out,
+    mlp_gain,
+    w_gate,
+    w_up,
+    w_down,
+):
+    _, tok_count, width = inputs.shape
+    count = lax.axis_size("ctx")
+    tensors = lax.axis_size("tensor")
+    rank = lax.axis_index("ctx")
+    half = lax.axis_index("tensor")
+    own_rows = tok_count // tensors
+    rows = own_rows * count
+    head_rows = w_out.shape[0]
+    score_scale = 1.0 / math.sqrt(HEAD_DIM)
+
+    q_cols = w_query.shape[1] // count
+    k_cols = w_key.shape[1] // count
+    local_kv = k_cols // HEAD_DIM
+    kv_heads = tensors * local_kv
+    group = q_cols // k_cols
+    in_width = q_cols + 2 * k_cols
+    piece = attn_gain.shape[0]
+    small = q_gain.shape[0]
+
+    input_own = lax.dynamic_slice_in_dim(inputs[0], half * own_rows, own_rows, 0)
+    grad_own = lax.dynamic_slice_in_dim(out_grad[0], half * own_rows, own_rows, 0)
+    own_gains = jnp.concatenate([attn_gain, mlp_gain, q_gain, k_gain]).astype(F32)
+    own_marks = jnp.concatenate([segment_ids[0], positions[0]])
+    gains, marks, input_all, in_weight = enter(
+        to_tile(own_gains), to_tile(own_marks), input_own, w_query, w_key, w_value
+    )
+    out_weight = lax.all_gather(w_out.T, ("tensor", "dp", "ctx"), axis=0, tiled=True).reshape(
+        tensors, width, head_rows
+    )
+    gains = gains.reshape(gains.shape[0], -1)
+    attn_scale = gains[:, :piece].reshape(-1)
+    mlp_scale = gains[:, piece : 2 * piece].reshape(-1)
+    query_scale = gains[:, 2 * piece : 2 * piece + small].reshape(-1)
+    key_scale = gains[:, 2 * piece + small : 2 * (piece + small)].reshape(-1)
+
+    mlp_shards = jnp.stack([w_gate, w_up, w_down.T]).reshape(3, -1, count, w_gate.shape[1] // count)
+    mlp_shards, in_weight = lax.optimization_barrier((mlp_shards, in_weight))
+    mlp_pieces = [
+        shift(
+            lax.dynamic_index_in_dim(mlp_shards, (rank + d) % count, 2, keepdims=False), "ctx", d
+        )
+        if d
+        else lax.dynamic_index_in_dim(mlp_shards, rank, 2, keepdims=False)
+        for d in range(count)
+    ]
+
+    marks = marks.reshape(count, -1)[:, : 2 * tok_count].reshape(count, 2, tensors, own_rows)
+    offsets = jnp.arange(count)[:, None] * tok_count + jnp.arange(own_rows)[None, :]
+
+    def marks_of(which):
+        segs = lax.dynamic_index_in_dim(marks[:, 0], which, 1, keepdims=False).reshape(rows)
+        return segs, (offsets + which * own_rows).reshape(rows)
+
+    own_segs, own_index = marks_of(half)
+    twin_segs, twin_index = marks_of(1 - half)
+    own_positions = lax.dynamic_index_in_dim(marks[:, 1], half, 1, keepdims=False).reshape(rows)
+
+    def allowed_of(key_segs, key_index):
+        return (key_index[None, :] <= own_index[:, None]) & (key_segs[None, :] == own_segs[:, None])
+
+    allowed = (allowed_of(own_segs, own_index), allowed_of(twin_segs, twin_index))
+
+    stream = input_own.astype(F32)
+    input_all = lax.dynamic_update_index_in_dim(input_all, input_own, rank, 0)
+    normed_low = rms_norm(input_all.reshape(rows, width).astype(F32), attn_scale).astype(BF16)
+    _, attn_norm_pullback = jax.vjp(rms_norm, stream, attn_scale)
+    raw = jnp.dot(normed_low, in_weight, preferred_element_type=F32)
+    raw = raw.reshape(rows, tensors, in_width)
+    query_raw = raw[..., :q_cols].reshape(rows, kv_heads * group, HEAD_DIM)
+    key_raw = raw[..., q_cols : q_cols + k_cols].reshape(rows, kv_heads, HEAD_DIM)
+    value_low = raw[..., q_cols + k_cols :].astype(BF16).reshape(rows, kv_heads, HEAD_DIM)
+    cosine_table, sine_table = rope_tables(own_positions, HEAD_DIM)
+    cosine_table = cosine_table[:, None, :]
+    sine_table = sine_table[:, None, :]
+
+    def norm_rope(raw_heads, gain_vector):
+        return head_norm(raw_heads, gain_vector, cosine_table, sine_table)
+
+    key_rot, key_pullback = jax.vjp(norm_rope, key_raw, key_scale)
+    key_low = key_rot.astype(BF16)
+    kv_own = jnp.stack([key_low, value_low])
+    kv_twin = shift(kv_own, "tensor", 1)
+    query_rot, query_pullback = jax.vjp(norm_rope, query_raw, query_scale)
+    query_low = query_rot.astype(BF16).reshape(rows, kv_heads, group, HEAD_DIM)
+    keys = (kv_own[0], kv_twin[0])
+    values = (kv_own[1], kv_twin[1])
+
+    scores = [
+        jnp.where(ok, dot32(query_low, key, "mkgd,nkd->kgmn") * score_scale, masked_value)
+        for ok, key in zip(allowed, keys)
+    ]
+    best = jnp.maximum(*[jnp.max(s, axis=-1, keepdims=True) for s in scores])
+    weights = [jnp.where(ok, jnp.exp(s - best), 0.0) for ok, s in zip(allowed, scores)]
+    total = sum(jnp.sum(w, axis=-1, keepdims=True) for w in weights)
+    prob = [w / total for w in weights]
+    prob_low = [p.astype(BF16) for p in prob]
+    attended = sum(dot32(p, v, "kgmn,nkd->mkgd") for p, v in zip(prob_low, values))
+    attended_low = attended.astype(BF16).reshape(rows, tensors * q_cols)
+    attended_own = swap_ctx(attended_low.reshape(count, own_rows, tensors * q_cols), 3)
+    attended_own = attended_own.reshape(count, own_rows, tensors, q_cols)
+    attended_own = attended_own.transpose(1, 2, 0, 3).reshape(own_rows, tensors, head_rows)
+    middle = stream + dot32(attended_own, out_weight, "mtr,tkr->mk")
+    normed_mid, mlp_norm_pullback = jax.vjp(rms_norm, middle, mlp_scale)
+    mid_own = normed_mid.astype(BF16)
+    mid_low, grad_low, gate_weight, up_weight, down_weight = spread_mlp(
+        mid_own, grad_own, mlp_pieces
+    )
+    mid_low = lax.dynamic_update_index_in_dim(mid_low, mid_own, rank, 0).reshape(rows, width)
+    grad_low = lax.dynamic_update_index_in_dim(grad_low, grad_own, rank, 0).reshape(rows, width)
+
+    gate = jnp.dot(mid_low, gate_weight, preferred_element_type=F32)
+    upward = jnp.dot(mid_low, up_weight, preferred_element_type=F32)
+    hidden, silu_pullback = jax.vjp(silu_product, gate, upward)
+    hidden_low = hidden.astype(BF16)
+    hidden_grad = jnp.dot(grad_low, down_weight, preferred_element_type=F32)
+    gate_grad, upward_grad = silu_pullback(hidden_grad)
+    gate_grad_low = gate_grad.astype(BF16)
+    upward_grad_low = upward_grad.astype(BF16)
+    mid_grad_part = jnp.dot(gate_grad_low, gate_weight.T, preferred_element_type=F32) + jnp.dot(
+        upward_grad_low, up_weight.T, preferred_element_type=F32
+    )
+    mid_grad = scatter_sum(mid_grad_part.astype(BF16).reshape(count, own_rows, width))
+    mlp_grads = [
+        weight_partial(mid_low, gate_grad_low),
+        weight_partial(mid_low, upward_grad_low),
+        weight_partial(grad_low, hidden_low),
+    ]
+    down_part = jnp.dot(hidden_low, down_weight.T, preferred_element_type=F32).astype(BF16)
+    mid_grad, down_part, mlp_grads = lax.optimization_barrier((mid_grad, down_part, mlp_grads))
+    gate_weight_grad, up_weight_grad, down_weight_grad = [shards_of(g) for g in mlp_grads]
+    down_weight_grad = down_weight_grad.T
+
+    middle_norm_grad, mlp_gain_grad = mlp_norm_pullback(mid_grad)
+    middle_grad = grad_own.astype(F32) + middle_norm_grad
+    branch_grad = middle_grad.astype(BF16)
+    attended_grad = dot32(branch_grad, out_weight, "mk,tkr->mtr").astype(BF16)
+    attended_grad = attended_grad.reshape(own_rows, tensors, count, q_cols).transpose(2, 0, 1, 3)
+    attended_grad = swap_ctx(attended_grad.reshape(count, own_rows, tensors * q_cols), 4)
+    branch_grad, down_part, attended_grad = lax.optimization_barrier(
+        (branch_grad, down_part, attended_grad)
+    )
+    down_sum = scatter_sum(down_part.reshape(count, own_rows, width))
+    output = with_twin((middle + down_sum).astype(BF16))[None]
+    branch_all = gather_ctx(branch_grad).reshape(rows, width)
+    out_weight_grad = shards_of(weight_partial(branch_all, attended_low)).T
+    attended_grad = attended_grad.reshape(rows, kv_heads, group, HEAD_DIM)
+    prob_grad = [dot32(attended_grad, v, "mkgd,nkd->kgmn") for v in values]
+    delta = sum(jnp.sum(p * g, axis=-1, keepdims=True) for p, g in zip(prob, prob_grad))
+    score_grad = [(p * (g - delta)).astype(BF16) for p, g in zip(prob, prob_grad)]
+
+    def key_side(i):
+        return jnp.stack(
+            [
+                dot32(score_grad[i], query_low, "kgmn,mkgd->nkd"),
+                dot32(prob_low[i], attended_grad, "kgmn,mkgd->nkd"),
+            ]
+        )
+
+    kv_back = shift(key_side(1).astype(BF16), "tensor", 1)
+    kv_grad = key_side(0) + kv_back.astype(F32)
+    query_grad = sum(dot32(g, k, "kgmn,nkd->mkgd") for g, k in zip(score_grad, keys)) * score_scale
+    query_raw_grad, query_gain_grad = query_pullback(query_grad.reshape(query_raw.shape))
+    key_raw_grad, key_gain_grad = key_pullback(kv_grad[0] * score_scale)
+    raw_grad_low = jnp.concatenate(
+        [
+            query_raw_grad.astype(BF16).reshape(rows, tensors, q_cols),
+            key_raw_grad.astype(BF16).reshape(rows, tensors, k_cols),
+            kv_grad[1].astype(BF16).reshape(rows, tensors, k_cols),
+        ],
+        axis=2,
+    ).reshape(rows, tensors * in_width)
+    normed_grad_part = jnp.dot(raw_grad_low, in_weight.T, preferred_element_type=F32)
+    normed_grad = scatter_sum(normed_grad_part.astype(BF16).reshape(count, own_rows, width))
+    in_weight_grad = shards_of(weight_partial(normed_low, raw_grad_low))
     in_weight_grad = in_weight_grad.reshape(-1, count, in_width)
     query_weight_grad = in_weight_grad[..., :q_cols].reshape(w_query.shape)
     key_weight_grad = in_weight_grad[..., q_cols : q_cols + k_cols].reshape(w_key.shape)

time: 924 us -> 832 us (0.900)
  waiting for transfers between devices: 426 us -> 247 us
  Pallas kernels: 66.5 us -> 238 us
  starting transfers between devices: 132 us -> 75.6 us
  matrix products: 118 us -> 93.5 us
    pallas_call x1 -> x4, Pallas kernels: 48.8 us -> 216 us  [the longest x1 99.7 us: enter(): pl.pallas_call(kernel, out_shape=(jax.ShapeDtypeStruct((owners, *TILE), F...]
    ppermute x58 -> x34, waiting for transfers between devices: 312 us -> 145 us  [shift(): return lax.ppermute(value, axis, pairs)]
    dot_general x20 -> x14, matrix products: 109 us -> 34.7 us  [dot32(): return jnp.einsum(spec, left, right, preferred_element_type=F32)]
    dot_general x0 -> x18, matrix products: none -> 58.7 us  [the longest x10 20.5 us: weight_partial(): jnp.dot(rows_side.T, columns_side[:, t * cols:(t + 1) * cols], preferred_...]
    ppermute x58 -> x34, starting transfers between devices: 131 us -> 74.9 us  [shift(): return lax.ppermute(value, axis, pairs)]
    convert_element_type x6 -> x0, local copies, waits for them, and re-layouts: 36.3 us -> none  [the longest x5 36.1 us: shards_of(): flat = partial.astype(BF16).reshape(-1, width)]
    concatenate x15 -> x1, other arithmetic: 12.2 us -> 0.07 us  [on_device_sliced(): jnp.concatenate([query_raw_grad.astype(BF16).reshape(rows, tensors, q_col...]
    all_gather x4 -> x0, waiting for transfers between devices: 10.8 us -> none  [slices_of(): full = lax.all_gather(mine, ('tensor', 'dp'), axis=0, tiled=True)]
  transfers between devices with their start and end apart: 68 -> 40, of which waited for: 35 -> 17; matrix products, arithmetic and copies ran while one was open for 24% -> 20% of each run, Pallas kernels for 7% -> 16%
where the time goes in v3:
time: 832 us; the launch traced here: 824 us
  waiting for transfers between devices  247 us (30%)
  Pallas kernels  238 us (29%)
  local copies, waits for them, and re-layouts  97.8 us (12%)
  matrix products  93.5 us (11%)
  starting transfers between devices  75.6 us (9%)
  other arithmetic  55.8 us (7%)
  between operations  16.2 us (2%)
    ppermute x34, waiting for transfers between devices, shift(): return lax.ppermute(value, axis, pairs)  145 us
    pallas_call x1, Pallas kernels, enter(): pl.pallas_call(kernel, out_shape=(jax.ShapeDtypeStruct((owners, *TILE), F...  99.7 us
    reduce_scatter x5, waiting for transfers between devices, shards_of(): lax.psum_scatter(flat, ('tensor', 'dp'), scatter_dimension=0, tiled=True)  99.7 us
    pallas_call x1, Pallas kernels, spread_mlp(): pl.pallas_call(kernel, out_shape=(jax.ShapeDtypeStruct((count, rows, feat...  89.7 us
    ppermute x34, starting transfers between devices, shift(): return lax.ppermute(value, axis, pairs)  74.9 us
    dot_general x14, matrix products, dot32(): return jnp.einsum(spec, left, right, preferred_element_type=F32)  34.7 us
    unnamed x221, local copies, waits for them, and re-layouts  30 us
    pallas_call x2, Pallas kernels, swap_ctx(): pl.pallas_call(kernel, out_shape=jax.ShapeDtypeStruct(blocks.shape, block...  26.6 us
  transfers between devices with their start and end apart: 40, of which 17 were waited for; matrix products, arithmetic and copies ran while one was open for 20% of the time, Pallas kernels for 16%

profile of v3, /device:TPU:0, one launch (start us, length us, event | category | flops | bytes accessed | tf_op | source)
XLA Modules:
  0.0 823.7 jit_solution(17354354299586307265)
XLA Ops:
  8.0 2.1 stack.153
  16.5 99.7 %enter.1 = (f32[16,8,128]{2,1,0:T(8,128)}, s32[4,8,128]{2,1,0:T(8,128)}, bf16[4,128,2048]{2,1,0:T(8,128)(2,1)}, bf16[2048,1024]{1,0:T(8,128)(2,1)}) custom-call(f32[8,128]{1,0:T(8,128)} %fusion.88.gain_ref, s32[8,128]{1,0:T(8,128)} %pad_bitcast_fusion.mark_ref, bf16[128,2048]{1,0:T(8,128)(2,1)} %get-tuple-element.78.block_ref, bf16[128,1024]{1,0:T(8,128)(2,1)} %wq_ref.1, ...), custom_call_target="tpu_custom_call" | custom-call | tf_op jit(solution)/shard_map/enter/pallas_call | solution.py:1167
  119.4 9.5 %collective-permute-start.3 = (bf16[3,128,768]{2,1,0:T(8,128)(2,1)}, bf16[3,128,768]{2,1,0:T(8,128)(2,1)S(1)}, u32[]{:S(2)}, u32[]{:S(2)}) collective-permute-start(bf16[3,128,768]{2,1,0:T(8,128)(2,1)} %get-tuple-element.82), channel_id=1, source_target_pairs={{0,6},{2,0},{4,2},{6,4},{1,7},{3,1},{5,3},{7,5},{8,14},{10,8},{12,... | collective-permute-start | bytes 1769480 | tf_op jit(solution)/shard_map/ppermute | solution.py:886
  130.9 6.6 copy.171
  139.0 2.2 multiply_reduce_fusion
  142.5 2.4 fusion.106
  152.5 2.0 copy.107
  161.7 2.3 fusion.1
  166.0 2.3 fusion.23
  168.4 2.6 fusion.54
  171.0 3.4 fusion.30
  176.7 13.8 %swap_ctx_3.1 = bf16[4,128,512]{2,1,0:T(8,128)(2,1)} custom-call(bf16[4,128,512]{2,1,0:T(8,128)(2,1)} %copy.176.blocks_ref), custom_call_target="tpu_custom_call" | custom-call | tf_op jit(solution)/shard_map/swap_ctx_3/pallas_call | solution.py:1316
  192.9 2.2 reshape.489
  195.2 12.0 %copy.115 = bf16[4096,1024]{1,0:T(8,128)(2,1)} copy(bf16[4096,1024]{0,1:T(8,128)(2,1)} %all-gather.2.cloned.1.call-done) | data formatting | bytes 16777216 | tf_op jit(solution)/shard_map/all_gather | solution.py:1449
  207.2 6.6 multiply_reduce_fusion.5
  214.0 89.7 %spread_mlp.1 = (bf16[4,128,2048]{2,1,0:T(8,128)(2,1)S(1)}, bf16[4,128,2048]{2,1,0:T(8,128)(2,1)S(1)}, bf16[2048,1536]{1,0:T(8,128)(2,1)S(1)}, bf16[2048,1536]{1,0:T(8,128)(2,1)S(1)}, bf16[2048,1536]{1,0:T(8,128)(2,1)S(1)}) custom-call(bf16[128,2048]{1,0:T(8,128)(2,1)S(1)} %multiply_convert_fusion.3.first_ref, ...), custom_call_target="tpu_custom_call" | custom-call | tf_op jit(solution)/shard_map/spread_mlp/pallas_call | solution.py:1269
  304.0 3.4 fusion.107
  307.4 5.2 fusion.108
  312.6 7.5 multiply_convert_fusion.1
  320.1 4.7 convolution_convert_fusion.9
  330.4 3.6 fusion.14
  334.0 5.1 fusion.109
  339.1 3.6 fusion.17
  342.7 3.5 fusion.16
  346.2 5.3 add_convert_fusion
  352.8 3.8 collective-permute-start.6
  356.6 3.2 pad_maximum_fusion.2
  359.8 3.7 pad_maximum_fusion
  364.9 3.6 pad_maximum_fusion.1
  369.7 7.0 collective-permute-done.6
  376.7 22.7 %collective-permute-done.5 = bf16[128,2048]{1,0:T(8,128)(2,1)} collective-permute-done((bf16[128,2048]{1,0:T(8,128)(2,1)S(1)}, bf16[128,2048]{1,0:T(8,128)(2,1)}, u32[]{:S(2)}, u32[]{:S(2)}) %collective-permute-start.5) | collective-permute-done | bytes 524320 | tf_op jit(solution)/shard_map/ppermute | solution.py:886
  403.4 2.4 convolution_convert_fusion.12
  407.8 12.7 %swap_ctx_4.1 = bf16[4,128,512]{2,1,0:T(8,128)(2,1)} custom-call(bf16[4,128,512]{2,1,0:T(8,128)(2,1)} %reshape.495.blocks_ref), custom_call_target="tpu_custom_call" | custom-call | tf_op jit(solution)/shard_map/swap_ctx_4/pallas_call | solution.py:1316
  422.7 3.8 fusion.33
  426.6 2.3 convolution_bitcast_fusion.3
  428.9 2.4 collective-permute-start.21
  435.5 4.3 fusion.2
  439.8 2.9 fusion.4
  449.3 15.3 %collective-permute-done.19 = bf16[128,2048]{1,0:T(8,128)(2,1)S(1)} collective-permute-done((bf16[128,2048]{1,0:T(8,128)(2,1)}, bf16[128,2048]{1,0:T(8,128)(2,1)S(1)}, u32[]{:S(2)}, u32[]{:S(2)}) %collective-permute-start.19) | collective-permute-done | bytes 524320 | tf_op jit(solution)/shard_map/ppermute | solution.py:886
  480.5 2.4 pad_maximum_fusion.3
  484.7 4.7 convolution_convert_fusion.6
  492.0 11.6 %collective-permute-start.12 = (bf16[128,2048]{1,0:T(8,128)(2,1)}, bf16[128,2048]{1,0:T(8,128)(2,1)}, u32[]{:S(2)}, u32[]{:S(2)}) collective-permute-start(bf16[128,2048]{1,0:T(8,128)(2,1)} %get-tuple-element.86), channel_id=1, source_target_pairs={{0,2},{2,4},{4,6},{6,0},{1,3},{3,5},{5,7},{7,1},{8,10},{10,12},{12... | collective-permute-start | bytes 1572872 | tf_op jit(solution)/shard_map/ppermute | solution.py:886
  505.7 2.7 dynamic-slice_bitcast_fusion.9
  508.5 2.0 collective-permute-start.7
  512.5 5.8 collective-permute-done.12
  518.3 12.6 %collective-permute-start.8 = (bf16[128,2048]{1,0:T(8,128)(2,1)}, bf16[128,2048]{1,0:T(8,128)(2,1)S(1)}, u32[]{:S(2)}, u32[]{:S(2)}) collective-permute-start(bf16[128,2048]{1,0:T(8,128)(2,1)} %get-tuple-element.91), channel_id=1, source_target_pairs={{0,4},{2,6},{4,0},{6,2},{1,5},{3,7},{5,1},{7,3},{8,12},{10,14},{12... | collective-permute-start | bytes 1572872 | tf_op jit(solution)/shard_map/ppermute | solution.py:886
  530.9 32.4 %collective-permute-done.13 = bf16[128,2048]{1,0:T(8,128)(2,1)} collective-permute-done((bf16[128,2048]{1,0:T(8,128)(2,1)}, bf16[128,2048]{1,0:T(8,128)(2,1)}, u32[]{:S(2)}, u32[]{:S(2)}) %collective-permute-start.13) | collective-permute-done | bytes 524320 | tf_op jit(solution)/shard_map/ppermute | solution.py:886
  563.3 2.1 fusion.42
  565.4 29.2 %collective-permute-done.8 = bf16[128,2048]{1,0:T(8,128)(2,1)S(1)} collective-permute-done((bf16[128,2048]{1,0:T(8,128)(2,1)}, bf16[128,2048]{1,0:T(8,128)(2,1)S(1)}, u32[]{:S(2)}, u32[]{:S(2)}) %collective-permute-start.8) | collective-permute-done | bytes 524320 | tf_op jit(solution)/shard_map/ppermute | solution.py:886
  594.7 3.2 fusion.38
  599.8 21.8 %owner_sums.1 = f32[8,128]{1,0:T(8,128)} custom-call(f32[16,8,128]{2,1,0:T(8,128)} %bitcast.529), custom_call_target="tpu_custom_call" | custom-call | tf_op jit(solution)/shard_map/owner_sums/pallas_call | solution.py:1363
  621.6 2.2 collective-permute-start.10
  628.5 12.9 %collective-permute-done.10 = bf16[128,2048]{1,0:T(8,128)(2,1)S(1)} collective-permute-done((bf16[128,2048]{1,0:T(8,128)(2,1)S(1)}, bf16[128,2048]{1,0:T(8,128)(2,1)S(1)}, u32[]{:S(2)}, u32[]{:S(2)}) %collective-permute-start.10) | collective-permute-done | bytes 524320 | tf_op jit(solution)/shard_map/ppermute | solution.py:886
  644.0 2.0 collective-permute-start.22
  648.5 4.5 collective-permute-done.23
  659.7 8.1 collective-permute-done.17
  674.2 2.1 collective-permute-start.31
  676.9 41.3 %reduce-scatter.12.cloned.1.call-done = bf16[512,768]{1,0:T(8,128)(2,1)} async-done(((bf16[4096,768]{1,0:T(8,128)(2,1)}), bf16[512,768]{1,0:T(8,128)(2,1)}) %reduce-scatter.12.cloned.1.call-update) | async-done | bytes 786448 | tf_op jit(solution)/shard_map/reduce_scatter | solution.py:1395
  718.2 2.0 dynamic-slice_bitcast_fusion.15
  721.7 2.4 collective-permute-start.29
  724.8 58.4 %reduce-scatter.10.cloned.1.call-done = bf16[512,768]{1,0:T(8,128)(2,1)} async-done(((bf16[4096,768]{1,0:T(8,128)(2,1)}), bf16[512,768]{1,0:T(8,128)(2,1)}) %reduce-scatter.10.cloned.1.call-update) | async-done | bytes 786448 | tf_op jit(solution)/shard_map/reduce_scatter | solution.py:1395
  783.2 2.1 dynamic-slice_bitcast_fusion.18
  785.3 3.3 collective-permute-start.28
  794.2 4.2 collective-permute-start.25
  (414 shorter events, 139.9 us)
Async XLA Ops:
  7.2 188.0 %all-gather.2.cloned.1.call-start = ((), (), s32[]{:S(2)}) async-start(), calls=%async_computation.5 | async-start | bytes 8650752 | tf_op jit(solution)/shard_map/all_gather | solution.py:1449
  7.9 634.7 %reduce-scatter.8.cloned.1.call-start = ((), (), s32[]{:S(2)}) async-start(), calls=%async_computation.7 | async-start | bytes 2359296 | tf_op jit(solution)/shard_map/reduce_scatter | solution.py:1395
  118.1 11.5 %copy-start.61 = (f32[16,8,128]{2,1,0:T(8,128)S(1)}, f32[16,8,128]{2,1,0:T(8,128)}, u32[]{:S(2)}) copy-start(f32[16,8,128]{2,1,0:T(8,128)} %get-tuple-element.33) | copy-start | bytes 196612
  118.2 11.5 %copy-start.64 = (s32[4,8,128]{2,1,0:T(8,128)S(1)}, s32[4,8,128]{2,1,0:T(8,128)}, u32[]{:S(2)}) copy-start(s32[4,8,128]{2,1,0:T(8,128)} %get-tuple-element.36) | copy-start | bytes 49156
  119.4 94.5 %collective-permute-start.3 = (bf16[3,128,768]{2,1,0:T(8,128)(2,1)}, bf16[3,128,768]{2,1,0:T(8,128)(2,1)S(1)}, u32[]{:S(2)}, u32[]{:S(2)}) collective-permute-start(bf16[3,128,768]{2,1,0:T(8,128)(2,1)} %get-tuple-element.82), channel_id=1, source_target_pairs={{0,6},{2,0},{4,2},{6,4},{1,7},{3,1},{5,3},{7,5},{8,14},{10,8},{12,... | collective-permute-start | bytes 1769480 | tf_op jit(solution)/shard_map/ppermute | solution.py:886
  128.9 85.0 %collective-permute-start.2 = (bf16[3,128,768]{2,1,0:T(8,128)(2,1)}, bf16[3,128,768]{2,1,0:T(8,128)(2,1)S(1)}, u32[]{:S(2)}, u32[]{:S(2)}) collective-permute-start(bf16[3,128,768]{2,1,0:T(8,128)(2,1)} %get-tuple-element.83), channel_id=1, source_target_pairs={{0,4},{2,6},{4,0},{6,2},{1,5},{3,7},{5,1},{7,3},{8,12},{10,14},{12... | collective-permute-start | bytes 1769480 | tf_op jit(solution)/shard_map/ppermute | solution.py:886
  128.9 85.0 %collective-permute-start.1 = (bf16[3,128,768]{2,1,0:T(8,128)(2,1)}, bf16[3,128,768]{2,1,0:T(8,128)(2,1)S(1)}, u32[]{:S(2)}, u32[]{:S(2)}) collective-permute-start(bf16[3,128,768]{2,1,0:T(8,128)(2,1)} %get-tuple-element.84), channel_id=1, source_target_pairs={{0,2},{2,4},{4,6},{6,0},{1,3},{3,5},{5,7},{7,1},{8,10},{10,12},{12... | collective-permute-start | bytes 1769480 | tf_op jit(solution)/shard_map/ppermute | solution.py:886
  141.8 19.9 %copy-start.53 = (f32[2048]{0:T(1024)}, f32[2048]{0:T(1024)S(1)}, u32[]{:S(2)}) copy-start(f32[2048]{0:T(1024)S(1)} %get-tuple-element.132) | copy-start | bytes 24580
  147.3 16.7 %collective-permute-start = (bf16[2,512,2,128]{1,3,2,0:T(8,128)(2,1)}, bf16[2,512,2,128]{1,3,2,0:T(8,128)(2,1)}, u32[]{:S(2)}, u32[]{:S(2)}) collective-permute-start(bf16[2,512,2,128]{1,3,2,0:T(8,128)(2,1)} %pad_maximum_fusion.8), channel_id=1, source_target_pairs={{0,1},{1,0},{2,3},{3,2},{4,5},{5,4},{6,7},{7,6},{8,9},{9,8},{10,11... | collective-permute-start | bytes 1572872 | tf_op jit(solution)/shard_map/ppermute | solution.py:886
  195.2 12.0 %copy-start.12 = (bf16[128,2048]{1,0:T(8,128)(2,1)S(1)}, bf16[128,2048]{1,0:T(8,128)(2,1)}, u32[]{:S(2)}) copy-start(bf16[128,2048]{1,0:T(8,128)(2,1)} %get-tuple-element.78.block_ref) | copy-start | bytes 1572868
  213.7 90.2 %copy-start.79 = (f32[128]{0:T(128)}, f32[128]{0:T(128)S(1)}, u32[]{:S(2)}) copy-start(f32[128]{0:T(128)S(1)} %get-tuple-element.157) | copy-start | bytes 1540
  213.7 187.9 %copy-start.2 = (f32[128,2048]{1,0:T(8,128)}, f32[128,2048]{1,0:T(8,128)S(1)}, u32[]{:S(2)}) copy-start(f32[128,2048]{1,0:T(8,128)S(1)} %get-tuple-element.158) | copy-start | bytes 3145732
  213.7 90.0 %copy-start.23 = (bf16[1,256,2048]{2,1,0:T(8,128)(2,1)S(1)}, bf16[1,256,2048]{2,1,0:T(8,128)(2,1)}, u32[]{:S(2)}) copy-start(bf16[1,256,2048]{2,1,0:T(8,128)(2,1)} %param.18) | copy-start | bytes 3145732
  213.8 90.2 %copy-start.65 = (f32[128]{0:T(128)}, f32[128]{0:T(128)S(1)}, u32[]{:S(2)}) copy-start(f32[128]{0:T(128)S(1)} %fusion.90) | copy-start | bytes 1540
  352.8 16.9 %collective-permute-start.4 = (bf16[128,2048]{1,0:T(8,128)(2,1)}, bf16[128,2048]{1,0:T(8,128)(2,1)}, u32[]{:S(2)}, u32[]{:S(2)}) collective-permute-start(bf16[128,2048]{1,0:T(8,128)(2,1)} %get-tuple-element.92), channel_id=1, source_target_pairs={{0,2},{2,4},{4,6},{6,0},{1,3},{3,5},{5,7},{7,1},{8,10},{10,12},{12... | collective-permute-start | bytes 1572872 | tf_op jit(solution)/shard_map/ppermute | solution.py:886
  352.8 23.9 %collective-permute-start.6 = (bf16[128,2048]{1,0:T(8,128)(2,1)}, bf16[128,2048]{1,0:T(8,128)(2,1)}, u32[]{:S(2)}, u32[]{:S(2)}) collective-permute-start(bf16[128,2048]{1,0:T(8,128)(2,1)} %get-tuple-element.93), channel_id=1, source_target_pairs={{0,6},{2,0},{4,2},{6,4},{1,7},{3,1},{5,3},{7,5},{8,14},{10,8},{12,... | collective-permute-start | bytes 1572872 | tf_op jit(solution)/shard_map/ppermute | solution.py:886
  356.6 42.8 %collective-permute-start.5 = (bf16[128,2048]{1,0:T(8,128)(2,1)S(1)}, bf16[128,2048]{1,0:T(8,128)(2,1)}, u32[]{:S(2)}, u32[]{:S(2)}) collective-permute-start(bf16[128,2048]{1,0:T(8,128)(2,1)S(1)} %get-tuple-element.94), channel_id=1, source_target_pairs={{0,4},{2,6},{4,0},{6,2},{1,5},{3,7},{5,1},{7,3},{8,12},{10,14},{12... | collective-permute-start | bytes 1572872 | tf_op jit(solution)/shard_map/ppermute | solution.py:886
  359.8 43.6 %slice-start = ((s8[8388608]{0:T(1024)(128)(4,1)}), s8[4194304]{0:T(1024)(128)(4,1)S(1)}, s32[]{:S(2)}) async-start(s8[8388608]{0:T(1024)(128)(4,1)} %bitcast.475), calls=%async_computation.11 | async-start | bytes 8388608
  364.9 38.5 %slice-start.1 = ((s8[8388608]{0:T(1024)(128)(4,1)}), s8[4194304]{0:T(1024)(128)(4,1)S(1)}, s32[]{:S(2)}) async-start(s8[8388608]{0:T(1024)(128)(4,1)} %bitcast.475), calls=%async_computation.12 | async-start | bytes 8388608
  368.6 32.7 %copy-start.66 = (f32[128]{0:T(128)S(1)}, f32[128]{0:T(128)}, u32[]{:S(2)}) copy-start(f32[128]{0:T(128)} %copy-done.65) | copy-start | bytes 1540
  368.6 33.1 %copy-start.80 = (f32[128]{0:T(128)S(1)}, f32[128]{0:T(128)}, u32[]{:S(2)}) copy-start(f32[128]{0:T(128)} %copy-done.79) | copy-start | bytes 1540
  368.6 33.7 %copy-start.24 = (bf16[1,256,2048]{2,1,0:T(8,128)(2,1)S(1)}, bf16[1,256,2048]{2,1,0:T(8,128)(2,1)}, u32[]{:S(2)}) copy-start(bf16[1,256,2048]{2,1,0:T(8,128)(2,1)} %param.18) | copy-start | bytes 3145732
  405.8 17.0 %copy-start.19 = (pred[512,512]{0,1:T(8,128)(4,1)S(1)}, pred[512,512]{0,1:T(8,128)(4,1)}, u32[]{:S(2)}) copy-start(pred[512,512]{0,1:T(8,128)(4,1)} %copy-done.18) | copy-start | bytes 786436
  428.9 36.6 %collective-permute-start.21 = (bf16[128,2048]{1,0:T(8,128)(2,1)}, bf16[128,2048]{1,0:T(8,128)(2,1)S(1)}, u32[]{:S(2)}, u32[]{:S(2)}) collective-permute-start(bf16[128,2048]{1,0:T(8,128)(2,1)} %fusion.96), channel_id=1, source_target_pairs={{0,2},{2,4},{4,6},{6,0},{1,3},{3,5},{5,7},{7,1},{8,10},{10,12},{12... | collective-permute-start | bytes 1572872 | tf_op jit(solution)/shard_map/ppermute | solution.py:886
  431.3 34.2 %collective-permute-start.20 = (bf16[128,2048]{1,0:T(8,128)(2,1)}, bf16[128,2048]{1,0:T(8,128)(2,1)S(1)}, u32[]{:S(2)}, u32[]{:S(2)}) collective-permute-start(bf16[128,2048]{1,0:T(8,128)(2,1)} %fusion.96), channel_id=1, source_target_pairs={{0,4},{2,6},{4,0},{6,2},{1,5},{3,7},{5,1},{7,3},{8,12},{10,14},{12... | collective-permute-start | bytes 1572872 | tf_op jit(solution)/shard_map/ppermute | solution.py:886
  432.7 31.9 %collective-permute-start.19 = (bf16[128,2048]{1,0:T(8,128)(2,1)}, bf16[128,2048]{1,0:T(8,128)(2,1)S(1)}, u32[]{:S(2)}, u32[]{:S(2)}) collective-permute-start(bf16[128,2048]{1,0:T(8,128)(2,1)} %fusion.96), channel_id=1, source_target_pairs={{0,6},{2,0},{4,2},{6,4},{1,7},{3,1},{5,3},{7,5},{8,14},{10,8},{12,... | collective-permute-start | bytes 1572872 | tf_op jit(solution)/shard_map/ppermute | solution.py:886
  445.7 19.8 %copy-start.20 = (f32[512,4,64]{0,2,1:T(8,128)}, f32[512,4,64]{0,2,1:T(8,128)S(1)}, u32[]{:S(2)}) copy-start(f32[512,4,64]{0,2,1:T(8,128)S(1)} %get-tuple-element.95) | copy-start | bytes 1572868
  445.7 19.8 %copy-start.21 = (f32[512,4,64]{0,2,1:T(8,128)}, f32[512,4,64]{0,2,1:T(8,128)S(1)}, u32[]{:S(2)}) copy-start(f32[512,4,64]{0,2,1:T(8,128)S(1)} %get-tuple-element.96) | copy-start | bytes 1572868
  448.2 26.6 %collective-permute-start.11 = (bf16[2,512,2,128]{1,3,2,0:T(8,128)(2,1)}, bf16[2,512,2,128]{1,3,2,0:T(8,128)(2,1)}, u32[]{:S(2)}, u32[]{:S(2)}) collective-permute-start(bf16[2,512,2,128]{1,3,2,0:T(8,128)(2,1)} %pad_maximum_fusion.9), channel_id=1, source_target_pairs={{0,1},{1,0},{2,3},{3,2},{4,5},{5,4},{6,7},{7,6},{8,9},{9,8},{10,11... | collective-permute-start | bytes 1572872 | tf_op jit(solution)/shard_map/ppermute | solution.py:886
  470.8 182.3 %reduce-scatter.6.cloned.1.call-start = ((), (), s32[]{:S(2)}) async-start(), calls=%async_computation.6 | async-start | bytes 4718592 | tf_op jit(solution)/shard_map/reduce_scatter | solution.py:1395
  483.0 189.2 %reduce-scatter.14.cloned.1.call-start = ((), (), s32[]{:S(2)}) async-start(), calls=%async_computation.10 | async-start | bytes 7077888 | tf_op jit(solution)/shard_map/reduce_scatter | solution.py:1395
  483.5 234.6 %reduce-scatter.12.cloned.1.call-start = ((), (), s32[]{:S(2)}) async-start(), calls=%async_computation.9 | async-start | bytes 7077888 | tf_op jit(solution)/shard_map/reduce_scatter | solution.py:1395
  484.1 299.1 %reduce-scatter.10.cloned.1.call-start = ((), (), s32[]{:S(2)}) async-start(), calls=%async_computation.8 | async-start | bytes 7077888 | tf_op jit(solution)/shard_map/reduce_scatter | solution.py:1395
  489.5 16.2 %copy-start.74 = (f32[128]{0:T(128)S(1)}, f32[128]{0:T(128)}, u32[]{:S(2)}) copy-start(f32[128]{0:T(128)} %get-tuple-element.77) | copy-start | bytes 1540
  490.8 72.5 %copy-start.13 = (bf16[128,2048]{1,0:T(8,128)(2,1)S(1)}, bf16[128,2048]{1,0:T(8,128)(2,1)}, u32[]{:S(2)}) copy-start(bf16[128,2048]{1,0:T(8,128)(2,1)} %get-tuple-element.78.block_ref) | copy-start | bytes 1572868
  490.8 72.5 %copy-start.54 = (f32[2048]{0:T(1024)S(1)}, f32[2048]{0:T(1024)}, u32[]{:S(2)}) copy-start(f32[2048]{0:T(1024)} %copy-done.53) | copy-start | bytes 24580
  492.0 26.3 %collective-permute-start.12 = (bf16[128,2048]{1,0:T(8,128)(2,1)}, bf16[128,2048]{1,0:T(8,128)(2,1)}, u32[]{:S(2)}, u32[]{:S(2)}) collective-permute-start(bf16[128,2048]{1,0:T(8,128)(2,1)} %get-tuple-element.86), channel_id=1, source_target_pairs={{0,2},{2,4},{4,6},{6,0},{1,3},{3,5},{5,7},{7,1},{8,10},{10,12},{12... | collective-permute-start | bytes 1572872 | tf_op jit(solution)/shard_map/ppermute | solution.py:886
  503.6 27.3 %collective-permute-start.14 = (bf16[128,2048]{1,0:T(8,128)(2,1)}, bf16[128,2048]{1,0:T(8,128)(2,1)}, u32[]{:S(2)}, u32[]{:S(2)}) collective-permute-start(bf16[128,2048]{1,0:T(8,128)(2,1)} %get-tuple-element.87), channel_id=1, source_target_pairs={{0,6},{2,0},{4,2},{6,4},{1,7},{3,1},{5,3},{7,5},{8,14},{10,8},{12,... | collective-permute-start | bytes 1572872 | tf_op jit(solution)/shard_map/ppermute | solution.py:886
  505.1 58.1 %collective-permute-start.13 = (bf16[128,2048]{1,0:T(8,128)(2,1)}, bf16[128,2048]{1,0:T(8,128)(2,1)}, u32[]{:S(2)}, u32[]{:S(2)}) collective-permute-start(bf16[128,2048]{1,0:T(8,128)(2,1)} %get-tuple-element.88), channel_id=1, source_target_pairs={{0,4},{2,6},{4,0},{6,2},{1,5},{3,7},{5,1},{7,3},{8,12},{10,14},{12... | collective-permute-start | bytes 1572872 | tf_op jit(solution)/shard_map/ppermute | solution.py:886
  505.7 89.0 %copy-start.3 = (f32[128,2048]{1,0:T(8,128)S(1)}, f32[128,2048]{1,0:T(8,128)}, u32[]{:S(2)}) copy-start(f32[128,2048]{1,0:T(8,128)} %copy-done.2) | copy-start | bytes 3145732
  505.7 89.0 %copy-start.11 = (f32[128,2048]{1,0:T(8,128)S(1)}, f32[128,2048]{1,0:T(8,128)}, u32[]{:S(2)}) copy-start(f32[128,2048]{1,0:T(8,128)} %copy-done.10) | copy-start | bytes 3145732
  505.7 88.9 %copy-start.67 = (f32[128]{0:T(128)S(1)}, f32[128]{0:T(128)}, u32[]{:S(2)}) copy-start(f32[128]{0:T(128)} %copy-done.65) | copy-start | bytes 1540
  508.5 56.9 %collective-permute-start.7 = (bf16[128,2048]{1,0:T(8,128)(2,1)}, bf16[128,2048]{1,0:T(8,128)(2,1)S(1)}, u32[]{:S(2)}, u32[]{:S(2)}) collective-permute-start(bf16[128,2048]{1,0:T(8,128)(2,1)} %get-tuple-element.89), channel_id=1, source_target_pairs={{0,2},{2,4},{4,6},{6,0},{1,3},{3,5},{5,7},{7,1},{8,10},{10,12},{12... | collective-permute-start | bytes 1572872 | tf_op jit(solution)/shard_map/ppermute | solution.py:886
  510.5 54.9 %collective-permute-start.9 = (bf16[128,2048]{1,0:T(8,128)(2,1)}, bf16[128,2048]{1,0:T(8,128)(2,1)}, u32[]{:S(2)}, u32[]{:S(2)}) collective-permute-start(bf16[128,2048]{1,0:T(8,128)(2,1)} %get-tuple-element.90), channel_id=1, source_target_pairs={{0,6},{2,0},{4,2},{6,4},{1,7},{3,1},{5,3},{7,5},{8,14},{10,8},{12,... | collective-permute-start | bytes 1572872 | tf_op jit(solution)/shard_map/ppermute | solution.py:886
  512.4 82.2 %copy-start.25 = (bf16[1,256,2048]{2,1,0:T(8,128)(2,1)S(1)}, bf16[1,256,2048]{2,1,0:T(8,128)(2,1)}, u32[]{:S(2)}) copy-start(bf16[1,256,2048]{2,1,0:T(8,128)(2,1)} %param.18) | copy-start | bytes 3145732
  518.3 76.4 %collective-permute-start.8 = (bf16[128,2048]{1,0:T(8,128)(2,1)}, bf16[128,2048]{1,0:T(8,128)(2,1)S(1)}, u32[]{:S(2)}, u32[]{:S(2)}) collective-permute-start(bf16[128,2048]{1,0:T(8,128)(2,1)} %get-tuple-element.91), channel_id=1, source_target_pairs={{0,4},{2,6},{4,0},{6,2},{1,5},{3,7},{5,1},{7,3},{8,12},{10,14},{12... | collective-permute-start | bytes 1572872 | tf_op jit(solution)/shard_map/ppermute | solution.py:886
  565.4 29.3 %copy-start.51 = (bf16[128,2048]{1,0:T(8,128)(2,1)}, bf16[128,2048]{1,0:T(8,128)(2,1)S(1)}, u32[]{:S(2)}) copy-start(bf16[128,2048]{1,0:T(8,128)(2,1)S(1)} %collective-permute-done.7) | copy-start | bytes 1572868
  597.9 28.5 %collective-permute-start.15 = (bf16[128,2048]{1,0:T(8,128)(2,1)}, bf16[128,2048]{1,0:T(8,128)(2,1)S(1)}, u32[]{:S(2)}, u32[]{:S(2)}) collective-permute-start(bf16[128,2048]{1,0:T(8,128)(2,1)} %get-tuple-element.103), channel_id=1, source_target_pairs={{0,1},{1,0},{2,3},{3,2},{4,5},{5,4},{6,7},{7,6},{8,9},{9,8},{10,11... | collective-permute-start | bytes 1572872 | tf_op jit(solution)/shard_map/ppermute | solution.py:886
  621.6 19.8 %collective-permute-start.10 = (bf16[128,2048]{1,0:T(8,128)(2,1)S(1)}, bf16[128,2048]{1,0:T(8,128)(2,1)S(1)}, u32[]{:S(2)}, u32[]{:S(2)}) collective-permute-start(bf16[128,2048]{1,0:T(8,128)(2,1)S(1)} %get-tuple-element.104), channel_id=1, source_target_pairs={{0,1},{1,0},{2,3},{3,2},{4,5},{5,4},{6,7},{7,6},{8,9},{9,8},{10,11... | collective-permute-start | bytes 1572872 | tf_op jit(solution)/shard_map/ppermute | solution.py:886
  644.0 4.5 collective-permute-start.22
  646.0 7.0 collective-permute-start.23
  646.0 7.0 collective-permute-start.24
  654.3 5.4 collective-permute-start.16
  656.6 11.2 %collective-permute-start.18 = (bf16[128,512]{1,0:T(8,128)(2,1)S(1)}, bf16[128,512]{1,0:T(8,128)(2,1)S(1)}, u32[]{:S(2)}, u32[]{:S(2)}) collective-permute-start(bf16[128,512]{1,0:T(8,128)(2,1)S(1)} %get-tuple-element.123), channel_id=1, source_target_pairs={{0,2},{2,4},{4,6},{6,0},{1,3},{3,5},{5,7},{7,1},{8,10},{10,12},{12... | collective-permute-start | bytes 393224 | tf_op jit(solution)/shard_map/ppermute | solution.py:886
  657.2 10.6 %collective-permute-start.17 = (bf16[128,512]{1,0:T(8,128)(2,1)S(1)}, bf16[128,512]{1,0:T(8,128)(2,1)S(1)}, u32[]{:S(2)}, u32[]{:S(2)}) collective-permute-start(bf16[128,512]{1,0:T(8,128)(2,1)S(1)} %get-tuple-element.125), channel_id=1, source_target_pairs={{0,4},{2,6},{4,0},{6,2},{1,5},{3,7},{5,1},{7,3},{8,12},{10,14},{12... | collective-permute-start | bytes 393224 | tf_op jit(solution)/shard_map/ppermute | solution.py:886
  674.2 111.1 %collective-permute-start.31 = (bf16[128,768]{0,1:T(8,128)(2,1)S(1)}, bf16[128,768]{0,1:T(8,128)(2,1)S(1)}, u32[]{:S(2)}, u32[]{:S(2)}) collective-permute-start(bf16[128,768]{0,1:T(8,128)(2,1)S(1)} %bitcast.532), channel_id=1, source_target_pairs={{0,6},{2,0},{4,2},{6,4},{1,7},{3,1},{5,3},{7,5},{8,14},{10,8},{12,... | collective-permute-start | bytes 589832 | tf_op jit(solution)/shard_map/ppermute | solution.py:886
  676.2 113.1 %collective-permute-start.32 = (bf16[128,768]{0,1:T(8,128)(2,1)S(1)}, bf16[128,768]{0,1:T(8,128)(2,1)S(1)}, u32[]{:S(2)}, u32[]{:S(2)}) collective-permute-start(bf16[128,768]{0,1:T(8,128)(2,1)S(1)} %bitcast.531), channel_id=1, source_target_pairs={{0,4},{2,6},{4,0},{6,2},{1,5},{3,7},{5,1},{7,3},{8,12},{10,14},{12... | collective-permute-start | bytes 589832 | tf_op jit(solution)/shard_map/ppermute | solution.py:886
  676.2 113.8 %collective-permute-start.33 = (bf16[128,768]{0,1:T(8,128)(2,1)S(1)}, bf16[128,768]{0,1:T(8,128)(2,1)S(1)}, u32[]{:S(2)}, u32[]{:S(2)}) collective-permute-start(bf16[128,768]{0,1:T(8,128)(2,1)S(1)} %bitcast.530), channel_id=1, source_target_pairs={{0,2},{2,4},{4,6},{6,0},{1,3},{3,5},{5,7},{7,1},{8,10},{10,12},{12... | collective-permute-start | bytes 589832 | tf_op jit(solution)/shard_map/ppermute | solution.py:886
  720.2 78.3 %collective-permute-start.30 = (bf16[128,768]{1,0:T(8,128)(2,1)S(1)}, bf16[128,768]{1,0:T(8,128)(2,1)S(1)}, u32[]{:S(2)}, u32[]{:S(2)}) collective-permute-start(bf16[128,768]{1,0:T(8,128)(2,1)S(1)} %get-tuple-element.111), channel_id=1, source_target_pairs={{0,2},{2,4},{4,6},{6,0},{1,3},{3,5},{5,7},{7,1},{8,10},{10,12},{12... | collective-permute-start | bytes 589832 | tf_op jit(solution)/shard_map/ppermute | solution.py:886
  721.7 76.8 %collective-permute-start.29 = (bf16[128,768]{1,0:T(8,128)(2,1)}, bf16[128,768]{1,0:T(8,128)(2,1)S(1)}, u32[]{:S(2)}, u32[]{:S(2)}) collective-permute-start(bf16[128,768]{1,0:T(8,128)(2,1)} %get-tuple-element.113), channel_id=1, source_target_pairs={{0,4},{2,6},{4,0},{6,2},{1,5},{3,7},{5,1},{7,3},{8,12},{10,14},{12... | collective-permute-start | bytes 589832 | tf_op jit(solution)/shard_map/ppermute | solution.py:886
  785.3 9.0 %collective-permute-start.28 = (bf16[128,768]{1,0:T(8,128)(2,1)}, bf16[128,768]{1,0:T(8,128)(2,1)S(1)}, u32[]{:S(2)}, u32[]{:S(2)}) collective-permute-start(bf16[128,768]{1,0:T(8,128)(2,1)} %get-tuple-element.114), channel_id=1, source_target_pairs={{0,6},{2,0},{4,2},{6,4},{1,7},{3,1},{5,3},{7,5},{8,14},{10,8},{12,... | collective-permute-start | bytes 589832 | tf_op jit(solution)/shard_map/ppermute | solution.py:886
  789.3 18.6 %collective-permute-start.27 = (bf16[128,768]{1,0:T(8,128)(2,1)}, bf16[128,768]{1,0:T(8,128)(2,1)S(1)}, u32[]{:S(2)}, u32[]{:S(2)}) collective-permute-start(bf16[128,768]{1,0:T(8,128)(2,1)} %get-tuple-element.115), channel_id=1, source_target_pairs={{0,2},{2,4},{4,6},{6,0},{1,3},{3,5},{5,7},{7,1},{8,10},{10,12},{12... | collective-permute-start | bytes 589832 | tf_op jit(solution)/shard_map/ppermute | solution.py:886
  790.0 17.2 %collective-permute-start.26 = (bf16[128,768]{1,0:T(8,128)(2,1)}, bf16[128,768]{1,0:T(8,128)(2,1)S(1)}, u32[]{:S(2)}, u32[]{:S(2)}) collective-permute-start(bf16[128,768]{1,0:T(8,128)(2,1)} %get-tuple-element.117), channel_id=1, source_target_pairs={{0,4},{2,6},{4,0},{6,2},{1,5},{3,7},{5,1},{7,3},{8,12},{10,14},{12... | collective-permute-start | bytes 589832 | tf_op jit(solution)/shard_map/ppermute | solution.py:886
  794.2 11.4 %collective-permute-start.25 = (bf16[128,768]{1,0:T(8,128)(2,1)}, bf16[128,768]{1,0:T(8,128)(2,1)}, u32[]{:S(2)}, u32[]{:S(2)}) collective-permute-start(bf16[128,768]{1,0:T(8,128)(2,1)} %get-tuple-element.118), channel_id=1, source_target_pairs={{0,6},{2,0},{4,2},{6,4},{1,7},{3,1},{5,3},{7,5},{8,14},{10,8},{12,... | collective-permute-start | bytes 589832 | tf_op jit(solution)/shard_map/ppermute | solution.py:886
  (62 other events, 212.0 us)
Sparse Core Ops, SparseCore 0:
  10.9 115.2 all-gather.1
  470.9 51.1 reduce-scatter.7
  525.5 51.1 reduce-scatter.5
  579.9 73.2 reduce-scatter.13
  656.4 61.7 reduce-scatter.11
  721.4 61.7 reduce-scatter.9
